TPU v7x, 256 devices: a whole 4x4x8 slice. The times are simulated.
256 devices in a mesh: gx: 64 (over x, z_hi, y, core), gy: 4 (over z_lo).
Axes of the slice: x: 4, y: 4, z: 8 (z_hi: 2, z_lo: 4; z = z_hi * 4 + z_lo), core: 2. Of those that a mesh axis runs over, the one named last changes fastest.
Arguments:
- adjoint: float32 [9, 256, 128, 512], P(None, 'gx', 'gy'), may hold values from -6 to 6
- buoyancy: float32 [256, 128, 512], P('gx', 'gy'), may hold values from 0.5 to 2
- lame_lambda: float32 [256, 128, 512], P('gx', 'gy'), may hold values from 0.5 to 2
- shear_mu: float32 [256, 128, 512], P('gx', 'gy'), may hold values from 0.3 to 1.2
- packed: int32 [64, 64, 4, 12, 256], P('gx', None, 'gy'), may hold values from -2147483648 to 2147483646
- scales: float32 [64, 64, 4, 12], P('gx', None, 'gy'), may hold values from 0.005 to 0.05
- perm: int32 [64, 64], P('gx'), may hold values from 0 to 63, each once within a row
Outputs:
- adjoint_out: float32 [9, 256, 128, 512], P(None, 'gx', 'gy')
- gradients: float32 [2, 256, 128, 512], P(None, 'gx', 'gy')
Inputs may be any that keep to these rules, and one draw needn't show every extreme that they name: Each row of perm names every number 0 to 63 once. The words of packed are stored inputs and may cross devices as they are, four signed bytes to a word; only values that a program computes travel in float32.
All inputs are finite; a program needn't handle non-finite values.
Results may differ from a plain program's by a relative error of at most 0.0003.
Values sent between devices are 32-bit elements; how exact they have to be, the bound alone decides.
No kernel may reach another device: no remote copies, remote signals or barrier semaphores. Data moves between devices by JAX's collectives and lax.ppermute only.
A program may use at most 128 MiB of HBM per device.

v0:
```python
import jax
import jax.numpy as jnp
from jax import lax
from jax.sharding import PartitionSpec as P

STEPS = 2


courant = 0.15


def passed_along(value, axis, steps):
    count = lax.axis_size(axis)
    first, last = (max(0, -steps), min(count, count - steps))
    return lax.ppermute(value, axis, [(source, source + steps) for source in range(first, last)])


def unpack(words):
    low = (words & 255) - 128
    middle = (jnp.right_shift(words, 8) & 255) - 128
    high = (jnp.right_shift(words, 16) & 255) - 128
    topmost = jnp.right_shift(words, 24)
    return jnp.concatenate([low, middle, high, topmost], axis=-1).astype(jnp.float32)


def inverse_order(row):
    count = row.shape[0]
    slots = jnp.arange(count, dtype=jnp.int32)
    hits = (row[None, :] == slots[:, None]).astype(jnp.int32)
    return jnp.sum(hits * slots[None, :], axis=1)


def frame(field, ahead_x, behind_x, ahead_y, behind_y):
    rows_x, rows_y, rows_z = field.shape
    zero_x = jnp.zeros((1, rows_y, rows_z), jnp.float32)
    lower_x = zero_x if behind_x is None else behind_x
    upper_x = zero_x if ahead_x is None else ahead_x
    middle = jnp.concatenate([lower_x, field, upper_x], axis=0)
    zero_y = jnp.zeros((rows_x, 1, rows_z), jnp.float32)
    lower_y = zero_y if behind_y is None else behind_y
    upper_y = zero_y if ahead_y is None else ahead_y
    lower_y = jnp.pad(lower_y, ((1, 1), (0, 0), (0, 0)))
    upper_y = jnp.pad(upper_y, ((1, 1), (0, 0), (0, 0)))
    joined = jnp.concatenate([lower_y, middle, upper_y], axis=1)
    return jnp.pad(joined, ((0, 0), (0, 0), (1, 1)))


def window(field, margin, out_margin, shift):
    start_x = margin - out_margin + shift[0]
    start_y = margin - out_margin + shift[1]
    start_z = 1 + shift[2]
    size_x = field.shape[0] - 2 * margin + 2 * out_margin
    size_y = field.shape[1] - 2 * margin + 2 * out_margin
    size_z = field.shape[2] - 2
    return lax.slice(
        field, (start_x, start_y, start_z), (start_x + size_x, start_y + size_y, start_z + size_z)
    )


def unit_shift(axis, amount):
    offsets = [0, 0, 0]
    offsets[axis] = amount
    return tuple(offsets)


def diff_ahead(field, axis, margin, out_margin):
    return window(field, margin, out_margin, unit_shift(axis, 1)) - window(
        field, margin, out_margin, (0, 0, 0)
    )


def diff_behind(field, axis, margin, out_margin):
    return window(field, margin, out_margin, (0, 0, 0)) - window(
        field, margin, out_margin, unit_shift(axis, -1)
    )


def move_velocity(velocity, stress, buoyancy, margin, out_margin):
    scaled = courant * buoyancy

    def ahead(field, axis):
        return diff_ahead(field, axis, margin, out_margin)

    def behind(field, axis):
        return diff_behind(field, axis, margin, out_margin)

    return [
        velocity[0] - scaled * (ahead(stress[0], 0) + behind(stress[3], 1) + behind(stress[4], 2)),
        velocity[1] - scaled * (behind(stress[3], 0) + ahead(stress[1], 1) + behind(stress[5], 2)),
        velocity[2] - scaled * (behind(stress[4], 0) + behind(stress[5], 1) + ahead(stress[2], 2)),
    ]


def strains(padded, margin):

    def ahead(field, axis):
        return diff_ahead(field, axis, margin, 0)

    def behind(field, axis):
        return diff_behind(field, axis, margin, 0)

    return [
        behind(padded[0], 0),
        behind(padded[1], 1),
        behind(padded[2], 2),
        ahead(padded[0], 1) + ahead(padded[1], 0),
        ahead(padded[0], 2) + ahead(padded[2], 0),
        ahead(padded[1], 2) + ahead(padded[2], 1),
    ]


def move_stress(stress, strain, lame_lambda, shear_mu):
    trace = strain[0] + strain[1] + strain[2]
    result = []
    for index in range(3):
        result.append(
            stress[index] - courant * (lame_lambda * trace + 2.0 * shear_mu * strain[index])
        )
    for index in range(3, 6):
        result.append(stress[index] - courant * shear_mu * strain[index])
    return result


def on_device(adjoint, buoyancy, lame_lambda, shear_mu, packed, scales, perm):
    cells_x, cells_y, cells_z = buoyancy.shape
    inverse = inverse_order(perm[0])
    words = lax.all_to_all(packed, "gx", split_axis=1, concat_axis=0, tiled=True)
    factor = lax.all_to_all(scales, "gx", split_axis=1, concat_axis=0, tiled=True)
    blocks = unpack(words[:, 0, 0]) * factor[:, 0, 0, :, None]
    ordered = jnp.take(blocks, inverse, axis=0)
    forward = jnp.transpose(ordered, (1, 0, 2)).reshape(blocks.shape[1], cells_x, cells_y, cells_z)
    velocity = [adjoint[index] for index in range(3)]
    stress = [adjoint[index] for index in range(3, 9)]
    grad_lambda = jnp.zeros(buoyancy.shape, jnp.float32)
    grad_mu = jnp.zeros(buoyancy.shape, jnp.float32)
    for step in range(STEPS):
        stress_xx, stress_yy, stress_zz, stress_xy, stress_xz, stress_yz = stress
        next_x = passed_along(stress_xx[0:1], "gx", -1)
        prior_x = passed_along(jnp.stack([stress_xy[-1:], stress_xz[-1:]]), "gx", 1)
        next_y = passed_along(stress_yy[:, 0:1], "gy", -1)
        prior_y = passed_along(jnp.stack([stress_xy[:, -1:], stress_yz[:, -1:]]), "gy", 1)
        framed = [
            frame(stress_xx, next_x, None, None, None),
            frame(stress_yy, None, None, next_y, None),
            frame(stress_zz, None, None, None, None),
            frame(stress_xy, None, prior_x[0], None, prior_y[0]),
            frame(stress_xz, None, prior_x[1], None, None),
            frame(stress_yz, None, None, None, prior_y[1]),
        ]
        velocity = move_velocity(velocity, framed, buoyancy, 1, 0)
        speed_x, speed_y, speed_z = velocity
        vel_next_x = passed_along(jnp.stack([speed_y[0:1], speed_z[0:1]]), "gx", -1)
        vel_prior_x = passed_along(speed_x[-1:], "gx", 1)
        vel_next_y = passed_along(jnp.stack([speed_x[:, 0:1], speed_z[:, 0:1]]), "gy", -1)
        vel_prior_y = passed_along(speed_y[:, -1:], "gy", 1)
        moved = [
            frame(speed_x, None, vel_prior_x, vel_next_y[0], None),
            frame(speed_y, vel_next_x[0], None, None, vel_prior_y),
            frame(speed_z, vel_next_x[1], None, vel_next_y[1], None),
        ]
        strain = strains(moved, 1)
        stress = move_stress(stress, strain, lame_lambda, shear_mu)
        trace = strain[0] + strain[1] + strain[2]
        stored = [forward[6 * step + index] for index in range(6)]
        grad_lambda = grad_lambda + trace * (stored[0] + stored[1] + stored[2])
        grad_mu = grad_mu + 2.0 * (
            strain[0] * stored[0] + strain[1] * stored[1] + strain[2] * stored[2]
        )
        grad_mu = grad_mu + strain[3] * stored[3] + strain[4] * stored[4] + strain[5] * stored[5]
    return (jnp.stack(velocity + stress), jnp.stack([grad_lambda, grad_mu]))


def solution(mesh):
    return jax.shard_map(
        on_device,
        mesh=mesh,
        in_specs=(
            P(None, "gx", "gy", None),
            P("gx", "gy", None),
            P("gx", "gy", None),
            P("gx", "gy", None),
            P("gx", None, "gy", None, None),
            P("gx", None, "gy", None),
            P("gx", None),
        ),
        out_specs=(P(None, "gx", "gy", None), P(None, "gx", "gy", None)),
        check_vma=False,
    )
```

profile of v0, /device:TPU:70, one launch (start us, length us, event | category | flops | bytes accessed | tf_op | source)
XLA Modules:
  0.0 199.1 jit_solution(1496756770010428238)
XLA Ops:
  0.6 13.3 %all-to-all-start = ((s32[1,64,1,12,256]{4,2,3,0,1:T(1,128)}), s32[1,64,1,12,256]{4,2,3,0,1:T(1,128)}, u32[]{:S(2)}, u32[]{:S(2)}) async-start(s32[1,64,1,12,256]{4,2,3,0,1:T(1,128)} %bitcast.137), calls=%async_computation | async-start | bytes 1572864 | tf_op jit(solution)/shard_map/all_to_all | solution.py:127
  14.0 1.5 slice_bitcast_fusion.20
  15.4 9.4 %collective-permute-start = (f32[1,32,512]{2,1,0:T(8,128)}, f32[1,32,512]{2,1,0:T(8,128)S(1)}, u32[]{:S(2)}, u32[]{:S(2)}) collective-permute-start(f32[1,32,512]{2,1,0:T(8,128)} %slice_bitcast_fusion.20), channel_id=1, source_target_pairs={{4,0},{8,4},{12,8},{16,12},{20,16},{24,20},{28,24},{32,28},{36,32}... | collective-permute-start | bytes 196616 | tf_op jit(solution)/shard_map/ppermute | solution.py:15
  24.8 1.6 stack.110
  26.4 2.2 %collective-permute-start.2 = (f32[2,1,32,512]{3,2,1,0:T(8,128)}, f32[2,1,32,512]{3,2,1,0:T(8,128)}, u32[]{:S(2)}, u32[]{:S(2)}) collective-permute-start(f32[2,1,32,512]{3,2,1,0:T(8,128)} %stack.110), channel_id=1, source_target_pairs={{0,4},{4,8},{8,12},{12,16},{16,20},{20,24},{24,28},{28,32},{32,36}... | collective-permute-start | bytes 393224 | tf_op jit(solution)/shard_map/ppermute | solution.py:15
  28.6 2.3 %slice_bitcast_fusion.1 = (f32[4,32,512]{2,1,0:T(8,128)S(1)}, f32[4,32,512]{2,1,0:T(8,128)S(1)}, f32[4,32,512]{2,1,0:T(8,128)S(1)}, f32[4,32,512]{2,1,0:T(8,128)...) fusion(f32[9,4,32,512]{3,2,1,0:T(8,128)} %param.7), kind=kLoop, calls=%fused_computation.226 | loop fusion | bytes 3145728 | tf_op jit(solution)/shard_map/squeeze | solution.py:133
  30.9 0.7 copy-done.42
  31.6 2.9 %collective-permute-start.4 = (f32[4,1,512]{2,1,0:T(1,128)S(1)}, f32[4,1,512]{2,1,0:T(1,128)S(1)}, u32[]{:S(2)}, u32[]{:S(2)}) collective-permute-start(f32[4,1,512]{2,1,0:T(1,128)S(1)} %slice.544), channel_id=1, source_target_pairs={{1,0},{2,1},{3,2},{5,4},{6,5},{7,6},{9,8},{10,9},{11,10},{13,12},{... | collective-permute-start | bytes 24584 | tf_op jit(solution)/shard_map/ppermute | solution.py:15
  34.6 2.9 %collective-permute-start.1 = (f32[2,4,1,512]{3,2,1,0:T(1,128)S(1)}, f32[2,4,1,512]{3,2,1,0:T(1,128)S(1)}, u32[]{:S(2)}, u32[]{:S(2)}) collective-permute-start(f32[2,4,1,512]{3,2,1,0:T(1,128)S(1)} %pad_maximum_fusion.68), channel_id=1, source_target_pairs={{0,1},{1,2},{2,3},{4,5},{5,6},{6,7},{8,9},{9,10},{10,11},{12,13},{... | collective-permute-start | bytes 49160 | tf_op jit(solution)/shard_map/ppermute | solution.py:15
  38.9 0.7 copy.49
  40.2 0.9 collective-permute-done.2
  41.1 0.9 slice_bitcast_fusion.19
  42.1 1.2 pad_maximum_fusion.6
  43.3 1.3 fusion.33
  44.9 1.3 fusion.27
  46.2 3.2 %collective-permute-start.5 = (f32[4,1,512]{2,1,0:T(1,128)S(1)}, f32[4,1,512]{2,1,0:T(1,128)S(1)}, u32[]{:S(2)}, u32[]{:S(2)}) collective-permute-start(f32[4,1,512]{2,1,0:T(1,128)S(1)} %slice.546), channel_id=1, source_target_pairs={{0,1},{1,2},{2,3},{4,5},{5,6},{6,7},{8,9},{9,10},{10,11},{12,13},{... | collective-permute-start | bytes 24584 | tf_op jit(solution)/shard_map/ppermute | solution.py:15
  49.5 2.6 %collective-permute-start.7 = (f32[2,4,1,512]{3,2,1,0:T(1,128)S(1)}, f32[2,4,1,512]{3,2,1,0:T(1,128)S(1)}, u32[]{:S(2)}, u32[]{:S(2)}) collective-permute-start(f32[2,4,1,512]{3,2,1,0:T(1,128)S(1)} %pad_maximum_fusion.69), channel_id=1, source_target_pairs={{1,0},{2,1},{3,2},{5,4},{6,5},{7,6},{9,8},{10,9},{11,10},{13,12},{... | collective-permute-start | bytes 49160 | tf_op jit(solution)/shard_map/ppermute | solution.py:15
  52.1 1.9 collective-permute-start.3
  54.1 10.6 %collective-permute-start.6 = (f32[2,1,32,512]{3,2,1,0:T(8,128)S(1)}, f32[2,1,32,512]{3,2,1,0:T(8,128)S(1)}, u32[]{:S(2)}, u32[]{:S(2)}) collective-permute-start(f32[2,1,32,512]{3,2,1,0:T(8,128)S(1)} %pad_maximum_fusion.65), channel_id=1, source_target_pairs={{4,0},{8,4},{12,8},{16,12},{20,16},{24,20},{28,24},{32,28},{36,32}... | collective-permute-start | bytes 393224 | tf_op jit(solution)/shard_map/ppermute | solution.py:15
  64.7 2.9 %collective-permute-done.6 = f32[2,1,32,512]{3,2,1,0:T(8,128)S(1)} collective-permute-done((f32[2,1,32,512]{3,2,1,0:T(8,128)S(1)}, f32[2,1,32,512]{3,2,1,0:T(8,128)S(1)}, u32[]{:S(2)}, u32[]{:S(2)}) %collective-permute-start.6) | collective-permute-done | bytes 131104 | tf_op jit(solution)/shard_map/ppermute | solution.py:15
  69.6 2.3 %collective-permute-start.11 = (f32[4,1,512]{2,1,0:T(1,128)S(1)}, f32[4,1,512]{2,1,0:T(1,128)S(1)}, u32[]{:S(2)}, u32[]{:S(2)}) collective-permute-start(f32[4,1,512]{2,1,0:T(1,128)S(1)} %slice.563), channel_id=1, source_target_pairs={{1,0},{2,1},{3,2},{5,4},{6,5},{7,6},{9,8},{10,9},{11,10},{13,12},{... | collective-permute-start | bytes 24584 | tf_op jit(solution)/shard_map/ppermute | solution.py:15
  71.9 10.5 %collective-permute-start.8 = (f32[1,32,512]{2,1,0:T(8,128)S(1)}, f32[1,32,512]{2,1,0:T(8,128)S(1)}, u32[]{:S(2)}, u32[]{:S(2)}) collective-permute-start(f32[1,32,512]{2,1,0:T(8,128)S(1)} %slice.554), channel_id=1, source_target_pairs={{4,0},{8,4},{12,8},{16,12},{20,16},{24,20},{28,24},{32,28},{36,32}... | collective-permute-start | bytes 196616 | tf_op jit(solution)/shard_map/ppermute | solution.py:15
  82.4 3.5 %collective-permute-start.9 = (f32[2,4,1,512]{3,2,1,0:T(1,128)S(1)}, f32[2,4,1,512]{3,2,1,0:T(1,128)S(1)}, u32[]{:S(2)}, u32[]{:S(2)}) collective-permute-start(f32[2,4,1,512]{3,2,1,0:T(1,128)S(1)} %pad_maximum_fusion.70), channel_id=1, source_target_pairs={{0,1},{1,2},{2,3},{4,5},{5,6},{6,7},{8,9},{9,10},{10,11},{12,13},{... | collective-permute-start | bytes 49160 | tf_op jit(solution)/shard_map/ppermute | solution.py:15
  86.0 1.9 collective-permute-start.10
  88.1 12.1 %collective-permute-done.10 = f32[2,1,32,512]{3,2,1,0:T(8,128)S(1)} collective-permute-done((f32[2,1,32,512]{3,2,1,0:T(8,128)S(1)}, f32[2,1,32,512]{3,2,1,0:T(8,128)S(1)}, u32[]{:S(2)}, u32[]{:S(2)}) %collective-permute-start.10) | collective-permute-done | bytes 131104 | tf_op jit(solution)/shard_map/ppermute | solution.py:15
  100.3 0.9 bitcast_dynamic-update-slice_fusion.8
  101.3 0.9 bitcast_dynamic-update-slice_fusion.7
  102.2 1.9 collective-permute-start.13
  104.2 0.9 bitcast_dynamic-update-slice_fusion.6
  105.1 3.9 %collective-permute-start.15 = (f32[2,4,1,512]{3,2,1,0:T(1,128)S(1)}, f32[2,4,1,512]{3,2,1,0:T(1,128)S(1)}, u32[]{:S(2)}, u32[]{:S(2)}) collective-permute-start(f32[2,4,1,512]{3,2,1,0:T(1,128)S(1)} %pad_maximum_fusion.71), channel_id=1, source_target_pairs={{1,0},{2,1},{3,2},{5,4},{6,5},{7,6},{9,8},{10,9},{11,10},{13,12},{... | collective-permute-start | bytes 49160 | tf_op jit(solution)/shard_map/ppermute | solution.py:15
  109.0 1.9 collective-permute-start.12
  111.0 10.6 %collective-permute-start.14 = (f32[2,1,32,512]{3,2,1,0:T(8,128)S(1)}, f32[2,1,32,512]{3,2,1,0:T(8,128)S(1)}, u32[]{:S(2)}, u32[]{:S(2)}) collective-permute-start(f32[2,1,32,512]{3,2,1,0:T(8,128)S(1)} %pad_maximum_fusion.67), channel_id=1, source_target_pairs={{4,0},{8,4},{12,8},{16,12},{20,16},{24,20},{28,24},{32,28},{36,32}... | collective-permute-start | bytes 393224 | tf_op jit(solution)/shard_map/ppermute | solution.py:15
  121.7 3.7 %collective-permute-done.14 = f32[2,1,32,512]{3,2,1,0:T(8,128)S(1)} collective-permute-done((f32[2,1,32,512]{3,2,1,0:T(8,128)S(1)}, f32[2,1,32,512]{3,2,1,0:T(8,128)S(1)}, u32[]{:S(2)}, u32[]{:S(2)}) %collective-permute-start.14) | collective-permute-done | bytes 131104 | tf_op jit(solution)/shard_map/ppermute | solution.py:15
  125.4 1.0 pad_maximum_fusion
  126.4 13.5 %all-to-all-start.1 = ((f32[1,64,1,12]{3,2,0,1:T(1,128)}), f32[1,64,1,12]{3,2,0,1:T(1,128)S(1)}, u32[]{:S(2)}, u32[]{:S(2)}) async-start(f32[1,64,1,12]{3,2,0,1:T(1,128)} %copy.49), calls=%async_computation.1 | async-start | bytes 65536 | tf_op jit(solution)/shard_map/all_to_all | solution.py:128
  140.0 3.0 %fusion.2 = (s32[64,12,256]{2,1,0:T(8,128)}, s32[64,12,256]{2,1,0:T(8,128)}, s32[64,12,256]{2,1,0:T(8,128)}) fusion(s32[1,64,1,12,256]{4,2,3,0,1:T(1,128)} %all-to-all-done), kind=kLoop, calls=%fused_computation.40 | loop fusion | flops 1572864 | bytes 3145728 | tf_op jit(solution)/shard_map/sub | solution.py:19
  143.0 1.3 fusion.9
  144.3 1.5 copy.48
  145.8 4.1 %all-to-all-done.1 = f32[1,64,1,12]{3,2,0,1:T(1,128)S(1)} async-done(((f32[1,64,1,12]{3,2,0,1:T(1,128)}), f32[1,64,1,12]{3,2,0,1:T(1,128)S(1)}, u32[]{:S(2)}, u32[]{:S(2)}) %all-to-all-start.1) | async-done | bytes 3104 | tf_op jit(solution)/shard_map/all_to_all | solution.py:128
  149.9 3.8 %fusion = f32[64,12,1024]{2,1,0:T(8,128)} fusion(s32[64,12,256]{2,1,0:T(8,128)} %copy.48, s32[64,12,256]{2,1,0:T(8,128)} %get-tuple-element.37, s32[64,12,256]{2,1,0:T(8,128)} %get-tuple-element.36, s32[64,12,256]{2,1,0:T(8,128)} %get-tuple-element.35, f32[64,12]{1,0:T(8,128)S(1)} %bitcast.138), kind=kLoop, calls=%fused_computation.2 | loop fusion | flops 3932160 | bytes 6294528 | tf_op jit(solution)/shard_map/mul | solution.py:129
  153.7 5.1 %gather_fusion = f32[64,12,1024]{2,1,0:T(8,128)} fusion(f32[64,12,1024]{2,1,0:T(8,128)} %fusion, s32[1024]{0:T(1024)} %pad_clamp_fusion), kind=kCustom, calls=%fused_computation | custom fusion | bytes 6291712 | tf_op jit(solution)/shard_map/jit(_take)/gather | solution.py:130
  158.8 2.5 %select_bitcast_fusion = f32[12,64,1024]{2,0,1:T(8,128)S(1)} fusion(f32[64,12,1024]{2,1,0:T(8,128)} %gather_fusion, pred[64]{0:T(512)(128)(4,1)S(1)} %copy-done.62), kind=kLoop, calls=%fused_computation.3 | loop fusion | flops 786432 | bytes 6291520 | tf_op jit(solution)/shard_map/jit(_take)/select_n | solution.py:130
  161.3 10.0 %slice_reduce_fusion.11 = (f32[64,1024]{1,0:T(8,128)}, f32[64,1024]{1,0:T(8,128)}, f32[64,1024]{1,0:T(8,128)}, f32[64,1024]{1,0:T(8,128)S(1)}, f32[64,1024]{1,0:...) fusion(f32[12,64,1024]{2,0,1:T(8,128)S(1)} %select_bitcast_fusion), kind=kLoop, calls=%fused_computation.171 | loop fusion | bytes 6291456 | tf_op jit(solution)/shard_map/slice | solution.py:164
  171.4 1.7 squeeze.137
  173.0 1.7 squeeze.142
  174.7 1.7 squeeze.141
  176.4 1.7 squeeze.140
  178.1 1.7 squeeze.139
  179.8 1.7 squeeze.138
  181.5 1.7 squeeze.148
  183.2 1.7 squeeze.147
  184.9 0.7 squeeze.146
  185.6 0.7 squeeze.145
  186.3 1.7 squeeze.144
  188.1 1.7 squeeze.143
  189.8 1.8 add_bitcast_fusion.1
  191.7 0.9 bitcast_dynamic-update-slice_fusion.5
  192.5 0.9 bitcast_dynamic-update-slice_fusion.4
  193.4 0.9 bitcast_dynamic-update-slice_fusion.3
  194.5 0.8 bitcast_dynamic-update-slice_fusion.2
  195.3 0.9 bitcast_dynamic-update-slice_fusion.1
  196.2 0.9 bitcast_dynamic-update-slice_fusion
  197.2 1.1 add_bitcast_fusion
  198.3 0.8 pad_maximum_fusion.48
  (197 shorter events, 4.9 us)
Async XLA Ops:
  0.6 36.9 %copy-start.63 = (s32[1,64]{1,0:T(1,128)S(1)}, s32[1,64]{1,0:T(1,128)}, u32[]{:S(2)}) copy-start(s32[1,64]{1,0:T(1,128)} %param.13) | copy-start | bytes 772
  0.6 38.3 %copy-start.61 = (f32[1,64,1,12]{1,2,3,0:T(1,128)S(1)}, f32[1,64,1,12]{1,2,3,0:T(1,128)}, u32[]{:S(2)}) copy-start(f32[1,64,1,12]{1,2,3,0:T(1,128)} %param.12) | copy-start | bytes 9220
  0.6 125.8 %all-to-all-start = ((s32[1,64,1,12,256]{4,2,3,0,1:T(1,128)}), s32[1,64,1,12,256]{4,2,3,0,1:T(1,128)}, u32[]{:S(2)}, u32[]{:S(2)}) async-start(s32[1,64,1,12,256]{4,2,3,0,1:T(1,128)} %bitcast.137), calls=%async_computation | async-start | bytes 1572864 | tf_op jit(solution)/shard_map/all_to_all | solution.py:127
  15.4 29.4 %collective-permute-start = (f32[1,32,512]{2,1,0:T(8,128)}, f32[1,32,512]{2,1,0:T(8,128)S(1)}, u32[]{:S(2)}, u32[]{:S(2)}) collective-permute-start(f32[1,32,512]{2,1,0:T(8,128)} %slice_bitcast_fusion.20), channel_id=1, source_target_pairs={{4,0},{8,4},{12,8},{16,12},{20,16},{24,20},{28,24},{32,28},{36,32}... | collective-permute-start | bytes 196616 | tf_op jit(solution)/shard_map/ppermute | solution.py:15
  26.4 16.9 %copy-start.1 = (f32[9,4,32,512]{3,2,1,0:T(8,128)S(1)}, f32[9,4,32,512]{3,2,1,0:T(8,128)}, u32[]{:S(2)}) copy-start(f32[9,4,32,512]{3,2,1,0:T(8,128)} %param.7) | copy-start | bytes 7077892
  26.4 16.9 %copy-start.2 = (f32[4,32,512]{2,1,0:T(8,128)S(1)}, f32[4,32,512]{2,1,0:T(8,128)}, u32[]{:S(2)}) copy-start(f32[4,32,512]{2,1,0:T(8,128)} %param.8) | copy-start | bytes 786436
  26.4 14.7 %collective-permute-start.2 = (f32[2,1,32,512]{3,2,1,0:T(8,128)}, f32[2,1,32,512]{3,2,1,0:T(8,128)}, u32[]{:S(2)}, u32[]{:S(2)}) collective-permute-start(f32[2,1,32,512]{3,2,1,0:T(8,128)} %stack.110), channel_id=1, source_target_pairs={{0,4},{4,8},{8,12},{12,16},{16,20},{20,24},{24,28},{28,32},{32,36}... | collective-permute-start | bytes 393224 | tf_op jit(solution)/shard_map/ppermute | solution.py:15
  30.9 12.4 %copy-start.27 = (f32[4,32,512]{2,1,0:T(8,128)}, f32[4,32,512]{2,1,0:T(8,128)S(1)}, u32[]{:S(2)}) copy-start(f32[4,32,512]{2,1,0:T(8,128)S(1)} %get-tuple-element.30) | copy-start | bytes 786436
  30.9 13.7 %copy-start.23 = (f32[4,32,512]{2,1,0:T(8,128)}, f32[4,32,512]{2,1,0:T(8,128)S(1)}, u32[]{:S(2)}) copy-start(f32[4,32,512]{2,1,0:T(8,128)S(1)} %get-tuple-element.32) | copy-start | bytes 786436
  31.6 13.0 %collective-permute-start.4 = (f32[4,1,512]{2,1,0:T(1,128)S(1)}, f32[4,1,512]{2,1,0:T(1,128)S(1)}, u32[]{:S(2)}, u32[]{:S(2)}) collective-permute-start(f32[4,1,512]{2,1,0:T(1,128)S(1)} %slice.544), channel_id=1, source_target_pairs={{1,0},{2,1},{3,2},{5,4},{6,5},{7,6},{9,8},{10,9},{11,10},{13,12},{... | collective-permute-start | bytes 24584 | tf_op jit(solution)/shard_map/ppermute | solution.py:15
  34.6 5.6 %collective-permute-start.1 = (f32[2,4,1,512]{3,2,1,0:T(1,128)S(1)}, f32[2,4,1,512]{3,2,1,0:T(1,128)S(1)}, u32[]{:S(2)}, u32[]{:S(2)}) collective-permute-start(f32[2,4,1,512]{3,2,1,0:T(1,128)S(1)} %pad_maximum_fusion.68), channel_id=1, source_target_pairs={{0,1},{1,2},{2,3},{4,5},{5,6},{6,7},{8,9},{9,10},{10,11},{12,13},{... | collective-permute-start | bytes 49160 | tf_op jit(solution)/shard_map/ppermute | solution.py:15
  44.9 22.9 %copy-start = (f32[4,32,512]{2,1,0:T(8,128)S(1)}, f32[4,32,512]{2,1,0:T(8,128)}, u32[]{:S(2)}) copy-start(f32[4,32,512]{2,1,0:T(8,128)} %param.10) | copy-start | bytes 786436
  44.9 22.9 %copy-start.8 = (f32[4,32,512]{2,1,0:T(8,128)S(1)}, f32[4,32,512]{2,1,0:T(8,128)}, u32[]{:S(2)}) copy-start(f32[4,32,512]{2,1,0:T(8,128)} %param.9) | copy-start | bytes 786436
  46.2 18.4 %collective-permute-start.5 = (f32[4,1,512]{2,1,0:T(1,128)S(1)}, f32[4,1,512]{2,1,0:T(1,128)S(1)}, u32[]{:S(2)}, u32[]{:S(2)}) collective-permute-start(f32[4,1,512]{2,1,0:T(1,128)S(1)} %slice.546), channel_id=1, source_target_pairs={{0,1},{1,2},{2,3},{4,5},{5,6},{6,7},{8,9},{9,10},{10,11},{12,13},{... | collective-permute-start | bytes 24584 | tf_op jit(solution)/shard_map/ppermute | solution.py:15
  49.5 15.2 %collective-permute-start.7 = (f32[2,4,1,512]{3,2,1,0:T(1,128)S(1)}, f32[2,4,1,512]{3,2,1,0:T(1,128)S(1)}, u32[]{:S(2)}, u32[]{:S(2)}) collective-permute-start(f32[2,4,1,512]{3,2,1,0:T(1,128)S(1)} %pad_maximum_fusion.69), channel_id=1, source_target_pairs={{1,0},{2,1},{3,2},{5,4},{6,5},{7,6},{9,8},{10,9},{11,10},{13,12},{... | collective-permute-start | bytes 49160 | tf_op jit(solution)/shard_map/ppermute | solution.py:15
  52.1 15.5 %collective-permute-start.3 = (f32[1,32,512]{2,1,0:T(8,128)S(1)}, f32[1,32,512]{2,1,0:T(8,128)S(1)}, u32[]{:S(2)}, u32[]{:S(2)}) collective-permute-start(f32[1,32,512]{2,1,0:T(8,128)S(1)} %slice.543), channel_id=1, source_target_pairs={{0,4},{4,8},{8,12},{12,16},{16,20},{20,24},{24,28},{28,32},{32,36}... | collective-permute-start | bytes 196616 | tf_op jit(solution)/shard_map/ppermute | solution.py:15
  54.1 13.5 %collective-permute-start.6 = (f32[2,1,32,512]{3,2,1,0:T(8,128)S(1)}, f32[2,1,32,512]{3,2,1,0:T(8,128)S(1)}, u32[]{:S(2)}, u32[]{:S(2)}) collective-permute-start(f32[2,1,32,512]{3,2,1,0:T(8,128)S(1)} %pad_maximum_fusion.65), channel_id=1, source_target_pairs={{4,0},{8,4},{12,8},{16,12},{20,16},{24,20},{28,24},{32,28},{36,32}... | collective-permute-start | bytes 393224 | tf_op jit(solution)/shard_map/ppermute | solution.py:15
  64.7 4.0 %copy-start.53 = (f32[6,1,512]{2,1,0:T(1,128)}, f32[6,1,512]{2,1,0:T(1,128)S(1)}, u32[]{:S(2)}) copy-start(f32[6,1,512]{2,1,0:T(1,128)S(1)} %pad.117) | copy-start | bytes 36868
  64.7 4.0 %copy-start.55 = (f32[6,1,512]{2,1,0:T(1,128)}, f32[6,1,512]{2,1,0:T(1,128)S(1)}, u32[]{:S(2)}) copy-start(f32[6,1,512]{2,1,0:T(1,128)S(1)} %pad.119) | copy-start | bytes 36868
  68.2 35.9 %copy-start.4 = (f32[4,32,512]{2,1,0:T(8,128)}, f32[4,32,512]{2,1,0:T(8,128)S(1)}, u32[]{:S(2)}) copy-start(f32[4,32,512]{2,1,0:T(8,128)S(1)} %get-tuple-element.26) | copy-start | bytes 786436
  68.2 35.9 %copy-start.19 = (f32[4,32,512]{2,1,0:T(8,128)}, f32[4,32,512]{2,1,0:T(8,128)S(1)}, u32[]{:S(2)}) copy-start(f32[4,32,512]{2,1,0:T(8,128)S(1)} %get-tuple-element.18) | copy-start | bytes 786436
  69.0 32.3 %copy-start.10 = (f32[4,32,512]{2,1,0:T(8,128)}, f32[4,32,512]{2,1,0:T(8,128)S(1)}, u32[]{:S(2)}) copy-start(f32[4,32,512]{2,1,0:T(8,128)S(1)} %get-tuple-element.28) | copy-start | bytes 786436
  69.0 35.1 %copy-start.6 = (f32[4,32,512]{2,1,0:T(8,128)}, f32[4,32,512]{2,1,0:T(8,128)S(1)}, u32[]{:S(2)}) copy-start(f32[4,32,512]{2,1,0:T(8,128)S(1)} %get-tuple-element.27) | copy-start | bytes 786436
  69.6 31.7 %copy-start.21 = (f32[4,32,512]{2,1,0:T(8,128)}, f32[4,32,512]{2,1,0:T(8,128)S(1)}, u32[]{:S(2)}) copy-start(f32[4,32,512]{2,1,0:T(8,128)S(1)} %get-tuple-element.25) | copy-start | bytes 786436
  69.6 31.7 %copy-start.24 = (f32[4,32,512]{2,1,0:T(8,128)}, f32[4,32,512]{2,1,0:T(8,128)S(1)}, u32[]{:S(2)}) copy-start(f32[4,32,512]{2,1,0:T(8,128)S(1)} %get-tuple-element.24) | copy-start | bytes 786436
  69.6 31.7 %collective-permute-start.11 = (f32[4,1,512]{2,1,0:T(1,128)S(1)}, f32[4,1,512]{2,1,0:T(1,128)S(1)}, u32[]{:S(2)}, u32[]{:S(2)}) collective-permute-start(f32[4,1,512]{2,1,0:T(1,128)S(1)} %slice.563), channel_id=1, source_target_pairs={{1,0},{2,1},{3,2},{5,4},{6,5},{7,6},{9,8},{10,9},{11,10},{13,12},{... | collective-permute-start | bytes 24584 | tf_op jit(solution)/shard_map/ppermute | solution.py:15
  71.9 28.4 %collective-permute-start.8 = (f32[1,32,512]{2,1,0:T(8,128)S(1)}, f32[1,32,512]{2,1,0:T(8,128)S(1)}, u32[]{:S(2)}, u32[]{:S(2)}) collective-permute-start(f32[1,32,512]{2,1,0:T(8,128)S(1)} %slice.554), channel_id=1, source_target_pairs={{4,0},{8,4},{12,8},{16,12},{20,16},{24,20},{28,24},{32,28},{36,32}... | collective-permute-start | bytes 196616 | tf_op jit(solution)/shard_map/ppermute | solution.py:15
  82.4 5.6 %collective-permute-start.9 = (f32[2,4,1,512]{3,2,1,0:T(1,128)S(1)}, f32[2,4,1,512]{3,2,1,0:T(1,128)S(1)}, u32[]{:S(2)}, u32[]{:S(2)}) collective-permute-start(f32[2,4,1,512]{3,2,1,0:T(1,128)S(1)} %pad_maximum_fusion.70), channel_id=1, source_target_pairs={{0,1},{1,2},{2,3},{4,5},{5,6},{6,7},{8,9},{9,10},{10,11},{12,13},{... | collective-permute-start | bytes 49160 | tf_op jit(solution)/shard_map/ppermute | solution.py:15
  86.0 14.2 %collective-permute-start.10 = (f32[2,1,32,512]{3,2,1,0:T(8,128)S(1)}, f32[2,1,32,512]{3,2,1,0:T(8,128)S(1)}, u32[]{:S(2)}, u32[]{:S(2)}) collective-permute-start(f32[2,1,32,512]{3,2,1,0:T(8,128)S(1)} %pad_maximum_fusion.66), channel_id=1, source_target_pairs={{0,4},{4,8},{8,12},{12,16},{16,20},{20,24},{24,28},{28,32},{32,36}... | collective-permute-start | bytes 393224 | tf_op jit(solution)/shard_map/ppermute | solution.py:15
  102.2 19.3 %collective-permute-start.13 = (f32[4,1,512]{2,1,0:T(1,128)S(1)}, f32[4,1,512]{2,1,0:T(1,128)S(1)}, u32[]{:S(2)}, u32[]{:S(2)}) collective-permute-start(f32[4,1,512]{2,1,0:T(1,128)S(1)} %slice.566), channel_id=1, source_target_pairs={{0,1},{1,2},{2,3},{4,5},{5,6},{6,7},{8,9},{9,10},{10,11},{12,13},{... | collective-permute-start | bytes 24584 | tf_op jit(solution)/shard_map/ppermute | solution.py:15
  105.1 16.5 %collective-permute-start.15 = (f32[2,4,1,512]{3,2,1,0:T(1,128)S(1)}, f32[2,4,1,512]{3,2,1,0:T(1,128)S(1)}, u32[]{:S(2)}, u32[]{:S(2)}) collective-permute-start(f32[2,4,1,512]{3,2,1,0:T(1,128)S(1)} %pad_maximum_fusion.71), channel_id=1, source_target_pairs={{1,0},{2,1},{3,2},{5,4},{6,5},{7,6},{9,8},{10,9},{11,10},{13,12},{... | collective-permute-start | bytes 49160 | tf_op jit(solution)/shard_map/ppermute | solution.py:15
  109.0 16.4 %collective-permute-start.12 = (f32[1,32,512]{2,1,0:T(8,128)S(1)}, f32[1,32,512]{2,1,0:T(8,128)S(1)}, u32[]{:S(2)}, u32[]{:S(2)}) collective-permute-start(f32[1,32,512]{2,1,0:T(8,128)S(1)} %slice.565), channel_id=1, source_target_pairs={{0,4},{4,8},{8,12},{12,16},{16,20},{20,24},{24,28},{28,32},{32,36}... | collective-permute-start | bytes 196616 | tf_op jit(solution)/shard_map/ppermute | solution.py:15
  111.0 14.4 %collective-permute-start.14 = (f32[2,1,32,512]{3,2,1,0:T(8,128)S(1)}, f32[2,1,32,512]{3,2,1,0:T(8,128)S(1)}, u32[]{:S(2)}, u32[]{:S(2)}) collective-permute-start(f32[2,1,32,512]{3,2,1,0:T(8,128)S(1)} %pad_maximum_fusion.67), channel_id=1, source_target_pairs={{4,0},{8,4},{12,8},{16,12},{20,16},{24,20},{28,24},{32,28},{36,32}... | collective-permute-start | bytes 393224 | tf_op jit(solution)/shard_map/ppermute | solution.py:15
  121.6 21.4 %copy-start.51 = (f32[6,1,512]{2,1,0:T(1,128)}, f32[6,1,512]{2,1,0:T(1,128)S(1)}, u32[]{:S(2)}) copy-start(f32[6,1,512]{2,1,0:T(1,128)S(1)} %pad.128) | copy-start | bytes 36868
  121.6 21.3 %copy-start.57 = (f32[6,1,512]{2,1,0:T(1,128)}, f32[6,1,512]{2,1,0:T(1,128)S(1)}, u32[]{:S(2)}) copy-start(f32[6,1,512]{2,1,0:T(1,128)S(1)} %pad.131) | copy-start | bytes 36868
  121.7 21.3 %copy-start.59 = (f32[6,1,512]{2,1,0:T(1,128)}, f32[6,1,512]{2,1,0:T(1,128)S(1)}, u32[]{:S(2)}) copy-start(f32[6,1,512]{2,1,0:T(1,128)S(1)} %pad.129) | copy-start | bytes 36868
  125.3 17.6 %copy-start.40 = (f32[1,32,512]{2,1,0:T(8,128)}, f32[1,32,512]{2,1,0:T(8,128)S(1)}, u32[]{:S(2)}) copy-start(f32[1,32,512]{2,1,0:T(8,128)S(1)} %get-tuple-element.39) | copy-start | bytes 196612
  125.4 17.6 %copy-start.34 = (f32[1,32,512]{2,1,0:T(8,128)}, f32[1,32,512]{2,1,0:T(8,128)S(1)}, u32[]{:S(2)}) copy-start(f32[1,32,512]{2,1,0:T(8,128)S(1)} %collective-permute-done.12) | copy-start | bytes 196612
  126.4 23.5 %all-to-all-start.1 = ((f32[1,64,1,12]{3,2,0,1:T(1,128)}), f32[1,64,1,12]{3,2,0,1:T(1,128)S(1)}, u32[]{:S(2)}, u32[]{:S(2)}) async-start(f32[1,64,1,12]{3,2,0,1:T(1,128)} %copy.49), calls=%async_computation.1 | async-start | bytes 65536 | tf_op jit(solution)/shard_map/all_to_all | solution.py:128
  153.7 5.1 %copy-start.62 = (pred[64]{0:T(512)(128)(4,1)S(1)}, pred[64]{0:T(512)(128)(4,1)}, u32[]{:S(2)}) copy-start(pred[64]{0:T(512)(128)(4,1)} %compare_and_fusion) | copy-start | bytes 196
  186.3 5.3 %copy-start.9 = (f32[4,32,512]{2,1,0:T(8,128)S(1)}, f32[4,32,512]{2,1,0:T(8,128)}, u32[]{:S(2)}) copy-start(f32[4,32,512]{2,1,0:T(8,128)} %param.9) | copy-start | bytes 786436
  186.3 5.3 %copy-start.22 = (f32[4,32,512]{2,1,0:T(8,128)S(1)}, f32[4,32,512]{2,1,0:T(8,128)}, u32[]{:S(2)}) copy-start(f32[4,32,512]{2,1,0:T(8,128)} %copy-done.21) | copy-start | bytes 786436
  189.8 2.8 %copy-start.25 = (f32[4,32,512]{2,1,0:T(8,128)S(1)}, f32[4,32,512]{2,1,0:T(8,128)}, u32[]{:S(2)}) copy-start(f32[4,32,512]{2,1,0:T(8,128)} %copy-done.24) | copy-start | bytes 786436
  189.8 2.8 %copy-start.52 = (f32[6,1,512]{2,1,0:T(1,128)S(1)}, f32[6,1,512]{2,1,0:T(1,128)}, u32[]{:S(2)}) copy-start(f32[6,1,512]{2,1,0:T(1,128)} %copy-done.51) | copy-start | bytes 36868
  192.5 2.8 %copy-start.5 = (f32[4,32,512]{2,1,0:T(8,128)S(1)}, f32[4,32,512]{2,1,0:T(8,128)}, u32[]{:S(2)}) copy-start(f32[4,32,512]{2,1,0:T(8,128)} %copy-done.4) | copy-start | bytes 786436
  192.5 2.8 %copy-start.41 = (f32[1,32,512]{2,1,0:T(8,128)S(1)}, f32[1,32,512]{2,1,0:T(8,128)}, u32[]{:S(2)}) copy-start(f32[1,32,512]{2,1,0:T(8,128)} %copy-done.40) | copy-start | bytes 196612
  193.4 2.8 %copy-start.7 = (f32[4,32,512]{2,1,0:T(8,128)S(1)}, f32[4,32,512]{2,1,0:T(8,128)}, u32[]{:S(2)}) copy-start(f32[4,32,512]{2,1,0:T(8,128)} %copy-done.6) | copy-start | bytes 786436
  193.4 2.8 %copy-start.12 = (f32[6,34,512]{2,1,0:T(8,128)S(1)}, f32[6,34,512]{2,1,0:T(8,128)}, u32[]{:S(2)}) copy-start(f32[6,34,512]{2,1,0:T(8,128)} %get-tuple-element.46) | copy-start | bytes 1253380
  193.4 2.8 %copy-start.60 = (f32[6,1,512]{2,1,0:T(1,128)S(1)}, f32[6,1,512]{2,1,0:T(1,128)}, u32[]{:S(2)}) copy-start(f32[6,1,512]{2,1,0:T(1,128)} %copy-done.59) | copy-start | bytes 36868
  194.3 2.7 %copy-start.14 = (f32[6,34,512]{2,1,0:T(8,128)S(1)}, f32[6,34,512]{2,1,0:T(8,128)}, u32[]{:S(2)}) copy-start(f32[6,34,512]{2,1,0:T(8,128)} %copy-done.13) | copy-start | bytes 1253380
  194.3 2.7 %copy-start.16 = (f32[6,34,512]{2,1,0:T(8,128)S(1)}, f32[6,34,512]{2,1,0:T(8,128)}, u32[]{:S(2)}) copy-start(f32[6,34,512]{2,1,0:T(8,128)} %copy-done.15) | copy-start | bytes 1253380
  194.3 2.7 %copy-start.18 = (f32[6,34,512]{2,1,0:T(8,128)S(1)}, f32[6,34,512]{2,1,0:T(8,128)}, u32[]{:S(2)}) copy-start(f32[6,34,512]{2,1,0:T(8,128)} %copy-done.17) | copy-start | bytes 1253380
  194.3 2.7 %copy-start.28 = (f32[4,32,512]{2,1,0:T(8,128)S(1)}, f32[4,32,512]{2,1,0:T(8,128)}, u32[]{:S(2)}) copy-start(f32[4,32,512]{2,1,0:T(8,128)} %squeeze.137) | copy-start | bytes 786436
  194.3 2.7 %copy-start.29 = (f32[4,32,512]{2,1,0:T(8,128)S(1)}, f32[4,32,512]{2,1,0:T(8,128)}, u32[]{:S(2)}) copy-start(f32[4,32,512]{2,1,0:T(8,128)} %squeeze.142) | copy-start | bytes 786436
  194.3 2.7 %copy-start.30 = (f32[4,32,512]{2,1,0:T(8,128)S(1)}, f32[4,32,512]{2,1,0:T(8,128)}, u32[]{:S(2)}) copy-start(f32[4,32,512]{2,1,0:T(8,128)} %squeeze.141) | copy-start | bytes 786436
  194.3 2.7 %copy-start.31 = (f32[4,32,512]{2,1,0:T(8,128)S(1)}, f32[4,32,512]{2,1,0:T(8,128)}, u32[]{:S(2)}) copy-start(f32[4,32,512]{2,1,0:T(8,128)} %squeeze.140) | copy-start | bytes 786436
  194.4 2.7 %copy-start.32 = (f32[4,32,512]{2,1,0:T(8,128)S(1)}, f32[4,32,512]{2,1,0:T(8,128)}, u32[]{:S(2)}) copy-start(f32[4,32,512]{2,1,0:T(8,128)} %squeeze.139) | copy-start | bytes 786436
  194.4 2.7 %copy-start.33 = (f32[4,32,512]{2,1,0:T(8,128)S(1)}, f32[4,32,512]{2,1,0:T(8,128)}, u32[]{:S(2)}) copy-start(f32[4,32,512]{2,1,0:T(8,128)} %squeeze.138) | copy-start | bytes 786436
  194.4 2.7 %copy-start.37 = (f32[1,32,512]{2,1,0:T(8,128)S(1)}, f32[1,32,512]{2,1,0:T(8,128)}, u32[]{:S(2)}) copy-start(f32[1,32,512]{2,1,0:T(8,128)} %copy-done.36) | copy-start | bytes 196612
  194.4 2.7 %copy-start.39 = (f32[1,32,512]{2,1,0:T(8,128)S(1)}, f32[1,32,512]{2,1,0:T(8,128)}, u32[]{:S(2)}) copy-start(f32[1,32,512]{2,1,0:T(8,128)} %copy-done.38) | copy-start | bytes 196612
  194.4 2.7 %copy-start.45 = (f32[4,32,512]{2,1,0:T(8,128)S(1)}, f32[4,32,512]{2,1,0:T(8,128)}, u32[]{:S(2)}) copy-start(f32[4,32,512]{2,1,0:T(8,128)} %squeeze.148) | copy-start | bytes 786436
  194.4 2.7 %copy-start.46 = (f32[4,32,512]{2,1,0:T(8,128)S(1)}, f32[4,32,512]{2,1,0:T(8,128)}, u32[]{:S(2)}) copy-start(f32[4,32,512]{2,1,0:T(8,128)} %squeeze.147) | copy-start | bytes 786436
  194.4 2.7 %copy-start.47 = (f32[4,32,512]{2,1,0:T(8,128)S(1)}, f32[4,32,512]{2,1,0:T(8,128)}, u32[]{:S(2)}) copy-start(f32[4,32,512]{2,1,0:T(8,128)} %squeeze.146) | copy-start | bytes 786436
  194.4 2.7 %copy-start.48 = (f32[4,32,512]{2,1,0:T(8,128)S(1)}, f32[4,32,512]{2,1,0:T(8,128)}, u32[]{:S(2)}) copy-start(f32[4,32,512]{2,1,0:T(8,128)} %squeeze.145) | copy-start | bytes 786436
  (18 other events, 32.3 us)
where the time goes:
time: 203 us; the launch traced here: 199 us
  starting transfers between devices  99.1 us (49%)
  local copies, waits for them, and re-layouts  44 us (22%)
  other arithmetic  29.7 us (15%)
  waiting for transfers between devices  24.4 us (12%)
    ppermute x16, starting transfers between devices, passed_along(): lax.ppermute(value, axis, [(source, source + steps) for source in range(f...  72.2 us
    ppermute x16, waiting for transfers between devices, passed_along(): lax.ppermute(value, axis, [(source, source + steps) for source in range(f...  20.3 us
    squeeze x12, local copies, waits for them, and re-layouts, on_device(): stored = [forward[6 * step + index] for index in range(6)]  18.4 us
    all_to_all x1, starting transfers between devices, on_device(): lax.all_to_all(scales, 'gx', split_axis=1, concat_axis=0, tiled=True)  13.5 us
    all_to_all x1, starting transfers between devices, on_device(): lax.all_to_all(packed, 'gx', split_axis=1, concat_axis=0, tiled=True)  13.3 us
    slice x1, local copies, waits for them, and re-layouts, on_device(): stored = [forward[6 * step + index] for index in range(6)]  10 us
    unnamed x8, other arithmetic  7 us
    gather x1, local copies, waits for them, and re-layouts, on_device(): ordered = jnp.take(blocks, inverse, axis=0)  5.12 us
  transfers between devices with their start and end apart: 18, of which 7 were waited for; matrix products, arithmetic and copies ran while one was open for 12% of the time, Pallas kernels for 0%

commit v1 on v0

v1 whole, which is shorter than its diff:
```python
import jax
import jax.numpy as jnp
from jax import lax
from jax.experimental import pallas as pl
from jax.experimental.pallas import tpu as pltpu
from jax.sharding import PartitionSpec as P

courant = 0.15
FACTOR_UP = 2.0**35
FACTOR_DOWN = 2.0**-35
F32 = jnp.float32
ANY = pl.BlockSpec(memory_space=pl.ANY)
VMEM = pl.BlockSpec(memory_space=pltpu.VMEM)


def below_y(field, row):
    y = lax.broadcasted_iota(jnp.int32, field.shape, 0)
    return jnp.where(y == 0, row, pltpu.roll(field, 1, 0))


def above_y(field, row):
    count = field.shape[0]
    y = lax.broadcasted_iota(jnp.int32, field.shape, 0)
    return jnp.where(y == count - 1, row, pltpu.roll(field, count - 1, 0))


def below_z(field):
    z = lax.broadcasted_iota(jnp.int32, field.shape, 1)
    return jnp.where(z == 0, 0.0, pltpu.roll(field, 1, 1))


def above_z(field):
    count = field.shape[1]
    z = lax.broadcasted_iota(jnp.int32, field.shape, 1)
    return jnp.where(z == count - 1, 0.0, pltpu.roll(field, count - 1, 1))


def velocity_plane(vel, scaled, sxx, sxx_next, syy, syy_row, szz, sxy, sxy_prior, sxy_row, sxz, sxz_prior, syz, syz_row):
    vx, vy, vz = vel
    vx = vx - scaled * (sxx_next - sxx + (sxy - below_y(sxy, sxy_row)) + (sxz - below_z(sxz)))
    vy = vy - scaled * (sxy - sxy_prior + (above_y(syy, syy_row) - syy) + (syz - below_z(syz)))
    vz = vz - scaled * (sxz - sxz_prior + (syz - below_y(syz, syz_row)) + (above_z(szz) - szz))
    return vx, vy, vz


def strain_plane(vx, vx_prior, vx_row, vy, vy_next, vy_row, vz, vz_next, vz_row):
    exx = vx - vx_prior
    eyy = vy - below_y(vy, vy_row)
    ezz = vz - below_z(vz)
    exy = (above_y(vx, vx_row) - vx) + (vy_next - vy)
    exz = (above_z(vx) - vx) + (vz_next - vz)
    eyz = (above_z(vy) - vy) + (above_y(vz, vz_row) - vz)
    return exx, eyy, ezz, exy, exz, eyz


def stress_plane(stress, strain, lam, mu):
    trace = strain[0] + strain[1] + strain[2]
    direct = [stress[k] - courant * (lam * trace + 2.0 * mu * strain[k]) for k in range(3)]
    shear = [stress[k] - courant * mu * strain[k] for k in range(3, 6)]
    return direct + shear


def prepare(adj, lam, mu, packed, scales, message, to_next_x, to_prior_x, to_next_y, to_prior_y, words, rows, sems, word_sem):
    cells_x = adj.shape[1]
    cells_y = adj.shape[2]
    count = scales.shape[0]
    per = packed.shape[0] // count
    word_copy = pltpu.make_async_copy(packed, words, word_sem)
    word_copy.start()
    plans = [
        (adj.at[6, cells_x - 1], to_next_x.at[0]),
        (adj.at[7, cells_x - 1], to_next_x.at[1]),
        (mu.at[cells_x - 1], to_next_x.at[2]),
        (adj.at[3, 0], to_prior_x.at[0]),
        (lam.at[0], to_prior_x.at[1]),
        (mu.at[0], to_prior_x.at[2]),
        (adj.at[6, :, pl.ds(cells_y - 8, 8)], rows.at[0]),
        (adj.at[8, :, pl.ds(cells_y - 8, 8)], rows.at[1]),
        (mu.at[:, pl.ds(cells_y - 8, 8)], rows.at[2]),
        (adj.at[4, :, pl.ds(0, 8)], rows.at[3]),
        (lam.at[:, pl.ds(0, 8)], rows.at[4]),
        (mu.at[:, pl.ds(0, 8)], rows.at[5]),
    ]
    copies = [pltpu.make_async_copy(source, target, sems.at[n]) for n, (source, target) in enumerate(plans)]
    for copy in copies:
        copy.start()
    factor = (scales[...] * FACTOR_UP).astype(jnp.int32)
    message[pl.ds(per, count, stride=per + 1), :] = jnp.pad(factor, ((0, 0), (0, 128 - factor.shape[1])))
    for copy in copies:
        copy.wait()
    for k in range(3):
        for x in range(cells_x):
            to_next_y[k, x : x + 1, :] = rows[k, x, 7:8, :]
            to_prior_y[k, x : x + 1, :] = rows[3 + k, x, 0:1, :]
    word_copy.wait()
    for r in range(per):
        message[pl.ds(r, count, stride=per + 1), :] = words[pl.ds(r, count, stride=per), :]


def first_velocity(adj, buoy, prior_x, next_x, prior_y, next_y, v, to_next_x, to_prior_x, to_next_y, to_prior_y, to_lower, to_upper):
    cells_x = adj.shape[1]
    cells_y = adj.shape[2]
    for x in range(cells_x):
        sxy_prior = adj[6, x - 1] if x > 0 else prior_x[0]
        sxz_prior = adj[7, x - 1] if x > 0 else prior_x[1]
        sxx_next = adj[3, x + 1] if x < cells_x - 1 else next_x[0]
        new = velocity_plane(
            (adj[0, x], adj[1, x], adj[2, x]), courant * buoy[x], adj[3, x], sxx_next, adj[4, x], next_y[0, x : x + 1], adj[5, x],
            adj[6, x], sxy_prior, prior_y[0, x : x + 1], adj[7, x], sxz_prior, adj[8, x], prior_y[1, x : x + 1],
        )
        for k in range(3):
            v[k, x] = new[k]
            to_next_y[k, x : x + 1, :] = new[k][cells_y - 1 :, :]
            to_prior_y[k, x : x + 1, :] = new[k][0:1, :]
            if x == cells_x - 1:
                to_next_x[k] = new[k]
            if x == 0:
                to_prior_x[k] = new[k]
        if x == cells_x - 1:
            to_lower[...] = new[0][0:1, :]
        if x == 0:
            to_upper[...] = new[1][cells_y - 1 :, :]


def middle(
    adj, buoy, lam, mu, s_prior_x, s_next_x, s_prior_y, s_next_y, v, last_y, first_y,
    v_prior_x, v_next_x, v_prior_y, v_next_y, vx_corner, vy_corner,
    v_new, stress, strain, to_next_x, to_prior_x, to_next_y, to_prior_y,
):
    cells_x = adj.shape[1]
    cells_y = adj.shape[2]
    last = cells_x - 1
    vx_m, vy_m, vz_m = v_prior_x[0], v_prior_x[1], v_prior_x[2]
    vx_n, vy_n, vz_n = v_next_x[0], v_next_x[1], v_next_x[2]
    exx = vx_n - v[0, last]
    trace = exx + (vy_n - below_y(vy_n, vy_corner[...])) + (vz_n - below_z(vz_n))
    sxx_next = s_next_x[0] - courant * (s_next_x[1] * trace + 2.0 * s_next_x[2] * exx)
    exy = (above_y(vx_m, vx_corner[...]) - vx_m) + (v[1, 0] - vy_m)
    exz = (above_z(vx_m) - vx_m) + (v[2, 0] - vz_m)
    sxy_prior = s_prior_x[0] - courant * s_prior_x[2] * exy
    sxz_prior = s_prior_x[1] - courant * s_prior_x[2] * exz
    above = v_next_y[0]
    exx = above - jnp.concatenate([vx_corner[...], above[:last]], axis=0)
    eyy = v_next_y[1] - last_y[1]
    trace = exx + eyy + (v_next_y[2] - below_z(v_next_y[2]))
    syy_rows = s_next_y[0] - courant * (s_next_y[1] * trace + 2.0 * s_next_y[2] * eyy)
    under = v_prior_y[1]
    exy = (first_y[0] - v_prior_y[0]) + (jnp.concatenate([under[1:], vy_corner[...]], axis=0) - under)
    eyz = (above_z(under) - under) + (first_y[2] - v_prior_y[2])
    sxy_rows = s_prior_y[0] - courant * s_prior_y[2] * exy
    syz_rows = s_prior_y[1] - courant * s_prior_y[2] * eyz
    for x in range(cells_x):
        e = strain_plane(
            v[0, x], v[0, x - 1] if x > 0 else vx_m, v_next_y[0, x : x + 1],
            v[1, x], v[1, x + 1] if x < last else vy_n, v_prior_y[1, x : x + 1],
            v[2, x], v[2, x + 1] if x < last else vz_n, v_next_y[2, x : x + 1],
        )
        s = stress_plane([adj[3 + k, x] for k in range(6)], e, lam[x], mu[x])
        for k in range(6):
            strain[k, x] = e[k]
            stress[k, x] = s[k]
    for x in range(cells_x):
        new = velocity_plane(
            (v[0, x], v[1, x], v[2, x]), courant * buoy[x],
            stress[0, x], stress[0, x + 1] if x < last else sxx_next, stress[1, x], syy_rows[x : x + 1], stress[2, x],
            stress[3, x], stress[3, x - 1] if x > 0 else sxy_prior, sxy_rows[x : x + 1],
            stress[4, x], stress[4, x - 1] if x > 0 else sxz_prior, stress[5, x], syz_rows[x : x + 1],
        )
        for k in range(3):
            v_new[k, x] = new[k]
        to_next_y[0, x : x + 1, :] = new[1][cells_y - 1 :, :]
        to_prior_y[0, x : x + 1, :] = new[0][0:1, :]
        to_prior_y[1, x : x + 1, :] = new[2][0:1, :]
        if x == last:
            to_next_x[0] = new[0]
        if x == 0:
            to_prior_x[0] = new[1]
            to_prior_x[1] = new[2]


def second_stress(v, stress, lam, mu, prior_x, next_x, prior_y, next_y, out, strain):
    cells_x = v.shape[1]
    last = cells_x - 1
    for x in range(cells_x):
        e = strain_plane(
            v[0, x], v[0, x - 1] if x > 0 else prior_x[0], next_y[0, x : x + 1],
            v[1, x], v[1, x + 1] if x < last else next_x[0], prior_y[0, x : x + 1],
            v[2, x], v[2, x + 1] if x < last else next_x[1], next_y[1, x : x + 1],
        )
        s = stress_plane([stress[k, x] for k in range(6)], e, lam[x], mu[x])
        for k in range(3):
            out[k, x] = v[k, x]
        for k in range(6):
            strain[k, x] = e[k]
            out[3 + k, x] = s[k]


def gradients(message, perm, strain1, strain2, out):
    count = perm.shape[1]
    per = message.shape[0] // count
    cells_x, cells_y, cells_z = strain1.shape[1:]
    rows = cells_x * cells_y
    both = jnp.concatenate([perm[...], perm[...]], axis=1)
    r = lax.broadcasted_iota(jnp.int32, (rows, 2 * count), 0)
    k = lax.broadcasted_iota(jnp.int32, (rows, 2 * count), 1)
    mine = both == lax.shift_right_logical(r, 1)
    half = (k >= count) == ((r & 1) == 1)
    pick = jnp.where(mine & half, 1.0, 0.0).astype(jnp.bfloat16)
    pick_factor = jnp.where(mine & (k < count), 1.0, 0.0)
    factor = message[pl.ds(per - 1, count, stride=per), :].astype(F32) * FACTOR_DOWN
    factor = jnp.concatenate([factor, jnp.zeros_like(factor)], axis=0)
    factor = lax.dot(pick_factor, factor, precision=lax.Precision.HIGHEST, preferred_element_type=F32)

    def forward(c):
        w = [message[pl.ds(2 * c + t, count, stride=per), :] for t in range(2)]
        byte = [lambda w: w & 255, lambda w: lax.shift_right_logical(w, 8) & 255, lambda w: lax.shift_right_logical(w, 16) & 255]
        parts = [[(f(v) - 128) for v in w] for f in byte] + [[lax.shift_right_arithmetic(v, 24) for v in w]]
        parts = [[v.astype(F32).astype(jnp.bfloat16) for v in p] for p in parts]
        low = jnp.concatenate(parts[0] + parts[1], axis=1)
        high = jnp.concatenate(parts[2] + parts[3], axis=1)
        table = jnp.concatenate([low, high], axis=0)
        picked = lax.dot(pick, table, preferred_element_type=F32)
        return picked * factor[:, c : c + 1]

    grad_lambda = None
    grad_mu = None
    for step, strain in enumerate((strain1, strain2)):
        f = [forward(6 * step + n) for n in range(6)]
        e = [strain[n].reshape(rows, cells_z) for n in range(6)]
        add_lambda = (e[0] + e[1] + e[2]) * (f[0] + f[1] + f[2])
        add_mu = 2.0 * (e[0] * f[0] + e[1] * f[1] + e[2] * f[2])
        grad_lambda = add_lambda if step == 0 else grad_lambda + add_lambda
        grad_mu = add_mu if step == 0 else grad_mu + add_mu
        grad_mu = grad_mu + e[3] * f[3] + e[4] * f[4] + e[5] * f[5]
    out[0] = grad_lambda.reshape(cells_x, cells_y, cells_z)
    out[1] = grad_mu.reshape(cells_x, cells_y, cells_z)


def on_device(adjoint, buoyancy, lame_lambda, shear_mu, packed, scales, perm):
    cells_x, cells_y, cells_z = buoyancy.shape
    owners, comp, width = packed.shape[1], packed.shape[3], packed.shape[4]
    per = comp * width // 128

    def shape(*dims):
        return jax.ShapeDtypeStruct(dims, F32)

    plane = (cells_y, cells_z)
    line = (cells_x, cells_z)

    count_x = lax.axis_size("gx")
    count_y = lax.axis_size("gy")

    def along(value, step_x, step_y):
        pairs = [
            (x * count_y + y, (x + step_x) * count_y + y + step_y)
            for x in range(count_x)
            for y in range(count_y)
            if 0 <= x + step_x < count_x and 0 <= y + step_y < count_y
        ]
        return lax.ppermute(value, ("gx", "gy"), pairs)

    words = packed.reshape(owners * per, 128)
    message, nx, px, ny, py = pl.pallas_call(
        prepare,
        out_shape=(
            jax.ShapeDtypeStruct((owners * (per + 1), 128), jnp.int32),
            shape(3, *plane), shape(3, *plane), shape(3, *line), shape(3, *line),
        ),
        in_specs=[ANY, ANY, ANY, ANY, VMEM],
        out_specs=(VMEM,) * 5,
        scratch_shapes=[
            pltpu.VMEM((owners * per, 128), jnp.int32),
            pltpu.VMEM((6, cells_x, 8, cells_z), F32),
            pltpu.SemaphoreType.DMA((12,)),
            pltpu.SemaphoreType.DMA,
        ],
        name="prepare",
    )(adjoint, lame_lambda, shear_mu, words, scales.reshape(owners, comp))
    s_prior_x = along(nx, 1, 0)
    s_next_x = along(px, -1, 0)
    s_prior_y = along(ny, 0, 1)
    s_next_y = along(py, 0, -1)
    message = lax.all_to_all(message.reshape(owners, per + 1, 1, 128), "gx", split_axis=0, concat_axis=0, tiled=True)
    message = message.reshape(owners * (per + 1), 128)

    v, nx, px, ny, py, low, up = pl.pallas_call(
        first_velocity,
        out_shape=(
            shape(3, cells_x, *plane), shape(3, *plane), shape(3, *plane), shape(3, *line), shape(3, *line),
            shape(1, cells_z), shape(1, cells_z),
        ),
        in_specs=[VMEM] * 6,
        out_specs=(VMEM,) * 7,
        name="first_velocity",
    )(adjoint, buoyancy, s_prior_x, s_next_x, s_prior_y, s_next_y)
    v_prior_x = along(nx, 1, 0)
    v_next_x = along(px, -1, 0)
    v_prior_y = along(ny, 0, 1)
    v_next_y = along(py, 0, -1)
    vx_corner = along(low, 1, -1)
    vy_corner = along(up, -1, 1)

    v2, stress, strain1, nx, px, ny2, py2 = pl.pallas_call(
        middle,
        out_shape=(
            shape(3, cells_x, *plane), shape(6, cells_x, *plane), shape(6, cells_x, *plane),
            shape(1, *plane), shape(2, *plane), shape(1, *line), shape(2, *line),
        ),
        in_specs=[VMEM] * 17,
        out_specs=(VMEM,) * 7,
        name="middle",
    )(
        adjoint, buoyancy, lame_lambda, shear_mu, s_prior_x, s_next_x, s_prior_y, s_next_y, v, ny, py,
        v_prior_x, v_next_x, v_prior_y, v_next_y, vx_corner, vy_corner,
    )
    w_prior_x = along(nx, 1, 0)
    w_next_x = along(px, -1, 0)
    w_prior_y = along(ny2, 0, 1)
    w_next_y = along(py2, 0, -1)

    adjoint_out, strain2 = pl.pallas_call(
        second_stress,
        out_shape=(shape(*adjoint.shape), shape(6, cells_x, *plane)),
        in_specs=[VMEM] * 8,
        out_specs=(VMEM,) * 2,
        name="second_stress",
    )(v2, stress, lame_lambda, shear_mu, w_prior_x, w_next_x, w_prior_y, w_next_y)

    grads = pl.pallas_call(
        gradients,
        out_shape=shape(2, cells_x, *plane),
        in_specs=[VMEM] * 4,
        out_specs=VMEM,
        name="gradients",
    )(message, perm, strain1, strain2)
    return adjoint_out, grads


def solution(mesh):
    return jax.shard_map(
        on_device,
        mesh=mesh,
        in_specs=(
            P(None, "gx", "gy", None),
            P("gx", "gy", None),
            P("gx", "gy", None),
            P("gx", "gy", None),
            P("gx", None, "gy", None, None),
            P("gx", None, "gy", None),
            P("gx", None),
        ),
        out_specs=(P(None, "gx", "gy", None), P(None, "gx", "gy", None)),
        check_vma=False,
    )
```

time: 203 us -> 126 us (0.62); the launches traced: 199 us -> 125 us
  local copies, waits for them, and re-layouts: 44 us -> 5.06 us
  other arithmetic: 29.7 us -> 0 us
  starting transfers between devices: 99.1 us -> 69.7 us
  Pallas kernels: 0 us -> 19.9 us
  waiting for transfers between devices: 24.4 us -> 29.4 us
    squeeze x21 -> x0, local copies, waits for them, and re-layouts: 21.6 us -> none  [the longest x12 18.4 us: on_device(): stored = [forward[6 * step + index] for index in range(6)]]
    pallas_call x0 -> x5, Pallas kernels: none -> 19.9 us  [the longest x1 4.95 us: on_device(): pl.pallas_call(middle, out_shape=(shape(3, cells_x, *plane), shape(6, cel...]
    ppermute x16 -> x14, starting transfers between devices: 72.2 us -> 56.6 us  [along(): return lax.ppermute(value, ('gx', 'gy'), pairs)]
    all_to_all x2 -> x1, starting transfers between devices: 26.9 us -> 13.1 us  [on_device(): lax.all_to_all(message.reshape(owners, per + 1, 1, 128), 'gx', split_axis...]
    slice x9 -> x0, local copies, waits for them, and re-layouts: 11.6 us -> none  [the longest x1 10 us: on_device(): stored = [forward[6 * step + index] for index in range(6)]]
    ppermute x16 -> x14, waiting for transfers between devices: 20.3 us -> 29.4 us  [along(): return lax.ppermute(value, ('gx', 'gy'), pairs)]
    unnamed x8 -> x0, other arithmetic: 7 us -> none
    sub x7 -> x0, other arithmetic: 6.51 us -> none  [the longest x1 2.97 us: unpack(): low = (words & 255) - 128]
  transfers between devices with their start and end apart: 18 -> 15, of which waited for: 7 -> 6; matrix products, arithmetic and copies ran while one was open for 12% -> 0% of each run, Pallas kernels for 0% -> 10%
where the time goes in v1:
time: 126 us; the launch traced here: 125 us
  starting transfers between devices  69.7 us (55%)
  waiting for transfers between devices  29.4 us (23%)
  Pallas kernels  19.9 us (16%)
  local copies, waits for them, and re-layouts  5.06 us (4%)
    ppermute x14, starting transfers between devices, along(): return lax.ppermute(value, ('gx', 'gy'), pairs)  56.6 us
    ppermute x14, waiting for transfers between devices, along(): return lax.ppermute(value, ('gx', 'gy'), pairs)  29.4 us
    all_to_all x1, starting transfers between devices, on_device(): lax.all_to_all(message.reshape(owners, per + 1, 1, 128), 'gx', split_axis...  13.1 us
    unnamed x39, local copies, waits for them, and re-layouts  5.06 us
    pallas_call x1, Pallas kernels, on_device(): pl.pallas_call(middle, out_shape=(shape(3, cells_x, *plane), shape(6, cel...  4.95 us
    pallas_call x1, Pallas kernels, on_device(): pl.pallas_call(second_stress, out_shape=(shape(*adjoint.shape), shape(6,...  4.25 us
    pallas_call x1, Pallas kernels, on_device(): pl.pallas_call(gradients, out_shape=shape(2, cells_x, *plane), in_specs=[...  3.99 us
    pallas_call x1, Pallas kernels, on_device(): pl.pallas_call(prepare, out_shape=(jax.ShapeDtypeStruct((owners * (per +...  3.43 us
  transfers between devices with their start and end apart: 15, of which 6 were waited for; matrix products, arithmetic and copies ran while one was open for 0% of the time, Pallas kernels for 10%

profile of v1, /device:TPU:70, one launch (start us, length us, event | category | flops | bytes accessed | tf_op | source)
XLA Modules:
  0.0 125.0 jit_solution(11625231812979208046)
XLA Ops:
  0.6 1.4 %copy.11 = f32[1,64,1,12]{3,1,2,0:T(8,128)} copy(f32[1,64,1,12]{1,2,3,0:T(1,128)} %param.12) | data formatting | bytes 6144 | tf_op args[5]
  2.0 3.4 %prepare.1 = (s32[1600,128]{1,0:T(8,128)}, f32[3,32,512]{2,1,0:T(8,128)}, f32[3,32,512]{2,1,0:T(8,128)}, f32[3,4,512]{2,1,0:T(4,128)}, f32[3,4,512]{2,1,0:T(4,128)}) custom-call(f32[9,4,32,512]{3,2,1,0:T(8,128)} %adj.5, f32[4,32,512]{2,1,0:T(8,128)} %lam.5, f32[4,32,512]{2,1,0:T(8,128)} %mu.5, s32[1536,128]{1,0:T(8,128)} %bitcast.6, f32[64,12]{1,0:T(8,128)} %bitcast.7), custom_call_target="tpu_custom_call" | custom-call | tf_op jit(solution)/shard_map/prepare/pallas_call | solution.py:263
  5.5 0.0 copy-start.16
  5.5 0.0 copy-start.15
  5.5 0.0 copy-start.18
  5.5 0.0 copy-start.17
  5.5 13.1 %all-to-all-start = ((s32[64,25,1,128]{3,2,1,0:T(1,128)}), s32[64,25,1,128]{3,2,1,0:T(1,128)S(1)}, u32[]{:S(2)}, u32[]{:S(2)}) async-start(s32[64,25,1,128]{3,2,1,0:T(1,128)} %bitcast.5), calls=%async_computation | async-start | bytes 1638400 | tf_op jit(solution)/shard_map/all_to_all | solution.py:283
  18.7 0.0 copy-done.16
  18.7 2.0 %collective-permute-start = (f32[3,32,512]{2,1,0:T(8,128)S(1)}, f32[3,32,512]{2,1,0:T(8,128)S(1)}, u32[]{:S(2)}, u32[]{:S(2)}) collective-permute-start(f32[3,32,512]{2,1,0:T(8,128)S(1)} %copy-done.16), channel_id=1, source_target_pairs={{0,4},{1,5},{2,6},{3,7},{4,8},{5,9},{6,10},{7,11},{8,12},{9,13},{1... | collective-permute-start | bytes 589832 | tf_op jit(solution)/shard_map/ppermute | solution.py:260
  20.7 0.0 copy-done.15
  20.7 10.4 %collective-permute-start.1 = (f32[3,32,512]{2,1,0:T(8,128)S(1)}, f32[3,32,512]{2,1,0:T(8,128)S(1)}, u32[]{:S(2)}, u32[]{:S(2)}) collective-permute-start(f32[3,32,512]{2,1,0:T(8,128)S(1)} %copy-done.15), channel_id=1, source_target_pairs={{4,0},{5,1},{6,2},{7,3},{8,4},{9,5},{10,6},{11,7},{12,8},{13,9},{1... | collective-permute-start | bytes 589832 | tf_op jit(solution)/shard_map/ppermute | solution.py:260
  31.2 0.0 copy-done.18
  31.2 2.9 %collective-permute-start.2 = (f32[3,4,512]{2,1,0:T(4,128)S(1)}, f32[3,4,512]{2,1,0:T(4,128)S(1)}, u32[]{:S(2)}, u32[]{:S(2)}) collective-permute-start(f32[3,4,512]{2,1,0:T(4,128)S(1)} %copy-done.18), channel_id=1, source_target_pairs={{0,1},{1,2},{2,3},{4,5},{5,6},{6,7},{8,9},{9,10},{10,11},{12,13},{... | collective-permute-start | bytes 73736 | tf_op jit(solution)/shard_map/ppermute | solution.py:260
  34.1 0.0 copy-done.17
  34.1 2.9 %collective-permute-start.3 = (f32[3,4,512]{2,1,0:T(4,128)S(1)}, f32[3,4,512]{2,1,0:T(4,128)S(1)}, u32[]{:S(2)}, u32[]{:S(2)}) collective-permute-start(f32[3,4,512]{2,1,0:T(4,128)S(1)} %copy-done.17), channel_id=1, source_target_pairs={{1,0},{2,1},{3,2},{5,4},{6,5},{7,6},{9,8},{10,9},{11,10},{13,12},{... | collective-permute-start | bytes 73736 | tf_op jit(solution)/shard_map/ppermute | solution.py:260
  37.0 4.3 %collective-permute-done.2.prior_y.s_prior_y = f32[3,4,512]{2,1,0:T(4,128)S(1)} collective-permute-done((f32[3,4,512]{2,1,0:T(4,128)S(1)}, f32[3,4,512]{2,1,0:T(4,128)S(1)}, u32[]{:S(2)}, u32[]{:S(2)}) %collective-permute-start.2) | collective-permute-done | bytes 24608 | tf_op jit(solution)/shard_map/ppermute | solution.py:260
  41.3 0.0 copy-start.6
  41.3 0.0 collective-permute-done.3.next_y.s_next_y
  41.3 0.0 copy-start.7
  41.3 7.8 %collective-permute-done.prior_x.s_prior_x = f32[3,32,512]{2,1,0:T(8,128)S(1)} collective-permute-done((f32[3,32,512]{2,1,0:T(8,128)S(1)}, f32[3,32,512]{2,1,0:T(8,128)S(1)}, u32[]{:S(2)}, u32[]{:S(2)}) %collective-permute-start) | collective-permute-done | bytes 196640 | tf_op jit(solution)/shard_map/ppermute | solution.py:260
  49.1 0.0 collective-permute-done.1.next_x.s_next_x
  49.1 0.0 copy-done.6
  49.1 0.0 copy-done.7
  49.1 0.7 copy-done.1
  49.8 0.7 copy-done.2
  50.5 3.3 %first_velocity.1 = (f32[3,4,32,512]{3,2,1,0:T(8,128)}, f32[3,32,512]{2,1,0:T(8,128)}, f32[3,32,512]{2,1,0:T(8,128)}, f32[3,4,512]{2,1,0:T(4,128)}, f32[3,4,512]...) custom-call(f32[9,4,32,512]{3,2,1,0:T(8,128)} %adj.5, f32[4,32,512]{2,1,0:T(8,128)} %buoy.3, ...), custom_call_target="tpu_custom_call" | custom-call | tf_op jit(solution)/shard_map/first_velocity/pallas_call | solution.py:286
  53.7 1.9 %collective-permute-start.4 = (f32[3,32,512]{2,1,0:T(8,128)}, f32[3,32,512]{2,1,0:T(8,128)S(1)}, u32[]{:S(2)}, u32[]{:S(2)}) collective-permute-start(f32[3,32,512]{2,1,0:T(8,128)} %get-tuple-element.30), channel_id=1, source_target_pairs={{0,4},{1,5},{2,6},{3,7},{4,8},{5,9},{6,10},{7,11},{8,12},{9,13},{1... | collective-permute-start | bytes 589832 | tf_op jit(solution)/shard_map/ppermute | solution.py:260
  55.7 10.6 %collective-permute-start.5 = (f32[3,32,512]{2,1,0:T(8,128)}, f32[3,32,512]{2,1,0:T(8,128)S(1)}, u32[]{:S(2)}, u32[]{:S(2)}) collective-permute-start(f32[3,32,512]{2,1,0:T(8,128)} %get-tuple-element.31), channel_id=1, source_target_pairs={{4,0},{5,1},{6,2},{7,3},{8,4},{9,5},{10,6},{11,7},{12,8},{13,9},{1... | collective-permute-start | bytes 589832 | tf_op jit(solution)/shard_map/ppermute | solution.py:260
  66.2 2.4 %collective-permute-start.6 = (f32[3,4,512]{2,1,0:T(4,128)}, f32[3,4,512]{2,1,0:T(4,128)S(1)}, u32[]{:S(2)}, u32[]{:S(2)}) collective-permute-start(f32[3,4,512]{2,1,0:T(4,128)} %get-tuple-element.28.last_y), channel_id=1, source_target_pairs={{0,1},{1,2},{2,3},{4,5},{5,6},{6,7},{8,9},{9,10},{10,11},{12,13},{... | collective-permute-start | bytes 73736 | tf_op jit(solution)/shard_map/ppermute | solution.py:260
  68.6 3.5 %collective-permute-start.7 = (f32[3,4,512]{2,1,0:T(4,128)}, f32[3,4,512]{2,1,0:T(4,128)S(1)}, u32[]{:S(2)}, u32[]{:S(2)}) collective-permute-start(f32[3,4,512]{2,1,0:T(4,128)} %get-tuple-element.29.first_y), channel_id=1, source_target_pairs={{1,0},{2,1},{3,2},{5,4},{6,5},{7,6},{9,8},{10,9},{11,10},{13,12},{... | collective-permute-start | bytes 73736 | tf_op jit(solution)/shard_map/ppermute | solution.py:260
  72.1 1.9 %collective-permute-start.8 = (f32[1,512]{1,0:T(1,128)}, f32[1,512]{1,0:T(1,128)S(1)}, u32[]{:S(2)}, u32[]{:S(2)}) collective-permute-start(f32[1,512]{1,0:T(1,128)} %get-tuple-element.32), channel_id=1, source_target_pairs={{1,4},{2,5},{3,6},{5,8},{6,9},{7,10},{9,12},{10,13},{11,14},{13,16... | collective-permute-start | bytes 6152 | tf_op jit(solution)/shard_map/ppermute | solution.py:260
  74.0 9.2 %collective-permute-done.8.vx_corner = f32[1,512]{1,0:T(1,128)S(1)} collective-permute-done((f32[1,512]{1,0:T(1,128)}, f32[1,512]{1,0:T(1,128)S(1)}, u32[]{:S(2)}, u32[]{:S(2)}) %collective-permute-start.8) | collective-permute-done | bytes 2080 | tf_op jit(solution)/shard_map/ppermute | solution.py:260
  83.2 1.9 %collective-permute-start.9 = (f32[1,512]{1,0:T(1,128)}, f32[1,512]{1,0:T(1,128)S(1)}, u32[]{:S(2)}, u32[]{:S(2)}) collective-permute-start(f32[1,512]{1,0:T(1,128)} %get-tuple-element.33), channel_id=1, source_target_pairs={{4,1},{5,2},{6,3},{8,5},{9,6},{10,7},{12,9},{13,10},{14,11},{16,13... | collective-permute-start | bytes 6152 | tf_op jit(solution)/shard_map/ppermute | solution.py:260
  85.1 3.2 %collective-permute-done.9.vy_corner = f32[1,512]{1,0:T(1,128)S(1)} collective-permute-done((f32[1,512]{1,0:T(1,128)}, f32[1,512]{1,0:T(1,128)S(1)}, u32[]{:S(2)}, u32[]{:S(2)}) %collective-permute-start.9) | collective-permute-done | bytes 2080 | tf_op jit(solution)/shard_map/ppermute | solution.py:260
  88.3 0.0 collective-permute-done.6.v_prior_y
  88.3 0.0 collective-permute-done.7.v_next_y
  88.3 0.0 copy-start.10
  88.3 0.0 collective-permute-done.4.v_prior_x
  88.4 0.0 copy-start.3
  88.4 0.0 collective-permute-done.5.v_next_x
  88.4 0.0 copy-start.4
  88.4 0.0 copy-done.13
  88.4 0.5 copy-done.14
  88.9 0.1 copy-done.9
  88.9 0.0 copy-done.10
  89.0 0.1 copy-done.3
  89.1 0.1 copy-done.4
  89.1 4.9 %middle.1 = (f32[3,4,32,512]{3,2,1,0:T(8,128)}, f32[6,4,32,512]{3,2,1,0:T(8,128)}, f32[6,4,32,512]{3,2,1,0:T(8,128)}, f32[1,32,512]{2,1,0:T(8,128)}, f32[2,32,51...) custom-call(f32[9,4,32,512]{3,2,1,0:T(8,128)} %adj.5, f32[4,32,512]{2,1,0:T(8,128)} %buoy.3, ...), custom_call_target="tpu_custom_call" | custom-call | tf_op jit(solution)/shard_map/middle/pallas_call | solution.py:303
  94.1 8.4 %collective-permute-start.11 = (f32[2,32,512]{2,1,0:T(8,128)}, f32[2,32,512]{2,1,0:T(8,128)S(1)}, u32[]{:S(2)}, u32[]{:S(2)}) collective-permute-start(f32[2,32,512]{2,1,0:T(8,128)} %get-tuple-element.37), channel_id=1, source_target_pairs={{4,0},{5,1},{6,2},{7,3},{8,4},{9,5},{10,6},{11,7},{12,8},{13,9},{1... | collective-permute-start | bytes 393224 | tf_op jit(solution)/shard_map/ppermute | solution.py:260
  102.5 1.9 %collective-permute-start.10 = (f32[1,32,512]{2,1,0:T(8,128)}, f32[1,32,512]{2,1,0:T(8,128)S(1)}, u32[]{:S(2)}, u32[]{:S(2)}) collective-permute-start(f32[1,32,512]{2,1,0:T(8,128)} %get-tuple-element.36), channel_id=1, source_target_pairs={{0,4},{1,5},{2,6},{3,7},{4,8},{5,9},{6,10},{7,11},{8,12},{9,13},{1... | collective-permute-start | bytes 196616 | tf_op jit(solution)/shard_map/ppermute | solution.py:260
  104.4 1.9 %collective-permute-start.13 = (f32[2,4,512]{2,1,0:T(4,128)}, f32[2,4,512]{2,1,0:T(4,128)S(1)}, u32[]{:S(2)}, u32[]{:S(2)}) collective-permute-start(f32[2,4,512]{2,1,0:T(4,128)} %get-tuple-element.39), channel_id=1, source_target_pairs={{1,0},{2,1},{3,2},{5,4},{6,5},{7,6},{9,8},{10,9},{11,10},{13,12},{... | collective-permute-start | bytes 49160 | tf_op jit(solution)/shard_map/ppermute | solution.py:260
  106.3 3.9 %collective-permute-start.12 = (f32[1,4,512]{2,1,0:T(4,128)}, f32[1,4,512]{2,1,0:T(4,128)S(1)}, u32[]{:S(2)}, u32[]{:S(2)}) collective-permute-start(f32[1,4,512]{2,1,0:T(4,128)} %get-tuple-element.38), channel_id=1, source_target_pairs={{0,1},{1,2},{2,3},{4,5},{5,6},{6,7},{8,9},{9,10},{10,11},{12,13},{... | collective-permute-start | bytes 24584 | tf_op jit(solution)/shard_map/ppermute | solution.py:260
  110.2 1.8 %collective-permute-done.12.prior_y = f32[1,4,512]{2,1,0:T(4,128)S(1)} collective-permute-done((f32[1,4,512]{2,1,0:T(4,128)}, f32[1,4,512]{2,1,0:T(4,128)S(1)}, u32[]{:S(2)}, u32[]{:S(2)}) %collective-permute-start.12) | collective-permute-done | bytes 8224 | tf_op jit(solution)/shard_map/ppermute | solution.py:260
  112.1 0.0 collective-permute-done.13.next_y
  112.1 3.1 %collective-permute-done.10.prior_x = f32[1,32,512]{2,1,0:T(8,128)S(1)} collective-permute-done((f32[1,32,512]{2,1,0:T(8,128)}, f32[1,32,512]{2,1,0:T(8,128)S(1)}, u32[]{:S(2)}, u32[]{:S(2)}) %collective-permute-start.10) | collective-permute-done | bytes 65568 | tf_op jit(solution)/shard_map/ppermute | solution.py:260
  115.2 0.0 collective-permute-done.11.next_x
  115.2 0.0 copy-done.12
  115.2 0.0 copy-done.11
  115.2 0.6 copy-done.8
  115.8 0.0 copy-done.5
  115.8 4.2 %second_stress.1 = (f32[9,4,32,512]{3,2,1,0:T(8,128)}, f32[6,4,32,512]{3,2,1,0:T(8,128)}) custom-call(f32[3,4,32,512]{3,2,1,0:T(8,128)} %get-tuple-element.34.v, f32[6,4,32,512]{3,2,1,0:T(8,128)} %get-tuple-element.35.stress, f32[4,32,512]{2,1,0:T(8,128)} %lam.5, f32[4,32,512]{2,1,0:T(8,128)} %mu.5, f32[1,32,512]{2,1,0:T(8,128)} %copy-done.8, ...), custom_call_target="tpu_custom_call" | custom-call | tf_op jit(solution)/shard_map/second_stress/pallas_call | solution.py:321
  120.1 0.0 all-to-all-done
  120.1 0.9 copy-done
  121.0 4.0 %gradients.1 = f32[2,4,32,512]{3,2,1,0:T(8,128)} custom-call(s32[1600,128]{1,0:T(8,128)} %bitcast.4, s32[1,64]{1,0:T(1,128)} %perm.1, f32[6,4,32,512]{3,2,1,0:T(8,128)} %get-tuple-element.42.strain1, f32[6,4,32,512]{3,2,1,0:T(8,128)} %get-tuple-element.43.strain2), custom_call_target="tpu_custom_call" | custom-call | tf_op jit(solution)/shard_map/gradients/pallas_call | solution.py:329
  (10 shorter events, 0.0 us)
Async XLA Ops:
  5.5 13.2 %copy-start.16 = (f32[3,32,512]{2,1,0:T(8,128)S(1)}, f32[3,32,512]{2,1,0:T(8,128)}, u32[]{:S(2)}) copy-start(f32[3,32,512]{2,1,0:T(8,128)} %get-tuple-element.23) | copy-start | bytes 589828
  5.5 15.2 %copy-start.15 = (f32[3,32,512]{2,1,0:T(8,128)S(1)}, f32[3,32,512]{2,1,0:T(8,128)}, u32[]{:S(2)}) copy-start(f32[3,32,512]{2,1,0:T(8,128)} %get-tuple-element.24) | copy-start | bytes 589828
  5.5 25.7 %copy-start.18 = (f32[3,4,512]{2,1,0:T(4,128)S(1)}, f32[3,4,512]{2,1,0:T(4,128)}, u32[]{:S(2)}) copy-start(f32[3,4,512]{2,1,0:T(4,128)} %get-tuple-element.25) | copy-start | bytes 73732
  5.5 28.6 %copy-start.17 = (f32[3,4,512]{2,1,0:T(4,128)S(1)}, f32[3,4,512]{2,1,0:T(4,128)}, u32[]{:S(2)}) copy-start(f32[3,4,512]{2,1,0:T(4,128)} %get-tuple-element.26) | copy-start | bytes 73732
  5.5 114.6 %all-to-all-start = ((s32[64,25,1,128]{3,2,1,0:T(1,128)}), s32[64,25,1,128]{3,2,1,0:T(1,128)S(1)}, u32[]{:S(2)}, u32[]{:S(2)}) async-start(s32[64,25,1,128]{3,2,1,0:T(1,128)} %bitcast.5), calls=%async_computation | async-start | bytes 1638400 | tf_op jit(solution)/shard_map/all_to_all | solution.py:283
  18.7 30.5 %collective-permute-start = (f32[3,32,512]{2,1,0:T(8,128)S(1)}, f32[3,32,512]{2,1,0:T(8,128)S(1)}, u32[]{:S(2)}, u32[]{:S(2)}) collective-permute-start(f32[3,32,512]{2,1,0:T(8,128)S(1)} %copy-done.16), channel_id=1, source_target_pairs={{0,4},{1,5},{2,6},{3,7},{4,8},{5,9},{6,10},{7,11},{8,12},{9,13},{1... | collective-permute-start | bytes 589832 | tf_op jit(solution)/shard_map/ppermute | solution.py:260
  20.7 28.4 %collective-permute-start.1 = (f32[3,32,512]{2,1,0:T(8,128)S(1)}, f32[3,32,512]{2,1,0:T(8,128)S(1)}, u32[]{:S(2)}, u32[]{:S(2)}) collective-permute-start(f32[3,32,512]{2,1,0:T(8,128)S(1)} %copy-done.15), channel_id=1, source_target_pairs={{4,0},{5,1},{6,2},{7,3},{8,4},{9,5},{10,6},{11,7},{12,8},{13,9},{1... | collective-permute-start | bytes 589832 | tf_op jit(solution)/shard_map/ppermute | solution.py:260
  31.2 10.1 %collective-permute-start.2 = (f32[3,4,512]{2,1,0:T(4,128)S(1)}, f32[3,4,512]{2,1,0:T(4,128)S(1)}, u32[]{:S(2)}, u32[]{:S(2)}) collective-permute-start(f32[3,4,512]{2,1,0:T(4,128)S(1)} %copy-done.18), channel_id=1, source_target_pairs={{0,1},{1,2},{2,3},{4,5},{5,6},{6,7},{8,9},{9,10},{10,11},{12,13},{... | collective-permute-start | bytes 73736 | tf_op jit(solution)/shard_map/ppermute | solution.py:260
  34.1 7.2 %collective-permute-start.3 = (f32[3,4,512]{2,1,0:T(4,128)S(1)}, f32[3,4,512]{2,1,0:T(4,128)S(1)}, u32[]{:S(2)}, u32[]{:S(2)}) collective-permute-start(f32[3,4,512]{2,1,0:T(4,128)S(1)} %copy-done.17), channel_id=1, source_target_pairs={{1,0},{2,1},{3,2},{5,4},{6,5},{7,6},{9,8},{10,9},{11,10},{13,12},{... | collective-permute-start | bytes 73736 | tf_op jit(solution)/shard_map/ppermute | solution.py:260
  41.3 7.8 %copy-start.6 = (f32[3,4,512]{2,1,0:T(4,128)}, f32[3,4,512]{2,1,0:T(4,128)S(1)}, u32[]{:S(2)}) copy-start(f32[3,4,512]{2,1,0:T(4,128)S(1)} %collective-permute-done.2.prior_y.s_prior_y) | copy-start | bytes 73732
  41.3 7.8 %copy-start.7 = (f32[3,4,512]{2,1,0:T(4,128)}, f32[3,4,512]{2,1,0:T(4,128)S(1)}, u32[]{:S(2)}) copy-start(f32[3,4,512]{2,1,0:T(4,128)S(1)} %collective-permute-done.3.next_y.s_next_y) | copy-start | bytes 73732
  49.1 0.7 copy-start.1
  49.8 0.7 copy-start.2
  53.7 34.6 %collective-permute-start.4 = (f32[3,32,512]{2,1,0:T(8,128)}, f32[3,32,512]{2,1,0:T(8,128)S(1)}, u32[]{:S(2)}, u32[]{:S(2)}) collective-permute-start(f32[3,32,512]{2,1,0:T(8,128)} %get-tuple-element.30), channel_id=1, source_target_pairs={{0,4},{1,5},{2,6},{3,7},{4,8},{5,9},{6,10},{7,11},{8,12},{9,13},{1... | collective-permute-start | bytes 589832 | tf_op jit(solution)/shard_map/ppermute | solution.py:260
  55.7 32.7 %collective-permute-start.5 = (f32[3,32,512]{2,1,0:T(8,128)}, f32[3,32,512]{2,1,0:T(8,128)S(1)}, u32[]{:S(2)}, u32[]{:S(2)}) collective-permute-start(f32[3,32,512]{2,1,0:T(8,128)} %get-tuple-element.31), channel_id=1, source_target_pairs={{4,0},{5,1},{6,2},{7,3},{8,4},{9,5},{10,6},{11,7},{12,8},{13,9},{1... | collective-permute-start | bytes 589832 | tf_op jit(solution)/shard_map/ppermute | solution.py:260
  66.2 22.1 %collective-permute-start.6 = (f32[3,4,512]{2,1,0:T(4,128)}, f32[3,4,512]{2,1,0:T(4,128)S(1)}, u32[]{:S(2)}, u32[]{:S(2)}) collective-permute-start(f32[3,4,512]{2,1,0:T(4,128)} %get-tuple-element.28.last_y), channel_id=1, source_target_pairs={{0,1},{1,2},{2,3},{4,5},{5,6},{6,7},{8,9},{9,10},{10,11},{12,13},{... | collective-permute-start | bytes 73736 | tf_op jit(solution)/shard_map/ppermute | solution.py:260
  68.6 19.7 %collective-permute-start.7 = (f32[3,4,512]{2,1,0:T(4,128)}, f32[3,4,512]{2,1,0:T(4,128)S(1)}, u32[]{:S(2)}, u32[]{:S(2)}) collective-permute-start(f32[3,4,512]{2,1,0:T(4,128)} %get-tuple-element.29.first_y), channel_id=1, source_target_pairs={{1,0},{2,1},{3,2},{5,4},{6,5},{7,6},{9,8},{10,9},{11,10},{13,12},{... | collective-permute-start | bytes 73736 | tf_op jit(solution)/shard_map/ppermute | solution.py:260
  72.1 11.1 %collective-permute-start.8 = (f32[1,512]{1,0:T(1,128)}, f32[1,512]{1,0:T(1,128)S(1)}, u32[]{:S(2)}, u32[]{:S(2)}) collective-permute-start(f32[1,512]{1,0:T(1,128)} %get-tuple-element.32), channel_id=1, source_target_pairs={{1,4},{2,5},{3,6},{5,8},{6,9},{7,10},{9,12},{10,13},{11,14},{13,16... | collective-permute-start | bytes 6152 | tf_op jit(solution)/shard_map/ppermute | solution.py:260
  83.2 5.2 %copy-start.13 = (f32[1,512]{1,0:T(1,128)}, f32[1,512]{1,0:T(1,128)S(1)}, u32[]{:S(2)}) copy-start(f32[1,512]{1,0:T(1,128)S(1)} %collective-permute-done.8.vx_corner) | copy-start | bytes 6148
  83.2 5.1 %collective-permute-start.9 = (f32[1,512]{1,0:T(1,128)}, f32[1,512]{1,0:T(1,128)S(1)}, u32[]{:S(2)}, u32[]{:S(2)}) collective-permute-start(f32[1,512]{1,0:T(1,128)} %get-tuple-element.33), channel_id=1, source_target_pairs={{4,1},{5,2},{6,3},{8,5},{9,6},{10,7},{12,9},{13,10},{14,11},{16,13... | collective-permute-start | bytes 6152 | tf_op jit(solution)/shard_map/ppermute | solution.py:260
  88.3 0.6 copy-start.14
  88.3 0.6 copy-start.9
  88.3 0.6 copy-start.10
  88.4 0.7 copy-start.3
  88.4 0.7 copy-start.4
  94.1 21.1 %collective-permute-start.11 = (f32[2,32,512]{2,1,0:T(8,128)}, f32[2,32,512]{2,1,0:T(8,128)S(1)}, u32[]{:S(2)}, u32[]{:S(2)}) collective-permute-start(f32[2,32,512]{2,1,0:T(8,128)} %get-tuple-element.37), channel_id=1, source_target_pairs={{4,0},{5,1},{6,2},{7,3},{8,4},{9,5},{10,6},{11,7},{12,8},{13,9},{1... | collective-permute-start | bytes 393224 | tf_op jit(solution)/shard_map/ppermute | solution.py:260
  102.5 12.7 %collective-permute-start.10 = (f32[1,32,512]{2,1,0:T(8,128)}, f32[1,32,512]{2,1,0:T(8,128)S(1)}, u32[]{:S(2)}, u32[]{:S(2)}) collective-permute-start(f32[1,32,512]{2,1,0:T(8,128)} %get-tuple-element.36), channel_id=1, source_target_pairs={{0,4},{1,5},{2,6},{3,7},{4,8},{5,9},{6,10},{7,11},{8,12},{9,13},{1... | collective-permute-start | bytes 196616 | tf_op jit(solution)/shard_map/ppermute | solution.py:260
  104.4 7.7 %collective-permute-start.13 = (f32[2,4,512]{2,1,0:T(4,128)}, f32[2,4,512]{2,1,0:T(4,128)S(1)}, u32[]{:S(2)}, u32[]{:S(2)}) collective-permute-start(f32[2,4,512]{2,1,0:T(4,128)} %get-tuple-element.39), channel_id=1, source_target_pairs={{1,0},{2,1},{3,2},{5,4},{6,5},{7,6},{9,8},{10,9},{11,10},{13,12},{... | collective-permute-start | bytes 49160 | tf_op jit(solution)/shard_map/ppermute | solution.py:260
  106.3 5.8 %collective-permute-start.12 = (f32[1,4,512]{2,1,0:T(4,128)}, f32[1,4,512]{2,1,0:T(4,128)S(1)}, u32[]{:S(2)}, u32[]{:S(2)}) collective-permute-start(f32[1,4,512]{2,1,0:T(4,128)} %get-tuple-element.38), channel_id=1, source_target_pairs={{0,1},{1,2},{2,3},{4,5},{5,6},{6,7},{8,9},{9,10},{10,11},{12,13},{... | collective-permute-start | bytes 24584 | tf_op jit(solution)/shard_map/ppermute | solution.py:260
  112.1 3.1 %copy-start.12 = (f32[1,4,512]{2,1,0:T(4,128)}, f32[1,4,512]{2,1,0:T(4,128)S(1)}, u32[]{:S(2)}) copy-start(f32[1,4,512]{2,1,0:T(4,128)S(1)} %collective-permute-done.12.prior_y) | copy-start | bytes 24580
  112.1 3.1 %copy-start.11 = (f32[2,4,512]{2,1,0:T(4,128)}, f32[2,4,512]{2,1,0:T(4,128)S(1)}, u32[]{:S(2)}) copy-start(f32[2,4,512]{2,1,0:T(4,128)S(1)} %collective-permute-done.13.next_y) | copy-start | bytes 49156
  115.2 0.6 copy-start.8
  115.2 0.7 copy-start.5
  120.1 0.9 copy-start

commit v2 on v1

v2 whole, which is shorter than its diff:
```python
import jax
import jax.numpy as jnp
from jax import lax
from jax.experimental import pallas as pl
from jax.experimental.pallas import tpu as pltpu
from jax.sharding import PartitionSpec as P


courant = 0.15
FACTOR_UP = 2.0**35
FACTOR_DOWN = 2.0**-35
F32 = jnp.float32
ANY = pl.BlockSpec(memory_space=pl.ANY)
VMEM = pl.BlockSpec(memory_space=pltpu.VMEM)


def below_y(field, row):
    y = lax.broadcasted_iota(jnp.int32, field.shape, 0)
    return jnp.where(y == 0, row, pltpu.roll(field, 1, 0))


def above_y(field, row):
    count = field.shape[0]
    y = lax.broadcasted_iota(jnp.int32, field.shape, 0)
    return jnp.where(y == count - 1, row, pltpu.roll(field, count - 1, 0))


def below_z(field):
    z = lax.broadcasted_iota(jnp.int32, field.shape, 1)
    return jnp.where(z == 0, 0.0, pltpu.roll(field, 1, 1))


def above_z(field):
    count = field.shape[1]
    z = lax.broadcasted_iota(jnp.int32, field.shape, 1)
    return jnp.where(z == count - 1, 0.0, pltpu.roll(field, count - 1, 1))


def velocity_plane(vel, scaled, sxx, sxx_next, syy, syy_row, szz, sxy, sxy_prior, sxy_row, sxz, sxz_prior, syz, syz_row):
    vx, vy, vz = vel
    vx = vx - scaled * (sxx_next - sxx + (sxy - below_y(sxy, sxy_row)) + (sxz - below_z(sxz)))
    vy = vy - scaled * (sxy - sxy_prior + (above_y(syy, syy_row) - syy) + (syz - below_z(syz)))
    vz = vz - scaled * (sxz - sxz_prior + (syz - below_y(syz, syz_row)) + (above_z(szz) - szz))
    return vx, vy, vz


def strain_plane(vx, vx_prior, vx_row, vy, vy_next, vy_row, vz, vz_next, vz_row):
    exx = vx - vx_prior
    eyy = vy - below_y(vy, vy_row)
    ezz = vz - below_z(vz)
    exy = (above_y(vx, vx_row) - vx) + (vy_next - vy)
    exz = (above_z(vx) - vx) + (vz_next - vz)
    eyz = (above_z(vy) - vy) + (above_y(vz, vz_row) - vz)
    return exx, eyy, ezz, exy, exz, eyz


def stress_plane(stress, strain, lam, mu):
    trace = strain[0] + strain[1] + strain[2]
    direct = [stress[k] - courant * (lam * trace + 2.0 * mu * strain[k]) for k in range(3)]
    shear = [stress[k] - courant * mu * strain[k] for k in range(3, 6)]
    return direct + shear


UP_PLANES = (6, 7, 11)
DOWN_PLANES = (3, 10, 11)
UP_ROWS = (6, 8, 11, 1, 9, 4)
DOWN_ROWS = (4, 10, 11, 0, 9, 3, 6, 7)


def on_lower_core():
    return lax.axis_index("gx") % 2 == 0


def below_above(far, near):
    lower = on_lower_core()
    return lambda k: jnp.where(lower, far[k], near[k]), lambda k: jnp.where(lower, near[k], far[k])


def far_near(up, down):
    lower = on_lower_core()
    return jnp.where(lower, down, up), jnp.where(lower, up, down)


def prepare(adj, buoy, lam, mu, far, near, to_next_y, to_prior_y, rows, sems, row_sems):
    cells_x, cells_y = adj.shape[1:3]
    extra = (buoy, lam, mu)

    def whole(n):
        return adj.at[n] if n < 9 else extra[n - 9]

    def planes(core):
        plans = []
        for target, names, x in ((far, DOWN_PLANES, 0), (near, UP_PLANES, cells_x - 1)) if core == 0 else ((far, UP_PLANES, cells_x - 1), (near, DOWN_PLANES, 0)):
            plans += [(whole(n).at[x], target.at[k]) for k, n in enumerate(names)]
        return [pltpu.make_async_copy(source, target, sems.at[k]) for k, (source, target) in enumerate(plans)]

    def both(verb):
        lower = on_lower_core()
        for core in range(2):

            @pl.when(lower == (core == 0))
            def _():
                for copy in planes(core):
                    getattr(copy, verb)()

    both("start")
    plans = [(n, cells_y - 8) for n in UP_ROWS] + [(n, 0) for n in DOWN_ROWS]
    copies = [
        pltpu.make_async_copy(whole(n).at[:, pl.ds(start, 8)], rows.at[k], row_sems.at[k]) for k, (n, start) in enumerate(plans)
    ]
    for copy in copies:
        copy.start()
    for copy in copies:
        copy.wait()
    for k in range(len(UP_ROWS)):
        to_next_y[k] = rows[k, :, 7, :]
    for k in range(len(DOWN_ROWS)):
        to_prior_y[k] = rows[len(UP_ROWS) + k, :, 0, :]
    both("wait")


def merge(packed, scales, message):
    comp, _, count = scales.shape
    per = packed.shape[0] // count
    factor = jnp.pad(scales[:, 0, :], ((0, 128 - comp), (0, 128 - count)))
    factor = (jnp.transpose(factor)[:count] * FACTOR_UP).astype(jnp.int32)
    message[pl.ds(per, count, stride=per + 1), :] = factor
    for r in range(per):
        message[pl.ds(r, count, stride=per + 1), :] = packed[pl.ds(r, count, stride=per), :]


def first_velocity(adj, buoy, far_in, near_in, prior_y, next_y, v, far, near, to_next_y, to_prior_y):
    cells_x, cells_y = adj.shape[1:3]
    last = cells_x - 1
    below, above = below_above(far_in, near_in)
    for x in range(cells_x):
        new = velocity_plane(
            (adj[0, x], adj[1, x], adj[2, x]), courant * buoy[x],
            adj[3, x], adj[3, x + 1] if x < last else above(0), adj[4, x], next_y[0, x : x + 1], adj[5, x],
            adj[6, x], adj[6, x - 1] if x > 0 else below(0), prior_y[0, x : x + 1],
            adj[7, x], adj[7, x - 1] if x > 0 else below(1), adj[8, x], prior_y[1, x : x + 1],
        )
        for k in range(3):
            v[k, x] = new[k]
            to_next_y[k, x : x + 1, :] = new[k][cells_y - 1 :, :]
            to_prior_y[k, x : x + 1, :] = new[k][0:1, :]
    own = {n: next_y[k, last : last + 1] for k, n in enumerate(DOWN_ROWS)}
    scaled_up = courant * own[9]
    sides = (own[6] - adj[6, last][cells_y - 1 :, :]) + (own[7] - below_z(own[7]))
    part_up = own[0] - scaled_up * (sides - own[3])
    own = {n: prior_y[k, 0:1] for k, n in enumerate(UP_ROWS)}
    scaled_down = courant * own[9]
    sides = (adj[4, 0][0:1, :] - own[4]) + (own[8] - below_z(own[8]))
    part_down = own[1] - scaled_down * (own[6] + sides)
    for k in range(3):
        far[pl.ds(k * cells_y, cells_y), :], near[pl.ds(k * cells_y, cells_y), :] = far_near(v[k, last], v[k, 0])
    at = 3 * cells_y
    far[at : at + 1, :], near[at : at + 1, :] = far_near(part_up, part_down)
    far[at + 1 : at + 2, :], near[at + 1 : at + 2, :] = far_near(scaled_up, scaled_down)


def middle(
    adj, buoy, lam, mu, s_far, s_near, s_prior_y, s_next_y, v, last_y, first_y, v_far, v_near, v_prior_y, v_next_y,
    v_new, stress, strain, far, near, to_next_y, to_prior_y,
):
    cells_x, cells_y = adj.shape[1:3]
    last = cells_x - 1
    s_below, s_above = below_above(s_far, s_near)
    v_below, v_above = below_above(v_far, v_near)
    vx_m, vy_m, vz_m = (v_below(pl.ds(k * cells_y, cells_y)) for k in range(3))
    vx_n, vy_n, vz_n = (v_above(pl.ds(k * cells_y, cells_y)) for k in range(3))
    part, scaled = pl.ds(3 * cells_y, 1), pl.ds(3 * cells_y + 1, 1)
    vx_corner = v_below(part) - v_below(scaled) * s_next_y[DOWN_ROWS.index(3), 0:1]
    vy_corner = v_above(part) + v_above(scaled) * s_prior_y[UP_ROWS.index(6), last : last + 1]
    exx = vx_n - v[0, last]
    trace = exx + (vy_n - below_y(vy_n, vy_corner)) + (vz_n - below_z(vz_n))
    sxx_next = s_above(0) - courant * (s_above(1) * trace + 2.0 * s_above(2) * exx)
    exy = (above_y(vx_m, vx_corner) - vx_m) + (v[1, 0] - vy_m)
    exz = (above_z(vx_m) - vx_m) + (v[2, 0] - vz_m)
    sxy_prior = s_below(0) - courant * s_below(2) * exy
    sxz_prior = s_below(1) - courant * s_below(2) * exz
    over = v_next_y[0]
    exx = over - jnp.concatenate([vx_corner, over[:last]], axis=0)
    eyy = v_next_y[1] - last_y[1]
    trace = exx + eyy + (v_next_y[2] - below_z(v_next_y[2]))
    syy_rows = s_next_y[0] - courant * (s_next_y[1] * trace + 2.0 * s_next_y[2] * eyy)
    under = v_prior_y[1]
    exy = (first_y[0] - v_prior_y[0]) + (jnp.concatenate([under[1:], vy_corner], axis=0) - under)
    eyz = (above_z(under) - under) + (first_y[2] - v_prior_y[2])
    sxy_rows = s_prior_y[0] - courant * s_prior_y[2] * exy
    syz_rows = s_prior_y[1] - courant * s_prior_y[2] * eyz
    for x in range(cells_x):
        e = strain_plane(
            v[0, x], v[0, x - 1] if x > 0 else vx_m, v_next_y[0, x : x + 1],
            v[1, x], v[1, x + 1] if x < last else vy_n, v_prior_y[1, x : x + 1],
            v[2, x], v[2, x + 1] if x < last else vz_n, v_next_y[2, x : x + 1],
        )
        s = stress_plane([adj[3 + k, x] for k in range(6)], e, lam[x], mu[x])
        for k in range(6):
            strain[k, x] = e[k]
            stress[k, x] = s[k]
    for x in range(cells_x):
        new = velocity_plane(
            (v[0, x], v[1, x], v[2, x]), courant * buoy[x],
            stress[0, x], stress[0, x + 1] if x < last else sxx_next, stress[1, x], syy_rows[x : x + 1], stress[2, x],
            stress[3, x], stress[3, x - 1] if x > 0 else sxy_prior, sxy_rows[x : x + 1],
            stress[4, x], stress[4, x - 1] if x > 0 else sxz_prior, stress[5, x], syz_rows[x : x + 1],
        )
        for k in range(3):
            v_new[k, x] = new[k]
        to_next_y[0, x : x + 1, :] = new[1][cells_y - 1 :, :]
        to_prior_y[0, x : x + 1, :] = new[0][0:1, :]
        to_prior_y[1, x : x + 1, :] = new[2][0:1, :]
    far[0], near[0] = far_near(v_new[0, last], v_new[1, 0])
    far[1], near[1] = far_near(jnp.zeros_like(v_new[2, 0]), v_new[2, 0])


def second_stress(v, stress, lam, mu, v_far, v_near, prior_y, next_y, out, strain):
    cells_x = v.shape[1]
    last = cells_x - 1
    below, above = below_above(v_far, v_near)
    for x in range(cells_x):
        e = strain_plane(
            v[0, x], v[0, x - 1] if x > 0 else below(0), next_y[0, x : x + 1],
            v[1, x], v[1, x + 1] if x < last else above(0), prior_y[0, x : x + 1],
            v[2, x], v[2, x + 1] if x < last else above(1), next_y[1, x : x + 1],
        )
        s = stress_plane([stress[k, x] for k in range(6)], e, lam[x], mu[x])
        for k in range(3):
            out[k, x] = v[k, x]
        for k in range(6):
            strain[k, x] = e[k]
            out[3 + k, x] = s[k]


def gradients(message, perm, strain1, strain2, out):
    count = perm.shape[1]
    per = message.shape[0] // count
    cells_x, cells_y, cells_z = strain1.shape[1:]
    rows = cells_x * cells_y
    both = jnp.concatenate([perm[...], perm[...]], axis=1)
    r = lax.broadcasted_iota(jnp.int32, (rows, 2 * count), 0)
    k = lax.broadcasted_iota(jnp.int32, (rows, 2 * count), 1)
    mine = both == lax.shift_right_logical(r, 1)
    half = (k >= count) == ((r & 1) == 1)
    pick = jnp.where(mine & half, 1.0, 0.0).astype(jnp.bfloat16)
    pick_factor = jnp.where(mine & (k < count), 1.0, 0.0)
    factor = message[pl.ds(per - 1, count, stride=per), :].astype(F32) * FACTOR_DOWN
    factor = jnp.concatenate([factor, jnp.zeros_like(factor)], axis=0)
    factor = lax.dot(pick_factor, factor, precision=lax.Precision.HIGHEST, preferred_element_type=F32)

    def forward(c):
        w = [message[pl.ds(2 * c + t, count, stride=per), :] for t in range(2)]
        byte = [lambda w: w & 255, lambda w: lax.shift_right_logical(w, 8) & 255, lambda w: lax.shift_right_logical(w, 16) & 255]
        parts = [[(f(v) - 128) for v in w] for f in byte] + [[lax.shift_right_arithmetic(v, 24) for v in w]]
        parts = [[v.astype(F32).astype(jnp.bfloat16) for v in p] for p in parts]
        low = jnp.concatenate(parts[0] + parts[1], axis=1)
        high = jnp.concatenate(parts[2] + parts[3], axis=1)
        table = jnp.concatenate([low, high], axis=0)
        picked = lax.dot(pick, table, preferred_element_type=F32)
        return picked * factor[:, c : c + 1]

    grad_lambda = None
    grad_mu = None
    for step, strain in enumerate((strain1, strain2)):
        f = [forward(6 * step + n) for n in range(6)]
        e = [strain[n].reshape(rows, cells_z) for n in range(6)]
        add_lambda = (e[0] + e[1] + e[2]) * (f[0] + f[1] + f[2])
        add_mu = 2.0 * (e[0] * f[0] + e[1] * f[1] + e[2] * f[2])
        grad_lambda = add_lambda if step == 0 else grad_lambda + add_lambda
        grad_mu = add_mu if step == 0 else grad_mu + add_mu
        grad_mu = grad_mu + e[3] * f[3] + e[4] * f[4] + e[5] * f[5]
    out[0] = grad_lambda.reshape(cells_x, cells_y, cells_z)
    out[1] = grad_mu.reshape(cells_x, cells_y, cells_z)


def on_device(adjoint, buoyancy, lame_lambda, shear_mu, packed, scales, perm):
    cells_x, cells_y, cells_z = buoyancy.shape
    owners, comp, width = packed.shape[1], packed.shape[3], packed.shape[4]
    per = comp * width // 128

    def shape(*dims, dtype=F32):
        return jax.ShapeDtypeStruct(dims, dtype)

    def call(kernel, mebibytes, outs, args, in_specs=None, scratch=()):
        return pl.pallas_call(
            kernel,
            out_shape=outs,
            in_specs=in_specs or [VMEM] * len(args),
            out_specs=jax.tree.map(lambda _: VMEM, outs),
            scratch_shapes=scratch,
            compiler_params=pltpu.CompilerParams(vmem_limit_bytes=mebibytes << 20),
        )(*args)

    count_x = lax.axis_size("gx")
    count_y = lax.axis_size("gy")
    off_chip = [(x, x + 1 if x % 2 else x - 1) for x in range(1, count_x - 1)]
    on_chip = [(x, x ^ 1) for x in range(count_x)]
    upward = [(y, y + 1) for y in range(count_y - 1)]
    downward = [(y + 1, y) for y in range(count_y - 1)]

    def swap(far, near, to_next_y, to_prior_y):
        far = lax.ppermute(far, "gx", off_chip)
        near = lax.ppermute(near, "gx", on_chip)
        prior_y = lax.ppermute(to_next_y, "gy", upward)
        next_y = lax.ppermute(to_prior_y, "gy", downward)
        return far, near, prior_y, next_y

    def planes(*count):
        return shape(*count, cells_y, cells_z)

    def lines(count):
        return shape(count, cells_x, cells_z)

    sent = call(
        prepare, 8, (planes(3), planes(3), lines(len(UP_ROWS)), lines(len(DOWN_ROWS))),
        (adjoint, buoyancy, lame_lambda, shear_mu), [ANY] * 4,
        [
            pltpu.VMEM((len(UP_ROWS) + len(DOWN_ROWS), cells_x, 8, cells_z), F32),
            pltpu.SemaphoreType.DMA((6,)),
            pltpu.SemaphoreType.DMA((len(UP_ROWS) + len(DOWN_ROWS),)),
        ],
    )
    s_ghosts = swap(*sent)

    by_comp = jnp.transpose(scales.reshape(owners, comp)).reshape(comp, 1, owners)
    message = call(merge, 8, shape(owners * (per + 1), 128, dtype=jnp.int32), (packed.reshape(owners * per, 128), by_comp))
    message = lax.all_to_all(message.reshape(owners, per + 1, 1, 128), "gx", split_axis=0, concat_axis=0, tiled=True)
    message = message.reshape(owners * (per + 1), 128)

    faces = shape(3 * cells_y + 8, cells_z)
    v, *sent = call(
        first_velocity, 12, (planes(3, cells_x), faces, faces, lines(3), lines(3)), (adjoint, buoyancy, *s_ghosts)
    )
    last_y, first_y = sent[2:]
    v_ghosts = swap(*sent)

    v, stress, strain1, *sent = call(
        middle, 16,
        (planes(3, cells_x), planes(6, cells_x), planes(6, cells_x), planes(2), planes(2), lines(1), lines(2)),
        (adjoint, buoyancy, lame_lambda, shear_mu, *s_ghosts, v, last_y, first_y, *v_ghosts),
    )
    v_ghosts = swap(*sent)

    adjoint_out, strain2 = call(
        second_stress, 12, (shape(*adjoint.shape), planes(6, cells_x)), (v, stress, lame_lambda, shear_mu, *v_ghosts)
    )
    grads = call(gradients, 16, planes(2, cells_x), (message, perm, strain1, strain2))
    return adjoint_out, grads


def solution(mesh):
    return jax.shard_map(
        on_device,
        mesh=mesh,
        in_specs=(
            P(None, "gx", "gy", None),
            P("gx", "gy", None),
            P("gx", "gy", None),
            P("gx", "gy", None),
            P("gx", None, "gy", None, None),
            P("gx", None, "gy", None),
            P("gx", None),
        ),
        out_specs=(P(None, "gx", "gy", None), P(None, "gx", "gy", None)),
        check_vma=False,
    )
```

time: 126 us -> 88 us (0.70)
  starting transfers between devices: 69.7 us -> 46.6 us
  Pallas kernels: 19.9 us -> 6.58 us
  waiting for transfers between devices: 29.4 us -> 23.2 us
  local copies, waits for them, and re-layouts: 5.06 us -> 9.81 us
    ppermute x14 -> x12, starting transfers between devices: 56.6 us -> 33.6 us  [the longest x3 15.8 us: swap(): far = lax.ppermute(far, 'gx', off_chip)]
    pallas_call x5 -> x6, Pallas kernels: 19.9 us -> 6.58 us  [call(): pl.pallas_call(kernel, out_shape=outs, in_specs=in_specs or [VMEM] * len(...]
    ppermute x14 -> x12, waiting for transfers between devices: 29.4 us -> 23.2 us  [the longest x3 10.5 us: swap(): far = lax.ppermute(far, 'gx', off_chip)]
    unnamed x39 -> x27, local copies, waits for them, and re-layouts: 5.06 us -> 9.8 us
  transfers between devices with their start and end apart: 15 -> 13, of which waited for: 6 -> 8; matrix products, arithmetic and copies ran while one was open for 0% -> 0% of each run, Pallas kernels for 10% -> 5%
where the time goes in v2:
time: 88 us; the launch traced here: 87.1 us
  starting transfers between devices  46.6 us (53%)
  waiting for transfers between devices  23.2 us (26%)
  local copies, waits for them, and re-layouts  9.81 us (11%)
  Pallas kernels  6.58 us (7%)
    ppermute x3, starting transfers between devices, swap(): far = lax.ppermute(far, 'gx', off_chip)  15.8 us
    all_to_all x1, starting transfers between devices, on_device(): lax.all_to_all(message.reshape(owners, per + 1, 1, 128), 'gx', split_axis...  13 us
    ppermute x3, waiting for transfers between devices, swap(): far = lax.ppermute(far, 'gx', off_chip)  10.5 us
    unnamed x27, local copies, waits for them, and re-layouts  9.8 us
    ppermute x3, starting transfers between devices, swap(): next_y = lax.ppermute(to_prior_y, 'gy', downward)  9.06 us
    ppermute x3, waiting for transfers between devices, swap(): prior_y = lax.ppermute(to_next_y, 'gy', upward)  9.05 us
    ppermute x3, starting transfers between devices, swap(): prior_y = lax.ppermute(to_next_y, 'gy', upward)  8.46 us
    pallas_call x6, Pallas kernels, call(): pl.pallas_call(kernel, out_shape=outs, in_specs=in_specs or [VMEM] * len(...  6.58 us
  transfers between devices with their start and end apart: 13, of which 8 were waited for; matrix products, arithmetic and copies ran while one was open for 0% of the time, Pallas kernels for 5%

profile of v2, /device:TPU:70, one launch (start us, length us, event | category | flops | bytes accessed | tf_op | source)
XLA Modules:
  0.0 87.1 jit_solution(8249078535307587280)
XLA Ops:
  0.6 0.7 copy.12
  1.3 0.0 copy-start.11
  1.3 1.1 %copy-done.11 = s32[1,64,1,12,256]{4,2,3,1,0:T(1,128)S(1)} copy-done((s32[1,64,1,12,256]{4,2,3,1,0:T(1,128)S(1)}, s32[1,64,1,12,256]{4,2,3,1,0:T(1,128)}, u32[]{:S(2)}) %copy-start.11) | copy-done | bytes 786456
  2.5 0.0 copy-start
  2.5 0.0 copy-start.2
  2.5 0.2 shard_map.90
  2.6 0.0 copy-start.1
  2.6 0.9 %copy-done.1 = s32[1600,128]{1,0:T(8,128)} copy-done((s32[1600,128]{1,0:T(8,128)}, s32[1600,128]{1,0:T(8,128)S(1)}, u32[]{:S(2)}) %copy-start.1) | copy-done | bytes 819224
  3.6 13.0 %all-to-all-start = ((s32[64,25,1,128]{3,2,1,0:T(1,128)}), s32[64,25,1,128]{3,2,1,0:T(1,128)S(1)}, u32[]{:S(2)}, u32[]{:S(2)}) async-start(s32[64,25,1,128]{3,2,1,0:T(1,128)} %bitcast.9), calls=%async_computation | async-start | bytes 1638400 | tf_op jit(solution)/shard_map/all_to_all | solution.py:328
  16.6 0.0 copy-done
  16.6 0.0 copy-done.2
  16.6 0.0 copy-start.3
  16.6 0.9 %copy-done.3 = f32[4,32,512]{2,1,0:T(8,128)S(1)} copy-done((f32[4,32,512]{2,1,0:T(8,128)S(1)}, f32[4,32,512]{2,1,0:T(8,128)}, u32[]{:S(2)}) %copy-start.3) | copy-done | bytes 262168
  17.5 0.0 copy-start.5
  17.5 0.9 %copy-done.5 = f32[4,32,512]{2,1,0:T(8,128)S(1)} copy-done((f32[4,32,512]{2,1,0:T(8,128)S(1)}, f32[4,32,512]{2,1,0:T(8,128)}, u32[]{:S(2)}) %copy-start.5) | copy-done | bytes 262168
  18.5 1.0 %shard_map.86 = (f32[3,32,512]{2,1,0:T(8,128)S(1)}, f32[3,32,512]{2,1,0:T(8,128)S(1)}, f32[6,4,512]{2,1,0:T(4,128)S(1)}, f32[8,4,512]{2,1,0:T(4,128)S(1)}) custom-call(f32[9,4,32,512]{3,2,1,0:T(8,128)S(1)} %copy-done, f32[4,32,512]{2,1,0:T(8,128)S(1)} %copy-done.2, f32[4,32,512]{2,1,0:T(8,128)S(1)} %copy-done.3, f32[4,32,512]{2,1,0:T(8,128)S(1)} %copy-done.5), custom_call_target="tpu_custom_call" | custom-call | tf_op jit(solution)/shard_map/pallas_call | solution.py:286
  19.5 0.0 copy-start.4
  19.5 0.0 copy-start.6
  19.5 9.5 %collective-permute-start = (f32[3,32,512]{2,1,0:T(8,128)S(1)}, f32[3,32,512]{2,1,0:T(8,128)S(1)}, u32[]{:S(2)}, u32[]{:S(2)}) collective-permute-start(f32[3,32,512]{2,1,0:T(8,128)S(1)} %get-tuple-element.20), channel_id=1, source_target_pairs={{4,8},{8,4},{12,16},{16,12},{20,24},{24,20},{28,32},{32,28},{36,40... | collective-permute-start | bytes 589832 | tf_op jit(solution)/shard_map/ppermute | solution.py:303
  29.1 0.1 collective-permute-start.1
  29.2 2.9 %collective-permute-start.3 = (f32[8,4,512]{2,1,0:T(4,128)S(1)}, f32[8,4,512]{2,1,0:T(4,128)S(1)}, u32[]{:S(2)}, u32[]{:S(2)}) collective-permute-start(f32[8,4,512]{2,1,0:T(4,128)S(1)} %get-tuple-element.23), channel_id=1, source_target_pairs={{1,0},{2,1},{3,2},{5,4},{6,5},{7,6},{9,8},{10,9},{11,10},{13,12},{... | collective-permute-start | bytes 196616 | tf_op jit(solution)/shard_map/ppermute | solution.py:306
  32.1 2.9 %collective-permute-start.2 = (f32[6,4,512]{2,1,0:T(4,128)S(1)}, f32[6,4,512]{2,1,0:T(4,128)S(1)}, u32[]{:S(2)}, u32[]{:S(2)}) collective-permute-start(f32[6,4,512]{2,1,0:T(4,128)S(1)} %get-tuple-element.22), channel_id=1, source_target_pairs={{0,1},{1,2},{2,3},{4,5},{5,6},{6,7},{8,9},{9,10},{10,11},{12,13},{... | collective-permute-start | bytes 147464 | tf_op jit(solution)/shard_map/ppermute | solution.py:305
  35.0 5.3 %collective-permute-done.2.prior_y.s_prior_y = f32[6,4,512]{2,1,0:T(4,128)S(1)} collective-permute-done((f32[6,4,512]{2,1,0:T(4,128)S(1)}, f32[6,4,512]{2,1,0:T(4,128)S(1)}, u32[]{:S(2)}, u32[]{:S(2)}) %collective-permute-start.2) | collective-permute-done | bytes 49184 | tf_op jit(solution)/shard_map/ppermute | solution.py:305
  40.4 1.3 %collective-permute-done.3.next_y.s_next_y = f32[8,4,512]{2,1,0:T(4,128)S(1)} collective-permute-done((f32[8,4,512]{2,1,0:T(4,128)S(1)}, f32[8,4,512]{2,1,0:T(4,128)S(1)}, u32[]{:S(2)}, u32[]{:S(2)}) %collective-permute-start.3) | collective-permute-done | bytes 65568 | tf_op jit(solution)/shard_map/ppermute | solution.py:306
  41.7 5.8 %collective-permute-done.far_in.s_far = f32[3,32,512]{2,1,0:T(8,128)S(1)} collective-permute-done((f32[3,32,512]{2,1,0:T(8,128)S(1)}, f32[3,32,512]{2,1,0:T(8,128)S(1)}, u32[]{:S(2)}, u32[]{:S(2)}) %collective-permute-start) | collective-permute-done | bytes 196640 | tf_op jit(solution)/shard_map/ppermute | solution.py:303
  47.4 0.0 collective-permute-done.1.near_in.s_near
  47.4 0.4 shard_map.87
  47.9 2.7 %collective-permute-start.4 = (f32[104,512]{1,0:T(8,128)S(1)}, f32[104,512]{1,0:T(8,128)S(1)}, u32[]{:S(2)}, u32[]{:S(2)}) collective-permute-start(f32[104,512]{1,0:T(8,128)S(1)} %get-tuple-element.27), channel_id=1, source_target_pairs={{4,8},{8,4},{12,16},{16,12},{20,24},{24,20},{28,32},{32,28},{36,40... | collective-permute-start | bytes 638984 | tf_op jit(solution)/shard_map/ppermute | solution.py:303
  50.6 0.1 collective-permute-start.5
  50.7 3.1 %collective-permute-start.6 = (f32[3,4,512]{2,1,0:T(4,128)S(1)}, f32[3,4,512]{2,1,0:T(4,128)S(1)}, u32[]{:S(2)}, u32[]{:S(2)}) collective-permute-start(f32[3,4,512]{2,1,0:T(4,128)S(1)} %get-tuple-element.25.last_y), channel_id=1, source_target_pairs={{0,1},{1,2},{2,3},{4,5},{5,6},{6,7},{8,9},{9,10},{10,11},{12,13},{... | collective-permute-start | bytes 73736 | tf_op jit(solution)/shard_map/ppermute | solution.py:305
  53.8 2.7 %collective-permute-start.7 = (f32[3,4,512]{2,1,0:T(4,128)S(1)}, f32[3,4,512]{2,1,0:T(4,128)S(1)}, u32[]{:S(2)}, u32[]{:S(2)}) collective-permute-start(f32[3,4,512]{2,1,0:T(4,128)S(1)} %get-tuple-element.26.first_y), channel_id=1, source_target_pairs={{1,0},{2,1},{3,2},{5,4},{6,5},{7,6},{9,8},{10,9},{11,10},{13,12},{... | collective-permute-start | bytes 73736 | tf_op jit(solution)/shard_map/ppermute | solution.py:306
  56.5 0.6 collective-permute-done.6.v_prior_y
  57.2 2.3 %collective-permute-done.7.v_next_y = f32[3,4,512]{2,1,0:T(4,128)S(1)} collective-permute-done((f32[3,4,512]{2,1,0:T(4,128)S(1)}, f32[3,4,512]{2,1,0:T(4,128)S(1)}, u32[]{:S(2)}, u32[]{:S(2)}) %collective-permute-start.7) | collective-permute-done | bytes 24608 | tf_op jit(solution)/shard_map/ppermute | solution.py:306
  59.5 4.1 %collective-permute-done.4.v_far = f32[104,512]{1,0:T(8,128)S(1)} collective-permute-done((f32[104,512]{1,0:T(8,128)S(1)}, f32[104,512]{1,0:T(8,128)S(1)}, u32[]{:S(2)}, u32[]{:S(2)}) %collective-permute-start.4) | collective-permute-done | bytes 213024 | tf_op jit(solution)/shard_map/ppermute | solution.py:303
  63.6 0.0 collective-permute-done.5.v_near
  63.6 0.0 copy-done.4
  63.6 0.0 copy-done.6
  63.6 1.1 %shard_map.88 = (f32[3,4,32,512]{3,2,1,0:T(8,128)S(1)}, f32[6,4,32,512]{3,2,1,0:T(8,128)S(1)}, f32[6,4,32,512]{3,2,1,0:T(8,128)S(1)}, f32[2,32,512]{2,1,0:T(8,12...) custom-call(f32[9,4,32,512]{3,2,1,0:T(8,128)S(1)} %copy-done, ...), custom_call_target="tpu_custom_call" | custom-call | tf_op jit(solution)/shard_map/pallas_call | solution.py:286
  64.7 0.0 copy-start.7
  64.7 1.2 %copy-done.7 = f32[6,4,32,512]{3,2,1,0:T(8,128)} copy-done((f32[6,4,32,512]{3,2,1,0:T(8,128)}, f32[6,4,32,512]{3,2,1,0:T(8,128)S(1)}, u32[]{:S(2)}) %copy-start.7) | copy-done | bytes 1572888
  65.9 3.6 %collective-permute-start.8 = (f32[2,32,512]{2,1,0:T(8,128)S(1)}, f32[2,32,512]{2,1,0:T(8,128)S(1)}, u32[]{:S(2)}, u32[]{:S(2)}) collective-permute-start(f32[2,32,512]{2,1,0:T(8,128)S(1)} %get-tuple-element.31), channel_id=1, source_target_pairs={{4,8},{8,4},{12,16},{16,12},{20,24},{24,20},{28,32},{32,28},{36,40... | collective-permute-start | bytes 393224 | tf_op jit(solution)/shard_map/ppermute | solution.py:303
  69.5 0.1 collective-permute-start.9
  69.6 3.4 %collective-permute-start.11 = (f32[2,4,512]{2,1,0:T(4,128)S(1)}, f32[2,4,512]{2,1,0:T(4,128)S(1)}, u32[]{:S(2)}, u32[]{:S(2)}) collective-permute-start(f32[2,4,512]{2,1,0:T(4,128)S(1)} %get-tuple-element.34), channel_id=1, source_target_pairs={{1,0},{2,1},{3,2},{5,4},{6,5},{7,6},{9,8},{10,9},{11,10},{13,12},{... | collective-permute-start | bytes 49160 | tf_op jit(solution)/shard_map/ppermute | solution.py:306
  73.1 2.4 %collective-permute-start.10 = (f32[1,4,512]{2,1,0:T(4,128)S(1)}, f32[1,4,512]{2,1,0:T(4,128)S(1)}, u32[]{:S(2)}, u32[]{:S(2)}) collective-permute-start(f32[1,4,512]{2,1,0:T(4,128)S(1)} %get-tuple-element.33), channel_id=1, source_target_pairs={{0,1},{1,2},{2,3},{4,5},{5,6},{6,7},{8,9},{9,10},{10,11},{12,13},{... | collective-permute-start | bytes 24584 | tf_op jit(solution)/shard_map/ppermute | solution.py:305
  75.5 3.1 %collective-permute-done.10.prior_y = f32[1,4,512]{2,1,0:T(4,128)S(1)} collective-permute-done((f32[1,4,512]{2,1,0:T(4,128)S(1)}, f32[1,4,512]{2,1,0:T(4,128)S(1)}, u32[]{:S(2)}, u32[]{:S(2)}) %collective-permute-start.10) | collective-permute-done | bytes 8224 | tf_op jit(solution)/shard_map/ppermute | solution.py:305
  78.6 0.0 collective-permute-done.11.next_y
  78.6 0.7 collective-permute-done.8.v_far
  79.3 0.0 collective-permute-done.9.v_near
  79.3 0.0 copy-start.12
  79.3 2.0 %shard_map.89 = (f32[9,4,32,512]{3,2,1,0:T(8,128)}, f32[6,4,32,512]{3,2,1,0:T(8,128)S(1)}) custom-call(f32[3,4,32,512]{3,2,1,0:T(8,128)S(1)} %get-tuple-element.29.v, f32[6,4,32,512]{3,2,1,0:T(8,128)S(1)} %get-tuple-element.30.stress, f32[4,32,512]{2,1,0:T(8,128)S(1)} %copy-done.4, f32[4,32,512]{2,1,0:T(8,128)S(1)} %copy-done.6, ...), custom_call_target="tpu_custom_call" | custom-call | tf_op jit(solution)/shard_map/pallas_call | solution.py:286
  81.3 0.0 copy-start.9
  81.3 1.1 %copy-done.9 = f32[6,4,32,512]{3,2,1,0:T(8,128)} copy-done((f32[6,4,32,512]{3,2,1,0:T(8,128)}, f32[6,4,32,512]{3,2,1,0:T(8,128)S(1)}, u32[]{:S(2)}) %copy-start.9) | copy-done | bytes 1572888
  82.4 0.0 all-to-all-done
  82.4 0.0 copy-done.12
  82.4 0.0 copy-start.8
  82.4 1.4 %copy-done.8 = f32[6,4,32,512]{3,2,1,0:T(8,128)S(1)} copy-done((f32[6,4,32,512]{3,2,1,0:T(8,128)S(1)}, f32[6,4,32,512]{3,2,1,0:T(8,128)}, u32[]{:S(2)}) %copy-start.8) | copy-done | bytes 1572888
  83.8 0.0 copy-start.10
  83.8 1.4 %copy-done.10 = f32[6,4,32,512]{3,2,1,0:T(8,128)S(1)} copy-done((f32[6,4,32,512]{3,2,1,0:T(8,128)S(1)}, f32[6,4,32,512]{3,2,1,0:T(8,128)}, u32[]{:S(2)}) %copy-start.10) | copy-done | bytes 1572888
  85.2 1.9 %shard_map.91 = f32[2,4,32,512]{3,2,1,0:T(8,128)} custom-call(s32[1600,128]{1,0:T(8,128)S(1)} %bitcast.8, s32[1,64]{1,0:T(1,128)S(1)} %copy-done.12, f32[6,4,32,512]{3,2,1,0:T(8,128)S(1)} %copy-done.8, f32[6,4,32,512]{3,2,1,0:T(8,128)S(1)} %copy-done.10), custom_call_target="tpu_custom_call" | custom-call | tf_op jit(solution)/shard_map/pallas_call | solution.py:286
  (1 shorter events, 0.0 us)
Async XLA Ops:
  1.3 1.1 %copy-start.11 = (s32[1,64,1,12,256]{4,2,3,1,0:T(1,128)S(1)}, s32[1,64,1,12,256]{4,2,3,1,0:T(1,128)}, u32[]{:S(2)}) copy-start(s32[1,64,1,12,256]{4,2,3,1,0:T(1,128)} %param.11) | copy-start | bytes 2359300
  2.5 14.1 %copy-start = (f32[9,4,32,512]{3,2,1,0:T(8,128)S(1)}, f32[9,4,32,512]{3,2,1,0:T(8,128)}, u32[]{:S(2)}) copy-start(f32[9,4,32,512]{3,2,1,0:T(8,128)} %adj.5) | copy-start | bytes 7077892
  2.5 14.1 %copy-start.2 = (f32[4,32,512]{2,1,0:T(8,128)S(1)}, f32[4,32,512]{2,1,0:T(8,128)}, u32[]{:S(2)}) copy-start(f32[4,32,512]{2,1,0:T(8,128)} %buoy.5) | copy-start | bytes 786436
  2.6 0.9 %copy-start.1 = (s32[1600,128]{1,0:T(8,128)}, s32[1600,128]{1,0:T(8,128)S(1)}, u32[]{:S(2)}) copy-start(s32[1600,128]{1,0:T(8,128)S(1)} %shard_map.90) | copy-start | bytes 2457604
  3.6 78.9 %all-to-all-start = ((s32[64,25,1,128]{3,2,1,0:T(1,128)}), s32[64,25,1,128]{3,2,1,0:T(1,128)S(1)}, u32[]{:S(2)}, u32[]{:S(2)}) async-start(s32[64,25,1,128]{3,2,1,0:T(1,128)} %bitcast.9), calls=%async_computation | async-start | bytes 1638400 | tf_op jit(solution)/shard_map/all_to_all | solution.py:328
  16.6 1.0 %copy-start.3 = (f32[4,32,512]{2,1,0:T(8,128)S(1)}, f32[4,32,512]{2,1,0:T(8,128)}, u32[]{:S(2)}) copy-start(f32[4,32,512]{2,1,0:T(8,128)} %lam.5) | copy-start | bytes 786436
  17.5 0.9 %copy-start.5 = (f32[4,32,512]{2,1,0:T(8,128)S(1)}, f32[4,32,512]{2,1,0:T(8,128)}, u32[]{:S(2)}) copy-start(f32[4,32,512]{2,1,0:T(8,128)} %mu.5) | copy-start | bytes 786436
  19.5 44.1 %copy-start.4 = (f32[4,32,512]{2,1,0:T(8,128)S(1)}, f32[4,32,512]{2,1,0:T(8,128)}, u32[]{:S(2)}) copy-start(f32[4,32,512]{2,1,0:T(8,128)} %lam.5) | copy-start | bytes 786436
  19.5 44.1 %copy-start.6 = (f32[4,32,512]{2,1,0:T(8,128)S(1)}, f32[4,32,512]{2,1,0:T(8,128)}, u32[]{:S(2)}) copy-start(f32[4,32,512]{2,1,0:T(8,128)} %mu.5) | copy-start | bytes 786436
  19.5 27.9 %collective-permute-start = (f32[3,32,512]{2,1,0:T(8,128)S(1)}, f32[3,32,512]{2,1,0:T(8,128)S(1)}, u32[]{:S(2)}, u32[]{:S(2)}) collective-permute-start(f32[3,32,512]{2,1,0:T(8,128)S(1)} %get-tuple-element.20), channel_id=1, source_target_pairs={{4,8},{8,4},{12,16},{16,12},{20,24},{24,20},{28,32},{32,28},{36,40... | collective-permute-start | bytes 589832 | tf_op jit(solution)/shard_map/ppermute | solution.py:303
  29.1 18.4 %collective-permute-start.1 = (f32[3,32,512]{2,1,0:T(8,128)S(1)}, f32[3,32,512]{2,1,0:T(8,128)S(1)}, u32[]{:S(2)}, u32[]{:S(2)}) collective-permute-start(f32[3,32,512]{2,1,0:T(8,128)S(1)} %get-tuple-element.21), channel_id=1, source_target_pairs={{0,4},{4,0},{8,12},{12,8},{16,20},{20,16},{24,28},{28,24},{32,36},... | collective-permute-start | bytes 589832 | tf_op jit(solution)/shard_map/ppermute | solution.py:304
  29.2 12.5 %collective-permute-start.3 = (f32[8,4,512]{2,1,0:T(4,128)S(1)}, f32[8,4,512]{2,1,0:T(4,128)S(1)}, u32[]{:S(2)}, u32[]{:S(2)}) collective-permute-start(f32[8,4,512]{2,1,0:T(4,128)S(1)} %get-tuple-element.23), channel_id=1, source_target_pairs={{1,0},{2,1},{3,2},{5,4},{6,5},{7,6},{9,8},{10,9},{11,10},{13,12},{... | collective-permute-start | bytes 196616 | tf_op jit(solution)/shard_map/ppermute | solution.py:306
  32.1 8.3 %collective-permute-start.2 = (f32[6,4,512]{2,1,0:T(4,128)S(1)}, f32[6,4,512]{2,1,0:T(4,128)S(1)}, u32[]{:S(2)}, u32[]{:S(2)}) collective-permute-start(f32[6,4,512]{2,1,0:T(4,128)S(1)} %get-tuple-element.22), channel_id=1, source_target_pairs={{0,1},{1,2},{2,3},{4,5},{5,6},{6,7},{8,9},{9,10},{10,11},{12,13},{... | collective-permute-start | bytes 147464 | tf_op jit(solution)/shard_map/ppermute | solution.py:305
  47.9 15.7 %collective-permute-start.4 = (f32[104,512]{1,0:T(8,128)S(1)}, f32[104,512]{1,0:T(8,128)S(1)}, u32[]{:S(2)}, u32[]{:S(2)}) collective-permute-start(f32[104,512]{1,0:T(8,128)S(1)} %get-tuple-element.27), channel_id=1, source_target_pairs={{4,8},{8,4},{12,16},{16,12},{20,24},{24,20},{28,32},{32,28},{36,40... | collective-permute-start | bytes 638984 | tf_op jit(solution)/shard_map/ppermute | solution.py:303
  50.6 13.0 %collective-permute-start.5 = (f32[104,512]{1,0:T(8,128)S(1)}, f32[104,512]{1,0:T(8,128)S(1)}, u32[]{:S(2)}, u32[]{:S(2)}) collective-permute-start(f32[104,512]{1,0:T(8,128)S(1)} %get-tuple-element.28), channel_id=1, source_target_pairs={{0,4},{4,0},{8,12},{12,8},{16,20},{20,16},{24,28},{28,24},{32,36},... | collective-permute-start | bytes 638984 | tf_op jit(solution)/shard_map/ppermute | solution.py:304
  50.7 6.5 %collective-permute-start.6 = (f32[3,4,512]{2,1,0:T(4,128)S(1)}, f32[3,4,512]{2,1,0:T(4,128)S(1)}, u32[]{:S(2)}, u32[]{:S(2)}) collective-permute-start(f32[3,4,512]{2,1,0:T(4,128)S(1)} %get-tuple-element.25.last_y), channel_id=1, source_target_pairs={{0,1},{1,2},{2,3},{4,5},{5,6},{6,7},{8,9},{9,10},{10,11},{12,13},{... | collective-permute-start | bytes 73736 | tf_op jit(solution)/shard_map/ppermute | solution.py:305
  53.8 5.7 %collective-permute-start.7 = (f32[3,4,512]{2,1,0:T(4,128)S(1)}, f32[3,4,512]{2,1,0:T(4,128)S(1)}, u32[]{:S(2)}, u32[]{:S(2)}) collective-permute-start(f32[3,4,512]{2,1,0:T(4,128)S(1)} %get-tuple-element.26.first_y), channel_id=1, source_target_pairs={{1,0},{2,1},{3,2},{5,4},{6,5},{7,6},{9,8},{10,9},{11,10},{13,12},{... | collective-permute-start | bytes 73736 | tf_op jit(solution)/shard_map/ppermute | solution.py:306
  64.7 1.2 %copy-start.7 = (f32[6,4,32,512]{3,2,1,0:T(8,128)}, f32[6,4,32,512]{3,2,1,0:T(8,128)S(1)}, u32[]{:S(2)}) copy-start(f32[6,4,32,512]{3,2,1,0:T(8,128)S(1)} %get-tuple-element.36.strain1) | copy-start | bytes 4718596
  65.9 13.3 %collective-permute-start.8 = (f32[2,32,512]{2,1,0:T(8,128)S(1)}, f32[2,32,512]{2,1,0:T(8,128)S(1)}, u32[]{:S(2)}, u32[]{:S(2)}) collective-permute-start(f32[2,32,512]{2,1,0:T(8,128)S(1)} %get-tuple-element.31), channel_id=1, source_target_pairs={{4,8},{8,4},{12,16},{16,12},{20,24},{24,20},{28,32},{32,28},{36,40... | collective-permute-start | bytes 393224 | tf_op jit(solution)/shard_map/ppermute | solution.py:303
  69.5 9.7 %collective-permute-start.9 = (f32[2,32,512]{2,1,0:T(8,128)S(1)}, f32[2,32,512]{2,1,0:T(8,128)S(1)}, u32[]{:S(2)}, u32[]{:S(2)}) collective-permute-start(f32[2,32,512]{2,1,0:T(8,128)S(1)} %get-tuple-element.32), channel_id=1, source_target_pairs={{0,4},{4,0},{8,12},{12,8},{16,20},{20,16},{24,28},{28,24},{32,36},... | collective-permute-start | bytes 393224 | tf_op jit(solution)/shard_map/ppermute | solution.py:304
  69.6 9.0 %collective-permute-start.11 = (f32[2,4,512]{2,1,0:T(4,128)S(1)}, f32[2,4,512]{2,1,0:T(4,128)S(1)}, u32[]{:S(2)}, u32[]{:S(2)}) collective-permute-start(f32[2,4,512]{2,1,0:T(4,128)S(1)} %get-tuple-element.34), channel_id=1, source_target_pairs={{1,0},{2,1},{3,2},{5,4},{6,5},{7,6},{9,8},{10,9},{11,10},{13,12},{... | collective-permute-start | bytes 49160 | tf_op jit(solution)/shard_map/ppermute | solution.py:306
  73.1 5.5 %collective-permute-start.10 = (f32[1,4,512]{2,1,0:T(4,128)S(1)}, f32[1,4,512]{2,1,0:T(4,128)S(1)}, u32[]{:S(2)}, u32[]{:S(2)}) collective-permute-start(f32[1,4,512]{2,1,0:T(4,128)S(1)} %get-tuple-element.33), channel_id=1, source_target_pairs={{0,1},{1,2},{2,3},{4,5},{5,6},{6,7},{8,9},{9,10},{10,11},{12,13},{... | collective-permute-start | bytes 24584 | tf_op jit(solution)/shard_map/ppermute | solution.py:305
  79.3 3.1 %copy-start.12 = (s32[1,64]{1,0:T(1,128)S(1)}, s32[1,64]{1,0:T(1,128)}, u32[]{:S(2)}) copy-start(s32[1,64]{1,0:T(1,128)} %perm.1) | copy-start | bytes 772
  81.3 1.1 %copy-start.9 = (f32[6,4,32,512]{3,2,1,0:T(8,128)}, f32[6,4,32,512]{3,2,1,0:T(8,128)S(1)}, u32[]{:S(2)}) copy-start(f32[6,4,32,512]{3,2,1,0:T(8,128)S(1)} %get-tuple-element.37.strain2) | copy-start | bytes 4718596
  82.4 1.4 %copy-start.8 = (f32[6,4,32,512]{3,2,1,0:T(8,128)S(1)}, f32[6,4,32,512]{3,2,1,0:T(8,128)}, u32[]{:S(2)}) copy-start(f32[6,4,32,512]{3,2,1,0:T(8,128)} %copy-done.7) | copy-start | bytes 4718596
  83.8 1.4 %copy-start.10 = (f32[6,4,32,512]{3,2,1,0:T(8,128)S(1)}, f32[6,4,32,512]{3,2,1,0:T(8,128)}, u32[]{:S(2)}) copy-start(f32[6,4,32,512]{3,2,1,0:T(8,128)} %copy-done.9) | copy-start | bytes 4718596

commit v3 on v2

--- a/solution.py
+++ b/solution.py
@@ -81,7 +81,21 @@
     return jnp.where(lower, down, up), jnp.where(lower, up, down)
 
 
-def prepare(adj, buoy, lam, mu, far, near, to_next_y, to_prior_y, rows, sems, row_sems):
+def on_even_row():
+    return lax.axis_index("gy") % 2 == 0
+
+
+def prior_next(first, second):
+    even = on_even_row()
+    return jnp.where(even, second[...], first[...]), jnp.where(even, first[...], second[...])
+
+
+def first_second(to_next, to_prior):
+    even = on_even_row()
+    return jnp.where(even, to_next, to_prior), jnp.where(even, to_prior, to_next)
+
+
+def prepare(adj, buoy, lam, mu, far, near, first, second, rows, sems, row_sems):
     cells_x, cells_y = adj.shape[1:3]
     extra = (buoy, lam, mu)
 
@@ -112,24 +126,40 @@
         copy.start()
     for copy in copies:
         copy.wait()
-    for k in range(len(UP_ROWS)):
-        to_next_y[k] = rows[k, :, 7, :]
     for k in range(len(DOWN_ROWS)):
-        to_prior_y[k] = rows[len(UP_ROWS) + k, :, 0, :]
+        down = rows[len(UP_ROWS) + k, :, 0, :]
+        up = rows[k, :, 7, :] if k < len(UP_ROWS) else jnp.zeros_like(down)
+        first[k], second[k] = first_second(up, down)
     both("wait")
 
 
-def merge(packed, scales, message):
+def merge(packed, scales, message, words, build, word_sems, sems):
     comp, _, count = scales.shape
     per = packed.shape[0] // count
+    size = 16
+    starts = range(0, count, size)
+    loads = []
+    for n, start in enumerate(starts):
+        part = pl.ds(start * per, size * per)
+        loads.append(pltpu.make_async_copy(packed.at[part], words.at[part], word_sems.at[n]))
+        loads[-1].start()
     factor = jnp.pad(scales[:, 0, :], ((0, 128 - comp), (0, 128 - count)))
     factor = (jnp.transpose(factor)[:count] * FACTOR_UP).astype(jnp.int32)
-    message[pl.ds(per, count, stride=per + 1), :] = factor
-    for r in range(per):
-        message[pl.ds(r, count, stride=per + 1), :] = packed[pl.ds(r, count, stride=per), :]
-
-
-def first_velocity(adj, buoy, far_in, near_in, prior_y, next_y, v, far, near, to_next_y, to_prior_y):
+    build[pl.ds(per, count, stride=per + 1), :] = factor
+    copies = []
+    for n, start in enumerate(starts):
+        loads[n].wait()
+        for r in range(per):
+            build[pl.ds(start * (per + 1) + r, size, stride=per + 1), :] = words[pl.ds(start * per + r, size, stride=per), :]
+        part = pl.ds(start * (per + 1), size * (per + 1))
+        copies.append(pltpu.make_async_copy(build.at[part], message.at[part], sems.at[n]))
+        copies[-1].start()
+    for copy in copies:
+        copy.wait()
+
+
+def first_velocity(adj, buoy, far_in, near_in, first_in, second_in, v_out, far, near, first, second, v, sems):
+    prior_y, next_y = prior_next(first_in, second_in)
     cells_x, cells_y = adj.shape[1:3]
     last = cells_x - 1
     below, above = below_above(far_in, near_in)
@@ -142,8 +172,10 @@
         )
         for k in range(3):
             v[k, x] = new[k]
-            to_next_y[k, x : x + 1, :] = new[k][cells_y - 1 :, :]
-            to_prior_y[k, x : x + 1, :] = new[k][0:1, :]
+    copy = pltpu.make_async_copy(v, v_out, sems.at[0])
+    copy.start()
+    for k in range(3):
+        first[k], second[k] = first_second(v[k, :, cells_y - 1, :], v[k, :, 0, :])
     own = {n: next_y[k, last : last + 1] for k, n in enumerate(DOWN_ROWS)}
     scaled_up = courant * own[9]
     sides = (own[6] - adj[6, last][cells_y - 1 :, :]) + (own[7] - below_z(own[7]))
@@ -157,11 +189,12 @@
     at = 3 * cells_y
     far[at : at + 1, :], near[at : at + 1, :] = far_near(part_up, part_down)
     far[at + 1 : at + 2, :], near[at + 1 : at + 2, :] = far_near(scaled_up, scaled_down)
-
-
-def middle(
-    adj, buoy, lam, mu, s_far, s_near, s_prior_y, s_next_y, v, last_y, first_y, v_far, v_near, v_prior_y, v_next_y,
-    v_new, stress, strain, far, near, to_next_y, to_prior_y,
+    copy.wait()
+
+
+def half(
+    adj, buoy, lam, mu, s_far, s_near, s_prior_y, s_next_y, v, v_far, v_near, v_prior_y, v_next_y,
+    v_new, stress, strain, between,
 ):
     cells_x, cells_y = adj.shape[1:3]
     last = cells_x - 1
@@ -181,12 +214,12 @@
     sxz_prior = s_below(1) - courant * s_below(2) * exz
     over = v_next_y[0]
     exx = over - jnp.concatenate([vx_corner, over[:last]], axis=0)
-    eyy = v_next_y[1] - last_y[1]
+    eyy = v_next_y[1] - v[1, :, cells_y - 1, :]
     trace = exx + eyy + (v_next_y[2] - below_z(v_next_y[2]))
     syy_rows = s_next_y[0] - courant * (s_next_y[1] * trace + 2.0 * s_next_y[2] * eyy)
     under = v_prior_y[1]
-    exy = (first_y[0] - v_prior_y[0]) + (jnp.concatenate([under[1:], vy_corner], axis=0) - under)
-    eyz = (above_z(under) - under) + (first_y[2] - v_prior_y[2])
+    exy = (v[0, :, 0, :] - v_prior_y[0]) + (jnp.concatenate([under[1:], vy_corner], axis=0) - under)
+    eyz = (above_z(under) - under) + (v[2, :, 0, :] - v_prior_y[2])
     sxy_rows = s_prior_y[0] - courant * s_prior_y[2] * exy
     syz_rows = s_prior_y[1] - courant * s_prior_y[2] * eyz
     for x in range(cells_x):
@@ -197,8 +230,10 @@
         )
         s = stress_plane([adj[3 + k, x] for k in range(6)], e, lam[x], mu[x])
         for k in range(6):
-            strain[k, x] = e[k]
             stress[k, x] = s[k]
+            if strain is not None:
+                strain[k, x] = e[k]
+    between()
     for x in range(cells_x):
         new = velocity_plane(
             (v[0, x], v[1, x], v[2, x]), courant * buoy[x],
@@ -208,36 +243,53 @@
         )
         for k in range(3):
             v_new[k, x] = new[k]
-        to_next_y[0, x : x + 1, :] = new[1][cells_y - 1 :, :]
-        to_prior_y[0, x : x + 1, :] = new[0][0:1, :]
-        to_prior_y[1, x : x + 1, :] = new[2][0:1, :]
-    far[0], near[0] = far_near(v_new[0, last], v_new[1, 0])
+
+
+def middle(
+    adj, buoy, lam_in, mu_in, s_far_in, s_near_in, v_in, s_first, s_second, v_far, v_near, v_first, v_second,
+    fields, strain_out, far, near, first, second, lam, mu, s_far, s_near, v, v_new, stress, strain, load_sems, sems,
+):
+    plans = ((lam_in, lam), (mu_in, mu), (s_far_in, s_far), (s_near_in, s_near), (v_in, v))
+    loads = [pltpu.make_async_copy(source, target, load_sems.at[n]) for n, (source, target) in enumerate(plans)]
+    for copy in loads:
+        copy.start()
+    copies = [
+        pltpu.make_async_copy(strain, strain_out, sems.at[0]),
+        pltpu.make_async_copy(stress, fields.at[pl.ds(3, 6)], sems.at[1]),
+        pltpu.make_async_copy(v_new, fields.at[pl.ds(0, 3)], sems.at[2]),
+    ]
+    for copy in loads:
+        copy.wait()
+    half(
+        adj, buoy, lam, mu, s_far, s_near, *prior_next(s_first, s_second), v, v_far, v_near, *prior_next(v_first, v_second),
+        v_new, stress, strain, lambda: [copy.start() for copy in copies[:2]],
+    )
+    copies[2].start()
+    _, cells_x, cells_y, _ = v_new.shape
+    over, under = v_new[1, :, cells_y - 1, :], v_new[0, :, 0, :]
+    first[0], second[0] = first_second(over, under)
+    under = v_new[2, :, 0, :]
+    first[1], second[1] = first_second(jnp.zeros_like(under), under)
+    far[0], near[0] = far_near(v_new[0, cells_x - 1], v_new[1, 0])
     far[1], near[1] = far_near(jnp.zeros_like(v_new[2, 0]), v_new[2, 0])
-
-
-def second_stress(v, stress, lam, mu, v_far, v_near, prior_y, next_y, out, strain):
-    cells_x = v.shape[1]
-    last = cells_x - 1
-    below, above = below_above(v_far, v_near)
-    for x in range(cells_x):
-        e = strain_plane(
-            v[0, x], v[0, x - 1] if x > 0 else below(0), next_y[0, x : x + 1],
-            v[1, x], v[1, x + 1] if x < last else above(0), prior_y[0, x : x + 1],
-            v[2, x], v[2, x + 1] if x < last else above(1), next_y[1, x : x + 1],
-        )
-        s = stress_plane([stress[k, x] for k in range(6)], e, lam[x], mu[x])
-        for k in range(3):
-            out[k, x] = v[k, x]
-        for k in range(6):
-            strain[k, x] = e[k]
-            out[3 + k, x] = s[k]
-
-
-def gradients(message, perm, strain1, strain2, out):
+    for copy in copies:
+        copy.wait()
+
+
+def finish(
+    fields, lam_in, mu_in, strain_in, perm_in, v_far, v_near, v_first, v_second, message, out, out_grads,
+    v, stress, lam, mu, strain1, perm, strain2, forward, grads, sems,
+):
+    plans = ((fields.at[pl.ds(0, 3)], v), (fields.at[pl.ds(3, 6)], stress), (lam_in, lam), (mu_in, mu), (strain_in, strain1), (perm_in, perm))
+    prior_y, next_y = prior_next(v_first, v_second)
+    copies = [pltpu.make_async_copy(source, target, sems.at[n]) for n, (source, target) in enumerate(plans)]
+    for copy in copies:
+        copy.start()
     count = perm.shape[1]
     per = message.shape[0] // count
     cells_x, cells_y, cells_z = strain1.shape[1:]
     rows = cells_x * cells_y
+    copies[5].wait()
     both = jnp.concatenate([perm[...], perm[...]], axis=1)
     r = lax.broadcasted_iota(jnp.int32, (rows, 2 * count), 0)
     k = lax.broadcasted_iota(jnp.int32, (rows, 2 * count), 1)
@@ -249,7 +301,7 @@
     factor = jnp.concatenate([factor, jnp.zeros_like(factor)], axis=0)
     factor = lax.dot(pick_factor, factor, precision=lax.Precision.HIGHEST, preferred_element_type=F32)
 
-    def forward(c):
+    for c in range(forward.shape[0]):
         w = [message[pl.ds(2 * c + t, count, stride=per), :] for t in range(2)]
         byte = [lambda w: w & 255, lambda w: lax.shift_right_logical(w, 8) & 255, lambda w: lax.shift_right_logical(w, 16) & 255]
         parts = [[(f(v) - 128) for v in w] for f in byte] + [[lax.shift_right_arithmetic(v, 24) for v in w]]
@@ -258,20 +310,38 @@
         high = jnp.concatenate(parts[2] + parts[3], axis=1)
         table = jnp.concatenate([low, high], axis=0)
         picked = lax.dot(pick, table, preferred_element_type=F32)
-        return picked * factor[:, c : c + 1]
-
-    grad_lambda = None
-    grad_mu = None
+        forward[c] = picked * factor[:, c : c + 1]
+    last = cells_x - 1
+    below, above = below_above(v_far, v_near)
+    for copy in copies[:4]:
+        copy.wait()
+    for x in range(cells_x):
+        e = strain_plane(
+            v[0, x], v[0, x - 1] if x > 0 else below(0), next_y[0, x : x + 1],
+            v[1, x], v[1, x + 1] if x < last else above(0), prior_y[0, x : x + 1],
+            v[2, x], v[2, x + 1] if x < last else above(1), next_y[1, x : x + 1],
+        )
+        s = stress_plane([stress[k, x] for k in range(6)], e, lam[x], mu[x])
+        for k in range(6):
+            strain2[k, x] = e[k]
+            stress[k, x] = s[k]
+    stress_copy = pltpu.make_async_copy(stress, out.at[pl.ds(3, 6)], sems.at[5])
+    stress_copy.start()
+    copies[4].wait()
     for step, strain in enumerate((strain1, strain2)):
-        f = [forward(6 * step + n) for n in range(6)]
+        f = [forward[6 * step + n] for n in range(6)]
         e = [strain[n].reshape(rows, cells_z) for n in range(6)]
         add_lambda = (e[0] + e[1] + e[2]) * (f[0] + f[1] + f[2])
         add_mu = 2.0 * (e[0] * f[0] + e[1] * f[1] + e[2] * f[2])
         grad_lambda = add_lambda if step == 0 else grad_lambda + add_lambda
         grad_mu = add_mu if step == 0 else grad_mu + add_mu
         grad_mu = grad_mu + e[3] * f[3] + e[4] * f[4] + e[5] * f[5]
-    out[0] = grad_lambda.reshape(cells_x, cells_y, cells_z)
-    out[1] = grad_mu.reshape(cells_x, cells_y, cells_z)
+    grads[0] = grad_lambda.reshape(cells_x, cells_y, cells_z)
+    grads[1] = grad_mu.reshape(cells_x, cells_y, cells_z)
+    grads_copy = pltpu.make_async_copy(grads, out_grads, sems.at[6])
+    grads_copy.start()
+    for copy in (stress_copy, grads_copy):
+        copy.wait()
 
 
 def on_device(adjoint, buoyancy, lame_lambda, shear_mu, packed, scales, perm):
@@ -282,29 +352,33 @@
     def shape(*dims, dtype=F32):
         return jax.ShapeDtypeStruct(dims, dtype)
 
-    def call(kernel, mebibytes, outs, args, in_specs=None, scratch=()):
+    def in_hbm(*values):
+        return [pltpu.with_memory_space_constraint(value, pltpu.HBM) for value in values]
+
+    def call(kernel, mebibytes, outs, args, in_specs=None, scratch=(), out_specs=None, aliases={}):
         return pl.pallas_call(
             kernel,
             out_shape=outs,
             in_specs=in_specs or [VMEM] * len(args),
-            out_specs=jax.tree.map(lambda _: VMEM, outs),
+            out_specs=out_specs or (VMEM,) * len(outs),
             scratch_shapes=scratch,
             compiler_params=pltpu.CompilerParams(vmem_limit_bytes=mebibytes << 20),
+            input_output_aliases=aliases,
         )(*args)
 
     count_x = lax.axis_size("gx")
     count_y = lax.axis_size("gy")
     off_chip = [(x, x + 1 if x % 2 else x - 1) for x in range(1, count_x - 1)]
     on_chip = [(x, x ^ 1) for x in range(count_x)]
-    upward = [(y, y + 1) for y in range(count_y - 1)]
-    downward = [(y + 1, y) for y in range(count_y - 1)]
-
-    def swap(far, near, to_next_y, to_prior_y):
+    pairs = [[(y, y + 1) for y in range(start, count_y - 1, 2)] for start in (0, 1)]
+    pairs = [[*there, *((b, a) for a, b in there)] for there in pairs]
+
+    def swap(far, near, first, second):
         far = lax.ppermute(far, "gx", off_chip)
         near = lax.ppermute(near, "gx", on_chip)
-        prior_y = lax.ppermute(to_next_y, "gy", upward)
-        next_y = lax.ppermute(to_prior_y, "gy", downward)
-        return far, near, prior_y, next_y
+        first = lax.ppermute(first, "gy", pairs[0])
+        second = lax.ppermute(second, "gy", pairs[1])
+        return far, near, first, second
 
     def planes(*count):
         return shape(*count, cells_y, cells_z)
@@ -313,8 +387,8 @@
         return shape(count, cells_x, cells_z)
 
     sent = call(
-        prepare, 8, (planes(3), planes(3), lines(len(UP_ROWS)), lines(len(DOWN_ROWS))),
-        (adjoint, buoyancy, lame_lambda, shear_mu), [ANY] * 4,
+        prepare, 8, (planes(3), planes(3), lines(len(DOWN_ROWS)), lines(len(DOWN_ROWS))),
+        in_hbm(adjoint, buoyancy, lame_lambda, shear_mu), [ANY] * 4,
         [
             pltpu.VMEM((len(UP_ROWS) + len(DOWN_ROWS), cells_x, 8, cells_z), F32),
             pltpu.SemaphoreType.DMA((6,)),
@@ -324,28 +398,51 @@
     s_ghosts = swap(*sent)
 
     by_comp = jnp.transpose(scales.reshape(owners, comp)).reshape(comp, 1, owners)
-    message = call(merge, 8, shape(owners * (per + 1), 128, dtype=jnp.int32), (packed.reshape(owners * per, 128), by_comp))
+    size = (owners * (per + 1), 128)
+    (message,) = call(
+        merge, 8, (pltpu.HBM(size, jnp.int32),), (*in_hbm(packed.reshape(owners * per, 128)), by_comp), [ANY, VMEM],
+        [
+            pltpu.VMEM((owners * per, 128), jnp.int32), pltpu.VMEM(size, jnp.int32),
+            pltpu.SemaphoreType.DMA((4,)), pltpu.SemaphoreType.DMA((4,)),
+        ],
+        (ANY,),
+    )
     message = lax.all_to_all(message.reshape(owners, per + 1, 1, 128), "gx", split_axis=0, concat_axis=0, tiled=True)
     message = message.reshape(owners * (per + 1), 128)
 
     faces = shape(3 * cells_y + 8, cells_z)
+    strain = (6, cells_x, cells_y, cells_z)
+    speeds = (3, cells_x, cells_y, cells_z)
     v, *sent = call(
-        first_velocity, 12, (planes(3, cells_x), faces, faces, lines(3), lines(3)), (adjoint, buoyancy, *s_ghosts)
-    )
-    last_y, first_y = sent[2:]
+        first_velocity, 12, (pltpu.HBM(speeds, F32), faces, faces, lines(3), lines(3)), (adjoint, buoyancy, *s_ghosts),
+        scratch=[pltpu.VMEM(speeds, F32), pltpu.SemaphoreType.DMA((1,))], out_specs=(ANY, VMEM, VMEM, VMEM, VMEM),
+    )
     v_ghosts = swap(*sent)
 
-    v, stress, strain1, *sent = call(
+    fields, strain1, *sent = call(
         middle, 16,
-        (planes(3, cells_x), planes(6, cells_x), planes(6, cells_x), planes(2), planes(2), lines(1), lines(2)),
-        (adjoint, buoyancy, lame_lambda, shear_mu, *s_ghosts, v, last_y, first_y, *v_ghosts),
+        (pltpu.HBM(adjoint.shape, F32), pltpu.HBM(strain, F32), planes(2), planes(2), lines(2), lines(2)),
+        (adjoint, buoyancy, *in_hbm(lame_lambda, shear_mu, *s_ghosts[:2], v), *s_ghosts[2:], *v_ghosts),
+        [VMEM] * 2 + [ANY] * 5 + [VMEM] * 6,
+        [pltpu.VMEM(size, F32) for size in (speeds[1:], speeds[1:], speeds[:1] + speeds[2:], speeds[:1] + speeds[2:])]
+        + [pltpu.VMEM(size, F32) for size in (speeds, speeds, strain, strain)]
+        + [pltpu.SemaphoreType.DMA((5,)), pltpu.SemaphoreType.DMA((3,))],
+        (ANY, ANY, VMEM, VMEM, VMEM, VMEM),
     )
     v_ghosts = swap(*sent)
 
-    adjoint_out, strain2 = call(
-        second_stress, 12, (shape(*adjoint.shape), planes(6, cells_x)), (v, stress, lame_lambda, shear_mu, *v_ghosts)
-    )
-    grads = call(gradients, 16, planes(2, cells_x), (message, perm, strain1, strain2))
+    grads = (2, cells_x, cells_y, cells_z)
+    adjoint_out, grads = call(
+        finish, 24, (pltpu.HBM(adjoint.shape, F32), pltpu.HBM(grads, F32)),
+        (*in_hbm(fields, lame_lambda, shear_mu, strain1, perm), *v_ghosts, message),
+        [ANY] * 5 + [VMEM] * 5,
+        [pltpu.VMEM(size, F32) for size in (speeds, strain, speeds[1:], speeds[1:], strain)]
+        + [pltpu.VMEM(perm.shape, jnp.int32)]
+        + [pltpu.VMEM(size, F32) for size in (strain, (comp, cells_x * cells_y, cells_z), grads)]
+        + [pltpu.SemaphoreType.DMA((7,))],
+        (ANY, ANY),
+        {0: 0},
+    )
     return adjoint_out, grads
 
 

time: 88 us -> 89.7 us (1.019)
  the two profiles are of different devices: /device:TPU:70 before, /device:TPU:6 now
where the time goes in v3:
time: 89.7 us; the launch traced here: 89.2 us
  starting transfers between devices  37.1 us (41%)
  waiting for transfers between devices  36.9 us (41%)
  Pallas kernels  13.7 us (15%)
    ppermute x3, waiting for transfers between devices, swap(): first = lax.ppermute(first, 'gy', pairs[0])  21.8 us
    ppermute x3, starting transfers between devices, swap(): far = lax.ppermute(far, 'gx', off_chip)  16.4 us
    ppermute x3, waiting for transfers between devices, swap(): far = lax.ppermute(far, 'gx', off_chip)  15.1 us
    all_to_all x1, starting transfers between devices, on_device(): lax.all_to_all(message.reshape(owners, per + 1, 1, 128), 'gx', split_axis...  14.9 us
    pallas_call x5, Pallas kernels, call(): pl.pallas_call(kernel, out_shape=outs, in_specs=in_specs or [VMEM] * len(...  13.7 us
    ppermute x3, starting transfers between devices, swap(): first = lax.ppermute(first, 'gy', pairs[0])  3.46 us
    ppermute x3, starting transfers between devices, swap(): second = lax.ppermute(second, 'gy', pairs[1])  1.95 us
  transfers between devices with their start and end apart: 13, of which 6 were waited for; matrix products, arithmetic and copies ran while one was open for 0% of the time, Pallas kernels for 8%

profile of v3, /device:TPU:6, one launch (start us, length us, event | category | flops | bytes accessed | tf_op | source)
XLA Modules:
  0.0 89.2 jit_solution(10436633353110726850)
XLA Ops:
  0.6 0.7 copy.13
  1.3 2.0 %shard_map.89 = s32[1600,128]{1,0:T(8,128)} custom-call(s32[1536,128]{1,0:T(8,128)} %bitcast.10, f32[12,1,64]{2,1,0:T(1,128)S(1)} %reshape.21.scales), custom_call_target="tpu_custom_call" | custom-call | tf_op jit(solution)/shard_map/pallas_call | solution.py:359
  3.4 0.0 copy-start
  3.4 0.0 copy-start.1
  3.4 14.9 %all-to-all-start = ((s32[64,25,1,128]{3,2,1,0:T(1,128)}), s32[64,25,1,128]{3,2,1,0:T(1,128)S(1)}, u32[]{:S(2)}, u32[]{:S(2)}) async-start(s32[64,25,1,128]{3,2,1,0:T(1,128)} %bitcast.9), calls=%async_computation | async-start | bytes 1638400 | tf_op jit(solution)/shard_map/all_to_all | solution.py:410
  18.3 1.5 %shard_map.86 = (f32[3,32,512]{2,1,0:T(8,128)S(1)}, f32[3,32,512]{2,1,0:T(8,128)S(1)}, f32[8,4,512]{2,1,0:T(4,128)S(1)}, f32[8,4,512]{2,1,0:T(4,128)S(1)}) custom-call(f32[9,4,32,512]{3,2,1,0:T(8,128)} %adj.5, f32[4,32,512]{2,1,0:T(8,128)} %buoy.5, f32[4,32,512]{2,1,0:T(8,128)} %lam_in.3, f32[4,32,512]{2,1,0:T(8,128)} %mu_in.3), custom_call_target="tpu_custom_call" | custom-call | tf_op jit(solution)/shard_map/pallas_call | solution.py:359
  19.9 9.4 %collective-permute-start = (f32[3,32,512]{2,1,0:T(8,128)S(1)}, f32[3,32,512]{2,1,0:T(8,128)S(1)}, u32[]{:S(2)}, u32[]{:S(2)}) collective-permute-start(f32[3,32,512]{2,1,0:T(8,128)S(1)} %get-tuple-element.17), channel_id=1, source_target_pairs={{4,8},{8,4},{12,16},{16,12},{20,24},{24,20},{28,32},{32,28},{36,40... | collective-permute-start | bytes 589832 | tf_op jit(solution)/shard_map/ppermute | solution.py:377
  29.3 0.1 collective-permute-start.1
  29.4 1.1 %collective-permute-start.2 = (f32[8,4,512]{2,1,0:T(4,128)S(1)}, f32[8,4,512]{2,1,0:T(4,128)S(1)}, u32[]{:S(2)}, u32[]{:S(2)}) collective-permute-start(f32[8,4,512]{2,1,0:T(4,128)S(1)} %get-tuple-element.19), channel_id=1, source_target_pairs={{0,1},{2,3},{1,0},{3,2},{4,5},{6,7},{5,4},{7,6},{8,9},{10,11},{9,8... | collective-permute-start | bytes 196616 | tf_op jit(solution)/shard_map/ppermute | solution.py:379
  30.5 0.7 collective-permute-start.3
  31.2 12.2 %collective-permute-done.2.first_in.s_first = f32[8,4,512]{2,1,0:T(4,128)S(1)} collective-permute-done((f32[8,4,512]{2,1,0:T(4,128)S(1)}, f32[8,4,512]{2,1,0:T(4,128)S(1)}, u32[]{:S(2)}, u32[]{:S(2)}) %collective-permute-start.2) | collective-permute-done | bytes 65568 | tf_op jit(solution)/shard_map/ppermute | solution.py:379
  43.3 0.0 collective-permute-done.3.second_in.s_second
  43.3 5.3 %collective-permute-done.far_in.s_far_in = f32[3,32,512]{2,1,0:T(8,128)S(1)} collective-permute-done((f32[3,32,512]{2,1,0:T(8,128)S(1)}, f32[3,32,512]{2,1,0:T(8,128)S(1)}, u32[]{:S(2)}, u32[]{:S(2)}) %collective-permute-start) | collective-permute-done | bytes 196640 | tf_op jit(solution)/shard_map/ppermute | solution.py:377
  48.7 0.0 copy-start.2
  48.7 0.0 collective-permute-done.1.near_in.s_near_in
  48.7 0.0 copy-done
  48.7 0.0 copy-done.1
  48.7 0.0 copy-start.3
  48.7 1.4 %shard_map.87 = (f32[3,4,32,512]{3,2,1,0:T(8,128)}, f32[104,512]{1,0:T(8,128)S(1)}, f32[104,512]{1,0:T(8,128)S(1)}, f32[3,4,512]{2,1,0:T(4,128)S(1)}, f32[3,4,512]{2,1,0:T(4,128)S(1)}) custom-call(f32[9,4,32,512]{3,2,1,0:T(8,128)S(1)} %copy-done, f32[4,32,512]{2,1,0:T(8,128)S(1)} %copy-done.1, f32[3,32,512]{2,1,0:T(8,128)S(1)} %collective-permute-done.far_in.s_far_in, ...), custom_call_target="tpu_custom_call" | custom-call | tf_op jit(solution)/shard_map/pallas_call | solution.py:359
  50.1 3.8 %collective-permute-start.4 = (f32[104,512]{1,0:T(8,128)S(1)}, f32[104,512]{1,0:T(8,128)S(1)}, u32[]{:S(2)}, u32[]{:S(2)}) collective-permute-start(f32[104,512]{1,0:T(8,128)S(1)} %get-tuple-element.22), channel_id=1, source_target_pairs={{4,8},{8,4},{12,16},{16,12},{20,24},{24,20},{28,32},{32,28},{36,40... | collective-permute-start | bytes 638984 | tf_op jit(solution)/shard_map/ppermute | solution.py:377
  53.9 0.1 collective-permute-start.5
  54.0 0.9 collective-permute-start.6
  54.9 0.7 collective-permute-start.7
  55.5 5.8 %collective-permute-done.6.v_first = f32[3,4,512]{2,1,0:T(4,128)S(1)} collective-permute-done((f32[3,4,512]{2,1,0:T(4,128)S(1)}, f32[3,4,512]{2,1,0:T(4,128)S(1)}, u32[]{:S(2)}, u32[]{:S(2)}) %collective-permute-start.6) | collective-permute-done | bytes 24608 | tf_op jit(solution)/shard_map/ppermute | solution.py:379
  61.3 0.0 collective-permute-done.7.v_second
  61.3 5.4 %collective-permute-done.4.v_far = f32[104,512]{1,0:T(8,128)S(1)} collective-permute-done((f32[104,512]{1,0:T(8,128)S(1)}, f32[104,512]{1,0:T(8,128)S(1)}, u32[]{:S(2)}, u32[]{:S(2)}) %collective-permute-start.4) | collective-permute-done | bytes 213024 | tf_op jit(solution)/shard_map/ppermute | solution.py:377
  66.6 0.0 collective-permute-done.5.v_near
  66.6 0.0 copy-done.2
  66.6 0.0 copy-done.3
  66.6 4.1 %shard_map.88 = (f32[9,4,32,512]{3,2,1,0:T(8,128)}, f32[6,4,32,512]{3,2,1,0:T(8,128)}, f32[2,32,512]{2,1,0:T(8,128)S(1)}, f32[2,32,512]{2,1,0:T(8,128)S(1)}, f32...) custom-call(f32[9,4,32,512]{3,2,1,0:T(8,128)S(1)} %copy-done, f32[4,32,512]{2,1,0:T(8,128)S(1)} %copy-done.1, ...), custom_call_target="tpu_custom_call" | custom-call | tf_op jit(solution)/shard_map/pallas_call | solution.py:359
  70.7 3.3 %collective-permute-start.8 = (f32[2,32,512]{2,1,0:T(8,128)S(1)}, f32[2,32,512]{2,1,0:T(8,128)S(1)}, u32[]{:S(2)}, u32[]{:S(2)}) collective-permute-start(f32[2,32,512]{2,1,0:T(8,128)S(1)} %get-tuple-element.28), channel_id=1, source_target_pairs={{4,8},{8,4},{12,16},{16,12},{20,24},{24,20},{28,32},{32,28},{36,40... | collective-permute-start | bytes 393224 | tf_op jit(solution)/shard_map/ppermute | solution.py:377
  74.0 0.1 collective-permute-start.9
  74.1 1.5 %collective-permute-start.10 = (f32[2,4,512]{2,1,0:T(4,128)S(1)}, f32[2,4,512]{2,1,0:T(4,128)S(1)}, u32[]{:S(2)}, u32[]{:S(2)}) collective-permute-start(f32[2,4,512]{2,1,0:T(4,128)S(1)} %get-tuple-element.30), channel_id=1, source_target_pairs={{0,1},{2,3},{1,0},{3,2},{4,5},{6,7},{5,4},{7,6},{8,9},{10,11},{9,8... | collective-permute-start | bytes 49160 | tf_op jit(solution)/shard_map/ppermute | solution.py:379
  75.6 0.7 collective-permute-start.11
  76.3 3.8 %collective-permute-done.10.v_first = f32[2,4,512]{2,1,0:T(4,128)S(1)} collective-permute-done((f32[2,4,512]{2,1,0:T(4,128)S(1)}, f32[2,4,512]{2,1,0:T(4,128)S(1)}, u32[]{:S(2)}, u32[]{:S(2)}) %collective-permute-start.10) | collective-permute-done | bytes 16416 | tf_op jit(solution)/shard_map/ppermute | solution.py:379
  80.1 0.0 collective-permute-done.11.v_second
  80.1 4.4 %collective-permute-done.8.v_far = f32[2,32,512]{2,1,0:T(8,128)S(1)} collective-permute-done((f32[2,32,512]{2,1,0:T(8,128)S(1)}, f32[2,32,512]{2,1,0:T(8,128)S(1)}, u32[]{:S(2)}, u32[]{:S(2)}) %collective-permute-start.8) | collective-permute-done | bytes 131104 | tf_op jit(solution)/shard_map/ppermute | solution.py:377
  84.5 0.0 collective-permute-done.9.v_near
  84.5 0.0 all-to-all-done
  84.5 4.7 %shard_map.90 = (f32[9,4,32,512]{3,2,1,0:T(8,128)}, f32[2,4,32,512]{3,2,1,0:T(8,128)}) custom-call(f32[9,4,32,512]{3,2,1,0:T(8,128)} %get-tuple-element.26.fields, f32[4,32,512]{2,1,0:T(8,128)} %lam_in.3, f32[4,32,512]{2,1,0:T(8,128)} %mu_in.3, f32[6,4,32,512]{3,2,1,0:T(8,128)} %get-tuple-element.27.strain_in, ...), custom_call_target="tpu_custom_call", output_to_operand_aliasing={{0}: (0, {})} | custom-call | tf_op jit(solution)/shard_map/pallas_call | solution.py:359
  (1 shorter events, 0.0 us)
Async XLA Ops:
  3.4 45.3 %copy-start = (f32[9,4,32,512]{3,2,1,0:T(8,128)S(1)}, f32[9,4,32,512]{3,2,1,0:T(8,128)}, u32[]{:S(2)}) copy-start(f32[9,4,32,512]{3,2,1,0:T(8,128)} %adj.5) | copy-start | bytes 7077892
  3.4 45.3 %copy-start.1 = (f32[4,32,512]{2,1,0:T(8,128)S(1)}, f32[4,32,512]{2,1,0:T(8,128)}, u32[]{:S(2)}) copy-start(f32[4,32,512]{2,1,0:T(8,128)} %buoy.5) | copy-start | bytes 786436
  3.4 81.1 %all-to-all-start = ((s32[64,25,1,128]{3,2,1,0:T(1,128)}), s32[64,25,1,128]{3,2,1,0:T(1,128)S(1)}, u32[]{:S(2)}, u32[]{:S(2)}) async-start(s32[64,25,1,128]{3,2,1,0:T(1,128)} %bitcast.9), calls=%async_computation | async-start | bytes 1638400 | tf_op jit(solution)/shard_map/all_to_all | solution.py:410
  19.9 28.8 %collective-permute-start = (f32[3,32,512]{2,1,0:T(8,128)S(1)}, f32[3,32,512]{2,1,0:T(8,128)S(1)}, u32[]{:S(2)}, u32[]{:S(2)}) collective-permute-start(f32[3,32,512]{2,1,0:T(8,128)S(1)} %get-tuple-element.17), channel_id=1, source_target_pairs={{4,8},{8,4},{12,16},{16,12},{20,24},{24,20},{28,32},{32,28},{36,40... | collective-permute-start | bytes 589832 | tf_op jit(solution)/shard_map/ppermute | solution.py:377
  29.3 19.4 %collective-permute-start.1 = (f32[3,32,512]{2,1,0:T(8,128)S(1)}, f32[3,32,512]{2,1,0:T(8,128)S(1)}, u32[]{:S(2)}, u32[]{:S(2)}) collective-permute-start(f32[3,32,512]{2,1,0:T(8,128)S(1)} %get-tuple-element.18), channel_id=1, source_target_pairs={{0,4},{4,0},{8,12},{12,8},{16,20},{20,16},{24,28},{28,24},{32,36},... | collective-permute-start | bytes 589832 | tf_op jit(solution)/shard_map/ppermute | solution.py:378
  29.4 13.9 %collective-permute-start.2 = (f32[8,4,512]{2,1,0:T(4,128)S(1)}, f32[8,4,512]{2,1,0:T(4,128)S(1)}, u32[]{:S(2)}, u32[]{:S(2)}) collective-permute-start(f32[8,4,512]{2,1,0:T(4,128)S(1)} %get-tuple-element.19), channel_id=1, source_target_pairs={{0,1},{2,3},{1,0},{3,2},{4,5},{6,7},{5,4},{7,6},{8,9},{10,11},{9,8... | collective-permute-start | bytes 196616 | tf_op jit(solution)/shard_map/ppermute | solution.py:379
  30.5 12.8 %collective-permute-start.3 = (f32[8,4,512]{2,1,0:T(4,128)S(1)}, f32[8,4,512]{2,1,0:T(4,128)S(1)}, u32[]{:S(2)}, u32[]{:S(2)}) collective-permute-start(f32[8,4,512]{2,1,0:T(4,128)S(1)} %get-tuple-element.20), channel_id=1, source_target_pairs={{1,2},{2,1},{5,6},{6,5},{9,10},{10,9},{13,14},{14,13},{17,18},{18,... | collective-permute-start | bytes 196616 | tf_op jit(solution)/shard_map/ppermute | solution.py:380
  48.7 17.9 %copy-start.2 = (f32[3,32,512]{2,1,0:T(8,128)}, f32[3,32,512]{2,1,0:T(8,128)S(1)}, u32[]{:S(2)}) copy-start(f32[3,32,512]{2,1,0:T(8,128)S(1)} %collective-permute-done.far_in.s_far_in) | copy-start | bytes 589828
  48.7 17.9 %copy-start.3 = (f32[3,32,512]{2,1,0:T(8,128)}, f32[3,32,512]{2,1,0:T(8,128)S(1)}, u32[]{:S(2)}) copy-start(f32[3,32,512]{2,1,0:T(8,128)S(1)} %collective-permute-done.1.near_in.s_near_in) | copy-start | bytes 589828
  50.1 16.5 %collective-permute-start.4 = (f32[104,512]{1,0:T(8,128)S(1)}, f32[104,512]{1,0:T(8,128)S(1)}, u32[]{:S(2)}, u32[]{:S(2)}) collective-permute-start(f32[104,512]{1,0:T(8,128)S(1)} %get-tuple-element.22), channel_id=1, source_target_pairs={{4,8},{8,4},{12,16},{16,12},{20,24},{24,20},{28,32},{32,28},{36,40... | collective-permute-start | bytes 638984 | tf_op jit(solution)/shard_map/ppermute | solution.py:377
  53.9 12.8 %collective-permute-start.5 = (f32[104,512]{1,0:T(8,128)S(1)}, f32[104,512]{1,0:T(8,128)S(1)}, u32[]{:S(2)}, u32[]{:S(2)}) collective-permute-start(f32[104,512]{1,0:T(8,128)S(1)} %get-tuple-element.23), channel_id=1, source_target_pairs={{0,4},{4,0},{8,12},{12,8},{16,20},{20,16},{24,28},{28,24},{32,36},... | collective-permute-start | bytes 638984 | tf_op jit(solution)/shard_map/ppermute | solution.py:378
  54.0 7.3 %collective-permute-start.6 = (f32[3,4,512]{2,1,0:T(4,128)S(1)}, f32[3,4,512]{2,1,0:T(4,128)S(1)}, u32[]{:S(2)}, u32[]{:S(2)}) collective-permute-start(f32[3,4,512]{2,1,0:T(4,128)S(1)} %get-tuple-element.24), channel_id=1, source_target_pairs={{0,1},{2,3},{1,0},{3,2},{4,5},{6,7},{5,4},{7,6},{8,9},{10,11},{9,8... | collective-permute-start | bytes 73736 | tf_op jit(solution)/shard_map/ppermute | solution.py:379
  54.9 6.4 %collective-permute-start.7 = (f32[3,4,512]{2,1,0:T(4,128)S(1)}, f32[3,4,512]{2,1,0:T(4,128)S(1)}, u32[]{:S(2)}, u32[]{:S(2)}) collective-permute-start(f32[3,4,512]{2,1,0:T(4,128)S(1)} %get-tuple-element.25), channel_id=1, source_target_pairs={{1,2},{2,1},{5,6},{6,5},{9,10},{10,9},{13,14},{14,13},{17,18},{18,... | collective-permute-start | bytes 73736 | tf_op jit(solution)/shard_map/ppermute | solution.py:380
  70.7 13.8 %collective-permute-start.8 = (f32[2,32,512]{2,1,0:T(8,128)S(1)}, f32[2,32,512]{2,1,0:T(8,128)S(1)}, u32[]{:S(2)}, u32[]{:S(2)}) collective-permute-start(f32[2,32,512]{2,1,0:T(8,128)S(1)} %get-tuple-element.28), channel_id=1, source_target_pairs={{4,8},{8,4},{12,16},{16,12},{20,24},{24,20},{28,32},{32,28},{36,40... | collective-permute-start | bytes 393224 | tf_op jit(solution)/shard_map/ppermute | solution.py:377
  74.0 10.5 %collective-permute-start.9 = (f32[2,32,512]{2,1,0:T(8,128)S(1)}, f32[2,32,512]{2,1,0:T(8,128)S(1)}, u32[]{:S(2)}, u32[]{:S(2)}) collective-permute-start(f32[2,32,512]{2,1,0:T(8,128)S(1)} %get-tuple-element.29), channel_id=1, source_target_pairs={{0,4},{4,0},{8,12},{12,8},{16,20},{20,16},{24,28},{28,24},{32,36},... | collective-permute-start | bytes 393224 | tf_op jit(solution)/shard_map/ppermute | solution.py:378
  74.1 6.0 %collective-permute-start.10 = (f32[2,4,512]{2,1,0:T(4,128)S(1)}, f32[2,4,512]{2,1,0:T(4,128)S(1)}, u32[]{:S(2)}, u32[]{:S(2)}) collective-permute-start(f32[2,4,512]{2,1,0:T(4,128)S(1)} %get-tuple-element.30), channel_id=1, source_target_pairs={{0,1},{2,3},{1,0},{3,2},{4,5},{6,7},{5,4},{7,6},{8,9},{10,11},{9,8... | collective-permute-start | bytes 49160 | tf_op jit(solution)/shard_map/ppermute | solution.py:379
  75.6 4.5 %collective-permute-start.11 = (f32[2,4,512]{2,1,0:T(4,128)S(1)}, f32[2,4,512]{2,1,0:T(4,128)S(1)}, u32[]{:S(2)}, u32[]{:S(2)}) collective-permute-start(f32[2,4,512]{2,1,0:T(4,128)S(1)} %get-tuple-element.31), channel_id=1, source_target_pairs={{1,2},{2,1},{5,6},{6,5},{9,10},{10,9},{13,14},{14,13},{17,18},{18,... | collective-permute-start | bytes 49160 | tf_op jit(solution)/shard_map/ppermute | solution.py:380

commit v4 on v3

--- a/solution.py
+++ b/solution.py
@@ -61,8 +61,8 @@
     return direct + shear
 
 
-UP_PLANES = (6, 7, 11)
-DOWN_PLANES = (3, 10, 11)
+UP_PLANES = (6, 7)
+DOWN_PLANES = (3,)
 UP_ROWS = (6, 8, 11, 1, 9, 4)
 DOWN_ROWS = (4, 10, 11, 0, 9, 3, 6, 7)
 
@@ -158,11 +158,9 @@
         copy.wait()
 
 
-def first_velocity(adj, buoy, far_in, near_in, first_in, second_in, v_out, far, near, first, second, v, sems):
-    prior_y, next_y = prior_next(first_in, second_in)
-    cells_x, cells_y = adj.shape[1:3]
+def step_one(adj, buoy, below, above, prior_y, next_y, v):
+    cells_x = adj.shape[1]
     last = cells_x - 1
-    below, above = below_above(far_in, near_in)
     for x in range(cells_x):
         new = velocity_plane(
             (adj[0, x], adj[1, x], adj[2, x]), courant * buoy[x],
@@ -172,8 +170,22 @@
         )
         for k in range(3):
             v[k, x] = new[k]
-    copy = pltpu.make_async_copy(v, v_out, sems.at[0])
-    copy.start()
+
+
+def faces_of(cells_y):
+    return [pl.ds(k * cells_y, cells_y) for k in range(3)], 3 * cells_y, [pl.ds(3 * cells_y + 8 + k * cells_y, cells_y) for k in range(2)]
+
+
+def first_velocity(adj, buoy, lam, mu, far_in, near_in, first_in, second_in, far, near, first, second, v, planes, sems):
+    cells_x, cells_y = adj.shape[1:3]
+    last = cells_x - 1
+    loads = [
+        pltpu.make_async_copy(source, planes.at[k], sems.at[k]) for k, source in enumerate((mu.at[last], lam.at[0], mu.at[0]))
+    ]
+    for copy in loads:
+        copy.start()
+    prior_y, next_y = prior_next(first_in, second_in)
+    step_one(adj, buoy, *below_above(far_in, near_in), prior_y, next_y, v)
     for k in range(3):
         first[k], second[k] = first_second(v[k, :, cells_y - 1, :], v[k, :, 0, :])
     own = {n: next_y[k, last : last + 1] for k, n in enumerate(DOWN_ROWS)}
@@ -184,34 +196,39 @@
     scaled_down = courant * own[9]
     sides = (adj[4, 0][0:1, :] - own[4]) + (own[8] - below_z(own[8]))
     part_down = own[1] - scaled_down * (own[6] + sides)
-    for k in range(3):
-        far[pl.ds(k * cells_y, cells_y), :], near[pl.ds(k * cells_y, cells_y), :] = far_near(v[k, last], v[k, 0])
-    at = 3 * cells_y
+    places, at, others = faces_of(cells_y)
+    for k, place in enumerate(places):
+        far[place, :], near[place, :] = far_near(v[k, last], v[k, 0])
     far[at : at + 1, :], near[at : at + 1, :] = far_near(part_up, part_down)
     far[at + 1 : at + 2, :], near[at + 1 : at + 2, :] = far_near(scaled_up, scaled_down)
-    copy.wait()
-
-
-def half(
-    adj, buoy, lam, mu, s_far, s_near, s_prior_y, s_next_y, v, v_far, v_near, v_prior_y, v_next_y,
-    v_new, stress, strain, between,
-):
+    for copy in loads:
+        copy.wait()
+    far[others[0], :], near[others[0], :] = far_near(planes[0], planes[1])
+    far[others[1], :], near[others[1], :] = far_near(jnp.zeros_like(planes[2]), planes[2])
+
+
+def half(adj, buoy, lam, mu, s_far, s_near, s_first, s_second, v_far, v_near, v_first, v_second, v, stress, strain, between):
     cells_x, cells_y = adj.shape[1:3]
     last = cells_x - 1
     s_below, s_above = below_above(s_far, s_near)
     v_below, v_above = below_above(v_far, v_near)
-    vx_m, vy_m, vz_m = (v_below(pl.ds(k * cells_y, cells_y)) for k in range(3))
-    vx_n, vy_n, vz_n = (v_above(pl.ds(k * cells_y, cells_y)) for k in range(3))
-    part, scaled = pl.ds(3 * cells_y, 1), pl.ds(3 * cells_y + 1, 1)
+    s_prior_y, s_next_y = prior_next(s_first, s_second)
+    v_prior_y, v_next_y = prior_next(v_first, v_second)
+    step_one(adj, buoy, s_below, s_above, s_prior_y, s_next_y, v)
+    places, at, others = faces_of(cells_y)
+    vx_m, vy_m, vz_m = (v_below(place) for place in places)
+    vx_n, vy_n, vz_n = (v_above(place) for place in places)
+    part, scaled = pl.ds(at, 1), pl.ds(at + 1, 1)
+    mu_prior, lam_next, mu_next = v_below(others[0]), v_above(others[0]), v_above(others[1])
     vx_corner = v_below(part) - v_below(scaled) * s_next_y[DOWN_ROWS.index(3), 0:1]
     vy_corner = v_above(part) + v_above(scaled) * s_prior_y[UP_ROWS.index(6), last : last + 1]
     exx = vx_n - v[0, last]
     trace = exx + (vy_n - below_y(vy_n, vy_corner)) + (vz_n - below_z(vz_n))
-    sxx_next = s_above(0) - courant * (s_above(1) * trace + 2.0 * s_above(2) * exx)
+    sxx_next = s_above(0) - courant * (lam_next * trace + 2.0 * mu_next * exx)
     exy = (above_y(vx_m, vx_corner) - vx_m) + (v[1, 0] - vy_m)
     exz = (above_z(vx_m) - vx_m) + (v[2, 0] - vz_m)
-    sxy_prior = s_below(0) - courant * s_below(2) * exy
-    sxz_prior = s_below(1) - courant * s_below(2) * exz
+    sxy_prior = s_below(0) - courant * mu_prior * exy
+    sxz_prior = s_below(1) - courant * mu_prior * exz
     over = v_next_y[0]
     exx = over - jnp.concatenate([vx_corner, over[:last]], axis=0)
     eyy = v_next_y[1] - v[1, :, cells_y - 1, :]
@@ -242,54 +259,66 @@
             stress[4, x], stress[4, x - 1] if x > 0 else sxz_prior, stress[5, x], syz_rows[x : x + 1],
         )
         for k in range(3):
-            v_new[k, x] = new[k]
-
-
-def middle(
-    adj, buoy, lam_in, mu_in, s_far_in, s_near_in, v_in, s_first, s_second, v_far, v_near, v_first, v_second,
-    fields, strain_out, far, near, first, second, lam, mu, s_far, s_near, v, v_new, stress, strain, load_sems, sems,
+            v[k, x] = new[k]
+
+
+def load(plans, sems):
+    copies = [pltpu.make_async_copy(source, target, sems.at[n]) for n, (source, target) in enumerate(plans)]
+    for copy in copies:
+        copy.start()
+    return copies
+
+
+def edges(
+    adj_in, buoy_in, lam_in, mu_in, s_far_in, s_near_in, s_first_in, s_second_in, v_far, v_near, v_first, v_second,
+    far, near, first, second, adj, buoy, lam, mu, s_far, s_near, s_first, s_second, v, stress, sems,
 ):
-    plans = ((lam_in, lam), (mu_in, mu), (s_far_in, s_far), (s_near_in, s_near), (v_in, v))
-    loads = [pltpu.make_async_copy(source, target, load_sems.at[n]) for n, (source, target) in enumerate(plans)]
-    for copy in loads:
-        copy.start()
+    given = (adj_in, buoy_in, lam_in, mu_in, s_far_in, s_near_in, s_first_in, s_second_in)
+    here = (adj, buoy, lam, mu, s_far, s_near, s_first, s_second)
+    for copy in load(zip(given, here), sems):
+        copy.wait()
+    half(*here, v_far, v_near, v_first, v_second, v, stress, None, lambda: None)
+    _, cells_x, cells_y, _ = v.shape
+    over, under = v[1, :, cells_y - 1, :], v[0, :, 0, :]
+    first[0], second[0] = first_second(over, under)
+    under = v[2, :, 0, :]
+    first[1], second[1] = first_second(jnp.zeros_like(under), under)
+    far[0], near[0] = far_near(v[0, cells_x - 1], v[1, 0])
+    far[1], near[1] = far_near(jnp.zeros_like(v[2, 0]), v[2, 0])
+
+
+def inner(
+    adj_in, buoy_in, lam_in, mu_in, s_far_in, s_near_in, s_first_in, s_second_in, v_far, v_near, v_first, v_second, fields, strain_out,
+    adj, buoy, lam, mu, s_far, s_near, s_first, s_second, v, stress, strain, load_sems, sems,
+):
+    given = (adj_in, buoy_in, lam_in, mu_in, s_far_in, s_near_in, s_first_in, s_second_in)
+    here = (adj, buoy, lam, mu, s_far, s_near, s_first, s_second)
+    for copy in load(zip(given, here), load_sems):
+        copy.wait()
     copies = [
         pltpu.make_async_copy(strain, strain_out, sems.at[0]),
         pltpu.make_async_copy(stress, fields.at[pl.ds(3, 6)], sems.at[1]),
-        pltpu.make_async_copy(v_new, fields.at[pl.ds(0, 3)], sems.at[2]),
+        pltpu.make_async_copy(v, fields.at[pl.ds(0, 3)], sems.at[2]),
     ]
-    for copy in loads:
-        copy.wait()
-    half(
-        adj, buoy, lam, mu, s_far, s_near, *prior_next(s_first, s_second), v, v_far, v_near, *prior_next(v_first, v_second),
-        v_new, stress, strain, lambda: [copy.start() for copy in copies[:2]],
-    )
+    half(*here, v_far, v_near, v_first, v_second, v, stress, strain, lambda: [copy.start() for copy in copies[:2]])
     copies[2].start()
-    _, cells_x, cells_y, _ = v_new.shape
-    over, under = v_new[1, :, cells_y - 1, :], v_new[0, :, 0, :]
-    first[0], second[0] = first_second(over, under)
-    under = v_new[2, :, 0, :]
-    first[1], second[1] = first_second(jnp.zeros_like(under), under)
-    far[0], near[0] = far_near(v_new[0, cells_x - 1], v_new[1, 0])
-    far[1], near[1] = far_near(jnp.zeros_like(v_new[2, 0]), v_new[2, 0])
     for copy in copies:
         copy.wait()
 
 
 def finish(
-    fields, lam_in, mu_in, strain_in, perm_in, v_far, v_near, v_first, v_second, message, out, out_grads,
-    v, stress, lam, mu, strain1, perm, strain2, forward, grads, sems,
+    fields, lam_in, mu_in, strain_in, perm_in, far, near, first, second, message, out, out_grads,
+    v, stress, lam, mu, strain1, perm, strain2, forward, grads, load_sems, sems,
 ):
-    plans = ((fields.at[pl.ds(0, 3)], v), (fields.at[pl.ds(3, 6)], stress), (lam_in, lam), (mu_in, mu), (strain_in, strain1), (perm_in, perm))
-    prior_y, next_y = prior_next(v_first, v_second)
-    copies = [pltpu.make_async_copy(source, target, sems.at[n]) for n, (source, target) in enumerate(plans)]
-    for copy in copies:
-        copy.start()
+    cells_x, cells_y, cells_z = strain1.shape[1:]
+    plans = (
+        (fields.at[pl.ds(0, 3)], v), (perm_in, perm), (fields.at[pl.ds(3, 6)], stress), (lam_in, lam), (mu_in, mu), (strain_in, strain1),
+    )
+    copies = load(plans, load_sems)
     count = perm.shape[1]
     per = message.shape[0] // count
-    cells_x, cells_y, cells_z = strain1.shape[1:]
     rows = cells_x * cells_y
-    copies[5].wait()
+    copies[1].wait()
     both = jnp.concatenate([perm[...], perm[...]], axis=1)
     r = lax.broadcasted_iota(jnp.int32, (rows, 2 * count), 0)
     k = lax.broadcasted_iota(jnp.int32, (rows, 2 * count), 1)
@@ -311,23 +340,23 @@
         table = jnp.concatenate([low, high], axis=0)
         picked = lax.dot(pick, table, preferred_element_type=F32)
         forward[c] = picked * factor[:, c : c + 1]
+    for n in (0, 2, 3, 4):
+        copies[n].wait()
     last = cells_x - 1
-    below, above = below_above(v_far, v_near)
-    for copy in copies[:4]:
-        copy.wait()
+    below, above = below_above(far, near)
+    prior_y, next_y = prior_next(first, second)
     for x in range(cells_x):
         e = strain_plane(
             v[0, x], v[0, x - 1] if x > 0 else below(0), next_y[0, x : x + 1],
             v[1, x], v[1, x + 1] if x < last else above(0), prior_y[0, x : x + 1],
             v[2, x], v[2, x + 1] if x < last else above(1), next_y[1, x : x + 1],
         )
-        s = stress_plane([stress[k, x] for k in range(6)], e, lam[x], mu[x])
+        new = stress_plane([stress[k, x] for k in range(6)], e, lam[x], mu[x])
         for k in range(6):
             strain2[k, x] = e[k]
-            stress[k, x] = s[k]
-    stress_copy = pltpu.make_async_copy(stress, out.at[pl.ds(3, 6)], sems.at[5])
-    stress_copy.start()
-    copies[4].wait()
+            stress[k, x] = new[k]
+    results = load(((stress, out.at[pl.ds(3, 6)]),), sems)
+    copies[5].wait()
     for step, strain in enumerate((strain1, strain2)):
         f = [forward[6 * step + n] for n in range(6)]
         e = [strain[n].reshape(rows, cells_z) for n in range(6)]
@@ -338,9 +367,8 @@
         grad_mu = grad_mu + e[3] * f[3] + e[4] * f[4] + e[5] * f[5]
     grads[0] = grad_lambda.reshape(cells_x, cells_y, cells_z)
     grads[1] = grad_mu.reshape(cells_x, cells_y, cells_z)
-    grads_copy = pltpu.make_async_copy(grads, out_grads, sems.at[6])
-    grads_copy.start()
-    for copy in (stress_copy, grads_copy):
+    results += load(((grads, out_grads),), sems.at[pl.ds(1, 1)])
+    for copy in results:
         copy.wait()
 
 
@@ -387,7 +415,7 @@
         return shape(count, cells_x, cells_z)
 
     sent = call(
-        prepare, 8, (planes(3), planes(3), lines(len(DOWN_ROWS)), lines(len(DOWN_ROWS))),
+        prepare, 8, (planes(2), planes(2), lines(len(DOWN_ROWS)), lines(len(DOWN_ROWS))),
         in_hbm(adjoint, buoyancy, lame_lambda, shear_mu), [ANY] * 4,
         [
             pltpu.VMEM((len(UP_ROWS) + len(DOWN_ROWS), cells_x, 8, cells_z), F32),
@@ -410,38 +438,44 @@
     message = lax.all_to_all(message.reshape(owners, per + 1, 1, 128), "gx", split_axis=0, concat_axis=0, tiled=True)
     message = message.reshape(owners * (per + 1), 128)
 
-    faces = shape(3 * cells_y + 8, cells_z)
+    faces = shape(5 * cells_y + 8, cells_z)
     strain = (6, cells_x, cells_y, cells_z)
     speeds = (3, cells_x, cells_y, cells_z)
-    v, *sent = call(
-        first_velocity, 12, (pltpu.HBM(speeds, F32), faces, faces, lines(3), lines(3)), (adjoint, buoyancy, *s_ghosts),
-        scratch=[pltpu.VMEM(speeds, F32), pltpu.SemaphoreType.DMA((1,))], out_specs=(ANY, VMEM, VMEM, VMEM, VMEM),
+
+    def rooms(*sizes):
+        return [pltpu.VMEM(size, F32) for size in sizes]
+
+    def semaphores(*counts):
+        return [pltpu.SemaphoreType.DMA((count,)) for count in counts]
+
+    whole = adjoint.shape
+    plane = buoyancy.shape[1:]
+    pair = (2, *plane)
+    ghost_rows = (len(DOWN_ROWS), cells_x, cells_z)
+    sent = call(
+        first_velocity, 12, (faces, faces, lines(3), lines(3)), (adjoint, buoyancy, *in_hbm(lame_lambda, shear_mu), *s_ghosts),
+        [VMEM] * 2 + [ANY] * 2 + [VMEM] * 4, rooms(speeds, (3, *plane)) + semaphores(3),
     )
     v_ghosts = swap(*sent)
 
-    fields, strain1, *sent = call(
-        middle, 16,
-        (pltpu.HBM(adjoint.shape, F32), pltpu.HBM(strain, F32), planes(2), planes(2), lines(2), lines(2)),
-        (adjoint, buoyancy, *in_hbm(lame_lambda, shear_mu, *s_ghosts[:2], v), *s_ghosts[2:], *v_ghosts),
-        [VMEM] * 2 + [ANY] * 5 + [VMEM] * 6,
-        [pltpu.VMEM(size, F32) for size in (speeds[1:], speeds[1:], speeds[:1] + speeds[2:], speeds[:1] + speeds[2:])]
-        + [pltpu.VMEM(size, F32) for size in (speeds, speeds, strain, strain)]
-        + [pltpu.SemaphoreType.DMA((5,)), pltpu.SemaphoreType.DMA((3,))],
-        (ANY, ANY, VMEM, VMEM, VMEM, VMEM),
-    )
-    v_ghosts = swap(*sent)
-
-    grads = (2, cells_x, cells_y, cells_z)
+    kept = in_hbm(adjoint, buoyancy, lame_lambda, shear_mu, *s_ghosts)
+    small = (buoyancy.shape, buoyancy.shape, pair, pair, ghost_rows, ghost_rows)
+    sent = call(
+        edges, 16, (planes(2), planes(2), lines(2), lines(2)), (*kept, *v_ghosts),
+        [ANY] * 8 + [VMEM] * 4, rooms(whole, buoyancy.shape, *small, speeds, strain) + semaphores(8),
+    )
+    w_ghosts = swap(*sent)
+    fields, strain1 = call(
+        inner, 24, (pltpu.HBM(whole, F32), pltpu.HBM(strain, F32)), (*kept, *v_ghosts), [ANY] * 8 + [VMEM] * 4,
+        rooms(whole, buoyancy.shape, *small, speeds, strain, strain) + semaphores(8, 3), (ANY, ANY),
+    )
+    grads = (2, *buoyancy.shape)
     adjoint_out, grads = call(
-        finish, 24, (pltpu.HBM(adjoint.shape, F32), pltpu.HBM(grads, F32)),
-        (*in_hbm(fields, lame_lambda, shear_mu, strain1, perm), *v_ghosts, message),
-        [ANY] * 5 + [VMEM] * 5,
-        [pltpu.VMEM(size, F32) for size in (speeds, strain, speeds[1:], speeds[1:], strain)]
-        + [pltpu.VMEM(perm.shape, jnp.int32)]
-        + [pltpu.VMEM(size, F32) for size in (strain, (comp, cells_x * cells_y, cells_z), grads)]
-        + [pltpu.SemaphoreType.DMA((7,))],
-        (ANY, ANY),
-        {0: 0},
+        finish, 24, (pltpu.HBM(whole, F32), pltpu.HBM(grads, F32)),
+        (*in_hbm(fields, lame_lambda, shear_mu, strain1, perm), *w_ghosts, message), [ANY] * 5 + [VMEM] * 5,
+        rooms(speeds, strain, buoyancy.shape, buoyancy.shape, strain) + [pltpu.VMEM(perm.shape, jnp.int32)]
+        + rooms(strain, (comp, cells_x * cells_y, cells_z), grads) + semaphores(6, 2),
+        (ANY, ANY), {0: 0},
     )
     return adjoint_out, grads
 

time: 89.7 us -> 89.3 us (level)
  waiting for transfers between devices: 36.9 us -> 33.4 us
  Pallas kernels: 13.7 us -> 16.8 us
    pallas_call x5 -> x6, Pallas kernels: 13.7 us -> 16.8 us  [call(): pl.pallas_call(kernel, out_shape=outs, in_specs=in_specs or [VMEM] * len(...]
    ppermute x3, waiting for transfers between devices: 21.8 us -> 19.4 us  [swap(): first = lax.ppermute(first, 'gy', pairs[0])]
    ppermute x3, waiting for transfers between devices: 15.1 us -> 13.9 us  [swap(): far = lax.ppermute(far, 'gx', off_chip)]
    ppermute x3, starting transfers between devices: 16.4 us -> 15.4 us  [swap(): far = lax.ppermute(far, 'gx', off_chip)]
    ppermute x3, starting transfers between devices: 3.46 us -> 4.4 us  [swap(): first = lax.ppermute(first, 'gy', pairs[0])]
  transfers between devices with their start and end apart: 13 -> 13, of which waited for: 6 -> 5; matrix products, arithmetic and copies ran while one was open for 0% -> 0% of each run, Pallas kernels for 8% -> 13%
where the time goes in v4:
time: 89.3 us; the launch traced here: 88.7 us
  starting transfers between devices  37 us (41%)
  waiting for transfers between devices  33.4 us (37%)
  Pallas kernels  16.8 us (19%)
    ppermute x3, waiting for transfers between devices, swap(): first = lax.ppermute(first, 'gy', pairs[0])  19.4 us
    pallas_call x6, Pallas kernels, call(): pl.pallas_call(kernel, out_shape=outs, in_specs=in_specs or [VMEM] * len(...  16.8 us
    ppermute x3, starting transfers between devices, swap(): far = lax.ppermute(far, 'gx', off_chip)  15.4 us
    all_to_all x1, starting transfers between devices, on_device(): lax.all_to_all(message.reshape(owners, per + 1, 1, 128), 'gx', split_axis...  14.9 us
    ppermute x3, waiting for transfers between devices, swap(): far = lax.ppermute(far, 'gx', off_chip)  13.9 us
    ppermute x3, starting transfers between devices, swap(): first = lax.ppermute(first, 'gy', pairs[0])  4.4 us
    ppermute x3, starting transfers between devices, swap(): second = lax.ppermute(second, 'gy', pairs[1])  1.95 us
  transfers between devices with their start and end apart: 13, of which 5 were waited for; matrix products, arithmetic and copies ran while one was open for 0% of the time, Pallas kernels for 13%

profile of v4, /device:TPU:6, one launch (start us, length us, event | category | flops | bytes accessed | tf_op | source)
XLA Modules:
  0.0 88.7 jit_solution(2393385055566806689)
XLA Ops:
  0.6 0.7 copy.13
  1.3 2.0 %shard_map.90 = s32[1600,128]{1,0:T(8,128)} custom-call(s32[1536,128]{1,0:T(8,128)} %bitcast.10, f32[12,1,64]{2,1,0:T(1,128)S(1)} %reshape.21.scales), custom_call_target="tpu_custom_call" | custom-call | tf_op jit(solution)/shard_map/pallas_call | solution.py:387
  3.3 0.0 copy-start
  3.3 0.0 copy-start.1
  3.4 14.9 %all-to-all-start = ((s32[64,25,1,128]{3,2,1,0:T(1,128)}), s32[64,25,1,128]{3,2,1,0:T(1,128)S(1)}, u32[]{:S(2)}, u32[]{:S(2)}) async-start(s32[64,25,1,128]{3,2,1,0:T(1,128)} %bitcast.9), calls=%async_computation | async-start | bytes 1638400 | tf_op jit(solution)/shard_map/all_to_all | solution.py:438
  18.3 1.5 %shard_map.86 = (f32[2,32,512]{2,1,0:T(8,128)S(1)}, f32[2,32,512]{2,1,0:T(8,128)S(1)}, f32[8,4,512]{2,1,0:T(4,128)S(1)}, f32[8,4,512]{2,1,0:T(4,128)S(1)}) custom-call(f32[9,4,32,512]{3,2,1,0:T(8,128)} %adj_in.3, f32[4,32,512]{2,1,0:T(8,128)} %buoy_in.3, f32[4,32,512]{2,1,0:T(8,128)} %lam_in.5, f32[4,32,512]{2,1,0:T(8,128)} %mu_in.5), custom_call_target="tpu_custom_call" | custom-call | tf_op jit(solution)/shard_map/pallas_call | solution.py:387
  19.8 9.4 %collective-permute-start = (f32[2,32,512]{2,1,0:T(8,128)S(1)}, f32[2,32,512]{2,1,0:T(8,128)S(1)}, u32[]{:S(2)}, u32[]{:S(2)}) collective-permute-start(f32[2,32,512]{2,1,0:T(8,128)S(1)} %get-tuple-element.16), channel_id=1, source_target_pairs={{4,8},{8,4},{12,16},{16,12},{20,24},{24,20},{28,32},{32,28},{36,40... | collective-permute-start | bytes 393224 | tf_op jit(solution)/shard_map/ppermute | solution.py:405
  29.2 0.1 collective-permute-start.1
  29.3 1.1 %collective-permute-start.2 = (f32[8,4,512]{2,1,0:T(4,128)S(1)}, f32[8,4,512]{2,1,0:T(4,128)S(1)}, u32[]{:S(2)}, u32[]{:S(2)}) collective-permute-start(f32[8,4,512]{2,1,0:T(4,128)S(1)} %get-tuple-element.18), channel_id=1, source_target_pairs={{0,1},{2,3},{1,0},{3,2},{4,5},{6,7},{5,4},{7,6},{8,9},{10,11},{9,8... | collective-permute-start | bytes 196616 | tf_op jit(solution)/shard_map/ppermute | solution.py:407
  30.4 0.7 collective-permute-start.3
  31.1 10.8 %collective-permute-done.2.first_in.s_first_in = f32[8,4,512]{2,1,0:T(4,128)S(1)} collective-permute-done((f32[8,4,512]{2,1,0:T(4,128)S(1)}, f32[8,4,512]{2,1,0:T(4,128)S(1)}, u32[]{:S(2)}, u32[]{:S(2)}) %collective-permute-start.2) | collective-permute-done | bytes 65568 | tf_op jit(solution)/shard_map/ppermute | solution.py:407
  41.9 0.0 copy-start.4
  41.9 0.0 collective-permute-done.3.second_in.s_second_in
  41.9 0.0 copy-start.5
  41.9 5.3 %collective-permute-done.far_in.s_far_in = f32[2,32,512]{2,1,0:T(8,128)S(1)} collective-permute-done((f32[2,32,512]{2,1,0:T(8,128)S(1)}, f32[2,32,512]{2,1,0:T(8,128)S(1)}, u32[]{:S(2)}, u32[]{:S(2)}) %collective-permute-start) | collective-permute-done | bytes 131104 | tf_op jit(solution)/shard_map/ppermute | solution.py:405
  47.3 0.0 copy-start.2
  47.3 0.0 collective-permute-done.1.near_in.s_near_in
  47.3 0.0 copy-done
  47.3 0.0 copy-done.1
  47.3 0.0 copy-start.3
  47.3 1.2 %shard_map.87 = (f32[168,512]{1,0:T(8,128)S(1)}, f32[168,512]{1,0:T(8,128)S(1)}, f32[3,4,512]{2,1,0:T(4,128)S(1)}, f32[3,4,512]{2,1,0:T(4,128)S(1)}) custom-call(f32[9,4,32,512]{3,2,1,0:T(8,128)S(1)} %copy-done, f32[4,32,512]{2,1,0:T(8,128)S(1)} %copy-done.1, f32[4,32,512]{2,1,0:T(8,128)} %lam_in.5, f32[4,32,512]{2,1,0:T(8,128)} %mu_in.5, ...), custom_call_target="tpu_custom_call" | custom-call | tf_op jit(solution)/shard_map/pallas_call | solution.py:387
  48.5 3.8 %collective-permute-start.4 = (f32[168,512]{1,0:T(8,128)S(1)}, f32[168,512]{1,0:T(8,128)S(1)}, u32[]{:S(2)}, u32[]{:S(2)}) collective-permute-start(f32[168,512]{1,0:T(8,128)S(1)} %get-tuple-element.20), channel_id=1, source_target_pairs={{4,8},{8,4},{12,16},{16,12},{20,24},{24,20},{28,32},{32,28},{36,40... | collective-permute-start | bytes 1032200 | tf_op jit(solution)/shard_map/ppermute | solution.py:405
  52.3 0.1 collective-permute-start.5
  52.4 0.9 collective-permute-start.6
  53.2 0.7 collective-permute-start.7
  53.9 8.6 %collective-permute-done.6.v_first = f32[3,4,512]{2,1,0:T(4,128)S(1)} collective-permute-done((f32[3,4,512]{2,1,0:T(4,128)S(1)}, f32[3,4,512]{2,1,0:T(4,128)S(1)}, u32[]{:S(2)}, u32[]{:S(2)}) %collective-permute-start.6) | collective-permute-done | bytes 24608 | tf_op jit(solution)/shard_map/ppermute | solution.py:407
  62.5 0.0 collective-permute-done.7.v_second
  62.5 5.4 %collective-permute-done.4.v_far = f32[168,512]{1,0:T(8,128)S(1)} collective-permute-done((f32[168,512]{1,0:T(8,128)S(1)}, f32[168,512]{1,0:T(8,128)S(1)}, u32[]{:S(2)}, u32[]{:S(2)}) %collective-permute-start.4) | collective-permute-done | bytes 344096 | tf_op jit(solution)/shard_map/ppermute | solution.py:405
  67.9 0.0 collective-permute-done.5.v_near
  67.9 0.0 copy-done.4
  67.9 0.0 copy-done.5
  67.9 0.0 copy-done.2
  67.9 0.0 copy-done.3
  67.9 3.3 %shard_map.89 = (f32[2,32,512]{2,1,0:T(8,128)S(1)}, f32[2,32,512]{2,1,0:T(8,128)S(1)}, f32[2,4,512]{2,1,0:T(4,128)S(1)}, f32[2,4,512]{2,1,0:T(4,128)S(1)}) custom-call(f32[9,4,32,512]{3,2,1,0:T(8,128)} %adj_in.3, f32[4,32,512]{2,1,0:T(8,128)} %buoy_in.3, f32[4,32,512]{2,1,0:T(8,128)} %lam_in.5, f32[4,32,512]{2,1,0:T(8,128)} %mu_in.5, ...), custom_call_target="tpu_custom_call" | custom-call | tf_op jit(solution)/shard_map/pallas_call | solution.py:387
  71.3 2.2 %collective-permute-start.8 = (f32[2,32,512]{2,1,0:T(8,128)S(1)}, f32[2,32,512]{2,1,0:T(8,128)S(1)}, u32[]{:S(2)}, u32[]{:S(2)}) collective-permute-start(f32[2,32,512]{2,1,0:T(8,128)S(1)} %get-tuple-element.26), channel_id=1, source_target_pairs={{4,8},{8,4},{12,16},{16,12},{20,24},{24,20},{28,32},{32,28},{36,40... | collective-permute-start | bytes 393224 | tf_op jit(solution)/shard_map/ppermute | solution.py:405
  73.5 0.1 collective-permute-start.9
  73.6 2.4 %collective-permute-start.10 = (f32[2,4,512]{2,1,0:T(4,128)S(1)}, f32[2,4,512]{2,1,0:T(4,128)S(1)}, u32[]{:S(2)}, u32[]{:S(2)}) collective-permute-start(f32[2,4,512]{2,1,0:T(4,128)S(1)} %get-tuple-element.28), channel_id=1, source_target_pairs={{0,1},{2,3},{1,0},{3,2},{4,5},{6,7},{5,4},{7,6},{8,9},{10,11},{9,8... | collective-permute-start | bytes 49160 | tf_op jit(solution)/shard_map/ppermute | solution.py:407
  76.0 0.7 collective-permute-start.11
  76.7 5.1 %shard_map.88 = (f32[9,4,32,512]{3,2,1,0:T(8,128)}, f32[6,4,32,512]{3,2,1,0:T(8,128)}) custom-call(f32[9,4,32,512]{3,2,1,0:T(8,128)} %adj_in.3, f32[4,32,512]{2,1,0:T(8,128)} %buoy_in.3, f32[4,32,512]{2,1,0:T(8,128)} %lam_in.5, f32[4,32,512]{2,1,0:T(8,128)} %mu_in.5, f32[2,32,512]{2,1,0:T(8,128)} %copy-done.2, f32[2,32,512]{2,1,0:T(8,128)} %copy-done.3, ...), custom_call_target="tpu_custom_call" | custom-call | tf_op jit(solution)/shard_map/pallas_call | solution.py:387
  81.8 0.0 collective-permute-done.10.first
  81.9 0.0 collective-permute-done.11.second
  81.9 3.2 %collective-permute-done.8.far = f32[2,32,512]{2,1,0:T(8,128)S(1)} collective-permute-done((f32[2,32,512]{2,1,0:T(8,128)S(1)}, f32[2,32,512]{2,1,0:T(8,128)S(1)}, u32[]{:S(2)}, u32[]{:S(2)}) %collective-permute-start.8) | collective-permute-done | bytes 131104 | tf_op jit(solution)/shard_map/ppermute | solution.py:405
  85.0 0.0 collective-permute-done.9.near
  85.0 0.0 all-to-all-done
  85.0 3.7 %shard_map.91 = (f32[9,4,32,512]{3,2,1,0:T(8,128)}, f32[2,4,32,512]{3,2,1,0:T(8,128)}) custom-call(f32[9,4,32,512]{3,2,1,0:T(8,128)} %get-tuple-element.24.fields, f32[4,32,512]{2,1,0:T(8,128)} %lam_in.5, f32[4,32,512]{2,1,0:T(8,128)} %mu_in.5, f32[6,4,32,512]{3,2,1,0:T(8,128)} %get-tuple-element.25.strain_in, ...), custom_call_target="tpu_custom_call", output_to_operand_aliasing={{0}: (0, {})} | custom-call | tf_op jit(solution)/shard_map/pallas_call | solution.py:387
  (1 shorter events, 0.0 us)
Async XLA Ops:
  3.3 43.9 %copy-start = (f32[9,4,32,512]{3,2,1,0:T(8,128)S(1)}, f32[9,4,32,512]{3,2,1,0:T(8,128)}, u32[]{:S(2)}) copy-start(f32[9,4,32,512]{3,2,1,0:T(8,128)} %adj_in.3) | copy-start | bytes 7077892
  3.3 43.9 %copy-start.1 = (f32[4,32,512]{2,1,0:T(8,128)S(1)}, f32[4,32,512]{2,1,0:T(8,128)}, u32[]{:S(2)}) copy-start(f32[4,32,512]{2,1,0:T(8,128)} %buoy_in.3) | copy-start | bytes 786436
  3.4 81.7 %all-to-all-start = ((s32[64,25,1,128]{3,2,1,0:T(1,128)}), s32[64,25,1,128]{3,2,1,0:T(1,128)S(1)}, u32[]{:S(2)}, u32[]{:S(2)}) async-start(s32[64,25,1,128]{3,2,1,0:T(1,128)} %bitcast.9), calls=%async_computation | async-start | bytes 1638400 | tf_op jit(solution)/shard_map/all_to_all | solution.py:438
  19.8 27.4 %collective-permute-start = (f32[2,32,512]{2,1,0:T(8,128)S(1)}, f32[2,32,512]{2,1,0:T(8,128)S(1)}, u32[]{:S(2)}, u32[]{:S(2)}) collective-permute-start(f32[2,32,512]{2,1,0:T(8,128)S(1)} %get-tuple-element.16), channel_id=1, source_target_pairs={{4,8},{8,4},{12,16},{16,12},{20,24},{24,20},{28,32},{32,28},{36,40... | collective-permute-start | bytes 393224 | tf_op jit(solution)/shard_map/ppermute | solution.py:405
  29.2 18.1 %collective-permute-start.1 = (f32[2,32,512]{2,1,0:T(8,128)S(1)}, f32[2,32,512]{2,1,0:T(8,128)S(1)}, u32[]{:S(2)}, u32[]{:S(2)}) collective-permute-start(f32[2,32,512]{2,1,0:T(8,128)S(1)} %get-tuple-element.17), channel_id=1, source_target_pairs={{0,4},{4,0},{8,12},{12,8},{16,20},{20,16},{24,28},{28,24},{32,36},... | collective-permute-start | bytes 393224 | tf_op jit(solution)/shard_map/ppermute | solution.py:406
  29.3 12.6 %collective-permute-start.2 = (f32[8,4,512]{2,1,0:T(4,128)S(1)}, f32[8,4,512]{2,1,0:T(4,128)S(1)}, u32[]{:S(2)}, u32[]{:S(2)}) collective-permute-start(f32[8,4,512]{2,1,0:T(4,128)S(1)} %get-tuple-element.18), channel_id=1, source_target_pairs={{0,1},{2,3},{1,0},{3,2},{4,5},{6,7},{5,4},{7,6},{8,9},{10,11},{9,8... | collective-permute-start | bytes 196616 | tf_op jit(solution)/shard_map/ppermute | solution.py:407
  30.4 11.5 %collective-permute-start.3 = (f32[8,4,512]{2,1,0:T(4,128)S(1)}, f32[8,4,512]{2,1,0:T(4,128)S(1)}, u32[]{:S(2)}, u32[]{:S(2)}) collective-permute-start(f32[8,4,512]{2,1,0:T(4,128)S(1)} %get-tuple-element.19), channel_id=1, source_target_pairs={{1,2},{2,1},{5,6},{6,5},{9,10},{10,9},{13,14},{14,13},{17,18},{18,... | collective-permute-start | bytes 196616 | tf_op jit(solution)/shard_map/ppermute | solution.py:408
  41.9 26.0 %copy-start.4 = (f32[8,4,512]{2,1,0:T(4,128)}, f32[8,4,512]{2,1,0:T(4,128)S(1)}, u32[]{:S(2)}) copy-start(f32[8,4,512]{2,1,0:T(4,128)S(1)} %collective-permute-done.2.first_in.s_first_in) | copy-start | bytes 196612
  41.9 26.0 %copy-start.5 = (f32[8,4,512]{2,1,0:T(4,128)}, f32[8,4,512]{2,1,0:T(4,128)S(1)}, u32[]{:S(2)}) copy-start(f32[8,4,512]{2,1,0:T(4,128)S(1)} %collective-permute-done.3.second_in.s_second_in) | copy-start | bytes 196612
  47.3 20.7 %copy-start.2 = (f32[2,32,512]{2,1,0:T(8,128)}, f32[2,32,512]{2,1,0:T(8,128)S(1)}, u32[]{:S(2)}) copy-start(f32[2,32,512]{2,1,0:T(8,128)S(1)} %collective-permute-done.far_in.s_far_in) | copy-start | bytes 393220
  47.3 20.7 %copy-start.3 = (f32[2,32,512]{2,1,0:T(8,128)}, f32[2,32,512]{2,1,0:T(8,128)S(1)}, u32[]{:S(2)}) copy-start(f32[2,32,512]{2,1,0:T(8,128)S(1)} %collective-permute-done.1.near_in.s_near_in) | copy-start | bytes 393220
  48.5 19.4 %collective-permute-start.4 = (f32[168,512]{1,0:T(8,128)S(1)}, f32[168,512]{1,0:T(8,128)S(1)}, u32[]{:S(2)}, u32[]{:S(2)}) collective-permute-start(f32[168,512]{1,0:T(8,128)S(1)} %get-tuple-element.20), channel_id=1, source_target_pairs={{4,8},{8,4},{12,16},{16,12},{20,24},{24,20},{28,32},{32,28},{36,40... | collective-permute-start | bytes 1032200 | tf_op jit(solution)/shard_map/ppermute | solution.py:405
  52.3 15.6 %collective-permute-start.5 = (f32[168,512]{1,0:T(8,128)S(1)}, f32[168,512]{1,0:T(8,128)S(1)}, u32[]{:S(2)}, u32[]{:S(2)}) collective-permute-start(f32[168,512]{1,0:T(8,128)S(1)} %get-tuple-element.21), channel_id=1, source_target_pairs={{0,4},{4,0},{8,12},{12,8},{16,20},{20,16},{24,28},{28,24},{32,36},... | collective-permute-start | bytes 1032200 | tf_op jit(solution)/shard_map/ppermute | solution.py:406
  52.4 10.1 %collective-permute-start.6 = (f32[3,4,512]{2,1,0:T(4,128)S(1)}, f32[3,4,512]{2,1,0:T(4,128)S(1)}, u32[]{:S(2)}, u32[]{:S(2)}) collective-permute-start(f32[3,4,512]{2,1,0:T(4,128)S(1)} %get-tuple-element.22), channel_id=1, source_target_pairs={{0,1},{2,3},{1,0},{3,2},{4,5},{6,7},{5,4},{7,6},{8,9},{10,11},{9,8... | collective-permute-start | bytes 73736 | tf_op jit(solution)/shard_map/ppermute | solution.py:407
  53.2 9.2 %collective-permute-start.7 = (f32[3,4,512]{2,1,0:T(4,128)S(1)}, f32[3,4,512]{2,1,0:T(4,128)S(1)}, u32[]{:S(2)}, u32[]{:S(2)}) collective-permute-start(f32[3,4,512]{2,1,0:T(4,128)S(1)} %get-tuple-element.23), channel_id=1, source_target_pairs={{1,2},{2,1},{5,6},{6,5},{9,10},{10,9},{13,14},{14,13},{17,18},{18,... | collective-permute-start | bytes 73736 | tf_op jit(solution)/shard_map/ppermute | solution.py:408
  71.3 13.7 %collective-permute-start.8 = (f32[2,32,512]{2,1,0:T(8,128)S(1)}, f32[2,32,512]{2,1,0:T(8,128)S(1)}, u32[]{:S(2)}, u32[]{:S(2)}) collective-permute-start(f32[2,32,512]{2,1,0:T(8,128)S(1)} %get-tuple-element.26), channel_id=1, source_target_pairs={{4,8},{8,4},{12,16},{16,12},{20,24},{24,20},{28,32},{32,28},{36,40... | collective-permute-start | bytes 393224 | tf_op jit(solution)/shard_map/ppermute | solution.py:405
  73.5 11.5 %collective-permute-start.9 = (f32[2,32,512]{2,1,0:T(8,128)S(1)}, f32[2,32,512]{2,1,0:T(8,128)S(1)}, u32[]{:S(2)}, u32[]{:S(2)}) collective-permute-start(f32[2,32,512]{2,1,0:T(8,128)S(1)} %get-tuple-element.27), channel_id=1, source_target_pairs={{0,4},{4,0},{8,12},{12,8},{16,20},{20,16},{24,28},{28,24},{32,36},... | collective-permute-start | bytes 393224 | tf_op jit(solution)/shard_map/ppermute | solution.py:406
  73.6 8.2 %collective-permute-start.10 = (f32[2,4,512]{2,1,0:T(4,128)S(1)}, f32[2,4,512]{2,1,0:T(4,128)S(1)}, u32[]{:S(2)}, u32[]{:S(2)}) collective-permute-start(f32[2,4,512]{2,1,0:T(4,128)S(1)} %get-tuple-element.28), channel_id=1, source_target_pairs={{0,1},{2,3},{1,0},{3,2},{4,5},{6,7},{5,4},{7,6},{8,9},{10,11},{9,8... | collective-permute-start | bytes 49160 | tf_op jit(solution)/shard_map/ppermute | solution.py:407
  76.0 5.8 %collective-permute-start.11 = (f32[2,4,512]{2,1,0:T(4,128)S(1)}, f32[2,4,512]{2,1,0:T(4,128)S(1)}, u32[]{:S(2)}, u32[]{:S(2)}) collective-permute-start(f32[2,4,512]{2,1,0:T(4,128)S(1)} %get-tuple-element.29), channel_id=1, source_target_pairs={{1,2},{2,1},{5,6},{6,5},{9,10},{10,9},{13,14},{14,13},{17,18},{18,... | collective-permute-start | bytes 49160 | tf_op jit(solution)/shard_map/ppermute | solution.py:408

commit v5 on v4

--- a/solution.py
+++ b/solution.py
@@ -61,10 +61,9 @@
     return direct + shear
 
 
-UP_PLANES = (6, 7)
-DOWN_PLANES = (3,)
-UP_ROWS = (6, 8, 11, 1, 9, 4)
-DOWN_ROWS = (4, 10, 11, 0, 9, 3, 6, 7)
+UP_ROWS = tuple((n, 1) for n in (0, 1, 2, 3, 4, 5, 6, 7, 8, 9, 11)) + ((6, 2), (8, 2))
+DOWN_ROWS = tuple((n, 1) for n in range(12)) + ((4, 2),)
+PLANES = 7
 
 
 def on_lower_core():
@@ -95,42 +94,17 @@
     return jnp.where(even, to_next, to_prior), jnp.where(even, to_prior, to_next)
 
 
-def prepare(adj, buoy, lam, mu, far, near, first, second, rows, sems, row_sems):
-    cells_x, cells_y = adj.shape[1:3]
+def prepare(adj, buoy, lam, mu, first, second, rows, sems):
+    cells_y = adj.shape[2]
     extra = (buoy, lam, mu)
-
-    def whole(n):
-        return adj.at[n] if n < 9 else extra[n - 9]
-
-    def planes(core):
-        plans = []
-        for target, names, x in ((far, DOWN_PLANES, 0), (near, UP_PLANES, cells_x - 1)) if core == 0 else ((far, UP_PLANES, cells_x - 1), (near, DOWN_PLANES, 0)):
-            plans += [(whole(n).at[x], target.at[k]) for k, n in enumerate(names)]
-        return [pltpu.make_async_copy(source, target, sems.at[k]) for k, (source, target) in enumerate(plans)]
-
-    def both(verb):
-        lower = on_lower_core()
-        for core in range(2):
-
-            @pl.when(lower == (core == 0))
-            def _():
-                for copy in planes(core):
-                    getattr(copy, verb)()
-
-    both("start")
-    plans = [(n, cells_y - 8) for n in UP_ROWS] + [(n, 0) for n in DOWN_ROWS]
-    copies = [
-        pltpu.make_async_copy(whole(n).at[:, pl.ds(start, 8)], rows.at[k], row_sems.at[k]) for k, (n, start) in enumerate(plans)
-    ]
-    for copy in copies:
-        copy.start()
-    for copy in copies:
-        copy.wait()
-    for k in range(len(DOWN_ROWS)):
-        down = rows[len(UP_ROWS) + k, :, 0, :]
-        up = rows[k, :, 7, :] if k < len(UP_ROWS) else jnp.zeros_like(down)
-        first[k], second[k] = first_second(up, down)
-    both("wait")
+    plans = []
+    for side, start in enumerate((cells_y - 8, 0)):
+        plans.append((adj.at[:, :, pl.ds(start, 8)], rows.at[side, pl.ds(0, 9)]))
+        plans += [(extra[n].at[:, pl.ds(start, 8)], rows.at[side, 9 + n]) for n in range(3)]
+    for copy in load(plans, sems):
+        copy.wait()
+    for k, ((up, up_depth), (down, down_depth)) in enumerate(zip(UP_ROWS, DOWN_ROWS)):
+        first[k], second[k] = first_second(rows[0, up, :, 8 - up_depth, :], rows[1, down, :, down_depth - 1, :])
 
 
 def merge(packed, scales, message, words, build, word_sems, sems):
@@ -158,92 +132,116 @@
         copy.wait()
 
 
-def step_one(adj, buoy, below, above, prior_y, next_y, v):
-    cells_x = adj.shape[1]
+def load(plans, sems):
+    copies = [pltpu.make_async_copy(source, target, sems.at[n]) for n, (source, target) in enumerate(plans)]
+    for copy in copies:
+        copy.start()
+    return copies
+
+
+def step_one(adj, buoy, x, sxx_next, sxy_prior, sxz_prior, prior_y, next_y):
+    row = slice(x, x + 1)
+    return velocity_plane(
+        (adj[0, x], adj[1, x], adj[2, x]), courant * buoy[x], adj[3, x], sxx_next, adj[4, x], next_y[4, 1][row], adj[5, x],
+        adj[6, x], sxy_prior, prior_y[6, 1][row], adj[7, x], sxz_prior, adj[8, x], prior_y[8, 1][row],
+    )
+
+
+def named_rows(first, second):
+    prior_y, next_y = prior_next(first, second)
+    return {name: prior_y[k] for k, name in enumerate(UP_ROWS)}, {name: next_y[k] for k, name in enumerate(DOWN_ROWS)}
+
+
+def places(cells_y):
+    return [pl.ds(k * cells_y, cells_y) for k in range(PLANES)], [pl.ds(PLANES * cells_y + k, 1) for k in range(6)]
+
+
+def reach(adj, buoy, lam, mu, first, second, far, near, planes, sems):
+    cells_x, cells_y = adj.shape[1:3]
     last = cells_x - 1
+    loads = load(((mu.at[last], planes.at[0]), (lam.at[0], planes.at[1]), (mu.at[0], planes.at[2])), sems)
+    prior_y, next_y = named_rows(first, second)
+    blank = jnp.zeros_like(adj[0, 0])
+    up = [*step_one(adj, buoy, last, blank, adj[6, last - 1], adj[7, last - 1], prior_y, next_y), buoy[last], adj[6, last], adj[7, last]]
+    down = [*step_one(adj, buoy, 0, adj[3, 1], blank, blank, prior_y, next_y), buoy[0], adj[3, 0]]
+    own = {n: next_y[n, 1][last:] for n in range(10)}
+    scaled_up = courant * own[9]
+    sides = (own[6] - adj[6, last][cells_y - 1 :, :]) + (own[7] - below_z(own[7]))
+    up_rows = [own[0] - scaled_up * (sides - own[3]), scaled_up]
+    up_rows += [rows[n, 1][last:] for rows in (prior_y, next_y) for n in (6, 7)]
+    own = {n: prior_y[n, 1][0:1] for n in range(10)}
+    scaled_down = courant * own[9]
+    sides = (adj[4, 0][0:1, :] - own[4]) + (own[8] - below_z(own[8]))
+    down_rows = [own[1] - scaled_down * (own[6] + sides), scaled_down, own[3], next_y[3, 1][0:1]]
+    down_rows += [jnp.zeros_like(scaled_down)] * 2
+    whole, lines = places(cells_y)
+    for copy in loads:
+        copy.wait()
+    up.append(planes[0])
+    down += [planes[1], planes[2]]
+    for place, a, b in zip(whole + lines, up + up_rows, down + down_rows):
+        far[place, :], near[place, :] = far_near(a, b)
+
+
+def half(adj, buoy, lam, mu, far, near, first, second, v, stress, strain, between):
+    cells_x, cells_y = adj.shape[1:3]
+    last = cells_x - 1
+    from_below, from_above = below_above(far, near)
+    prior_y, next_y = named_rows(first, second)
+    whole, lines = places(cells_y)
+    vx_m, vy_m, vz_m, buoy_m, sxy_m, sxz_m, mu_m = (from_below(place) for place in whole)
+    vx_n, vy_n, vz_n, buoy_n, sxx_n, lam_n, mu_n = (from_above(place) for place in whole)
+    vx_m = vx_m - courant * buoy_m * adj[3, 0]
+    vy_n = vy_n + courant * buoy_n * adj[6, last]
+    vz_n = vz_n + courant * buoy_n * adj[7, last]
     for x in range(cells_x):
-        new = velocity_plane(
-            (adj[0, x], adj[1, x], adj[2, x]), courant * buoy[x],
-            adj[3, x], adj[3, x + 1] if x < last else above(0), adj[4, x], next_y[0, x : x + 1], adj[5, x],
-            adj[6, x], adj[6, x - 1] if x > 0 else below(0), prior_y[0, x : x + 1],
-            adj[7, x], adj[7, x - 1] if x > 0 else below(1), adj[8, x], prior_y[1, x : x + 1],
+        new = step_one(
+            adj, buoy, x, adj[3, x + 1] if x < last else sxx_n, adj[6, x - 1] if x > 0 else sxy_m, adj[7, x - 1] if x > 0 else sxz_m,
+            prior_y, next_y,
         )
         for k in range(3):
             v[k, x] = new[k]
-
-
-def faces_of(cells_y):
-    return [pl.ds(k * cells_y, cells_y) for k in range(3)], 3 * cells_y, [pl.ds(3 * cells_y + 8 + k * cells_y, cells_y) for k in range(2)]
-
-
-def first_velocity(adj, buoy, lam, mu, far_in, near_in, first_in, second_in, far, near, first, second, v, planes, sems):
-    cells_x, cells_y = adj.shape[1:3]
-    last = cells_x - 1
-    loads = [
-        pltpu.make_async_copy(source, planes.at[k], sems.at[k]) for k, source in enumerate((mu.at[last], lam.at[0], mu.at[0]))
-    ]
-    for copy in loads:
-        copy.start()
-    prior_y, next_y = prior_next(first_in, second_in)
-    step_one(adj, buoy, *below_above(far_in, near_in), prior_y, next_y, v)
-    for k in range(3):
-        first[k], second[k] = first_second(v[k, :, cells_y - 1, :], v[k, :, 0, :])
-    own = {n: next_y[k, last : last + 1] for k, n in enumerate(DOWN_ROWS)}
-    scaled_up = courant * own[9]
-    sides = (own[6] - adj[6, last][cells_y - 1 :, :]) + (own[7] - below_z(own[7]))
-    part_up = own[0] - scaled_up * (sides - own[3])
-    own = {n: prior_y[k, 0:1] for k, n in enumerate(UP_ROWS)}
-    scaled_down = courant * own[9]
-    sides = (adj[4, 0][0:1, :] - own[4]) + (own[8] - below_z(own[8]))
-    part_down = own[1] - scaled_down * (own[6] + sides)
-    places, at, others = faces_of(cells_y)
-    for k, place in enumerate(places):
-        far[place, :], near[place, :] = far_near(v[k, last], v[k, 0])
-    far[at : at + 1, :], near[at : at + 1, :] = far_near(part_up, part_down)
-    far[at + 1 : at + 2, :], near[at + 1 : at + 2, :] = far_near(scaled_up, scaled_down)
-    for copy in loads:
-        copy.wait()
-    far[others[0], :], near[others[0], :] = far_near(planes[0], planes[1])
-    far[others[1], :], near[others[1], :] = far_near(jnp.zeros_like(planes[2]), planes[2])
-
-
-def half(adj, buoy, lam, mu, s_far, s_near, s_first, s_second, v_far, v_near, v_first, v_second, v, stress, strain, between):
-    cells_x, cells_y = adj.shape[1:3]
-    last = cells_x - 1
-    s_below, s_above = below_above(s_far, s_near)
-    v_below, v_above = below_above(v_far, v_near)
-    s_prior_y, s_next_y = prior_next(s_first, s_second)
-    v_prior_y, v_next_y = prior_next(v_first, v_second)
-    step_one(adj, buoy, s_below, s_above, s_prior_y, s_next_y, v)
-    places, at, others = faces_of(cells_y)
-    vx_m, vy_m, vz_m = (v_below(place) for place in places)
-    vx_n, vy_n, vz_n = (v_above(place) for place in places)
-    part, scaled = pl.ds(at, 1), pl.ds(at + 1, 1)
-    mu_prior, lam_next, mu_next = v_below(others[0]), v_above(others[0]), v_above(others[1])
-    vx_corner = v_below(part) - v_below(scaled) * s_next_y[DOWN_ROWS.index(3), 0:1]
-    vy_corner = v_above(part) + v_above(scaled) * s_prior_y[UP_ROWS.index(6), last : last + 1]
+    vx_corner = from_below(lines[0]) - from_below(lines[1]) * next_y[3, 1][0:1]
+    vy_corner = from_above(lines[0]) + from_above(lines[1]) * prior_y[6, 1][last:]
+    ghosts = []
+    for side, here in enumerate((prior_y, next_y)):
+        scaled = courant * here[9, 1]
+        sxx, syy, szz, sxy, sxz, syz = (here[n, 1] for n in range(3, 9))
+        sxx_after = jnp.concatenate([sxx[1:], from_above(lines[2 + side])], axis=0)
+        sxy_before = jnp.concatenate([from_below(lines[2 + 2 * side]), sxy[:last]], axis=0)
+        sxz_before = jnp.concatenate([from_below(lines[3 + 2 * side]), sxz[:last]], axis=0)
+        if side == 0:
+            sxy_under, syz_under, syy_over = here[6, 2], here[8, 2], adj[4, :, 0, :]
+        else:
+            sxy_under, syz_under, syy_over = adj[6, :, cells_y - 1, :], adj[8, :, cells_y - 1, :], here[4, 2]
+        ghosts.append([
+            here[0, 1] - scaled * (sxx_after - sxx + (sxy - sxy_under) + (sxz - below_z(sxz))),
+            here[1, 1] - scaled * (sxy - sxy_before + (syy_over - syy) + (syz - below_z(syz))),
+            here[2, 1] - scaled * (sxz - sxz_before + (syz - syz_under) + (above_z(szz) - szz)),
+        ])
+    v_prior_y, v_next_y = ghosts
     exx = vx_n - v[0, last]
     trace = exx + (vy_n - below_y(vy_n, vy_corner)) + (vz_n - below_z(vz_n))
-    sxx_next = s_above(0) - courant * (lam_next * trace + 2.0 * mu_next * exx)
+    sxx_next = sxx_n - courant * (lam_n * trace + 2.0 * mu_n * exx)
     exy = (above_y(vx_m, vx_corner) - vx_m) + (v[1, 0] - vy_m)
     exz = (above_z(vx_m) - vx_m) + (v[2, 0] - vz_m)
-    sxy_prior = s_below(0) - courant * mu_prior * exy
-    sxz_prior = s_below(1) - courant * mu_prior * exz
+    sxy_prior = sxy_m - courant * mu_m * exy
+    sxz_prior = sxz_m - courant * mu_m * exz
     over = v_next_y[0]
     exx = over - jnp.concatenate([vx_corner, over[:last]], axis=0)
     eyy = v_next_y[1] - v[1, :, cells_y - 1, :]
     trace = exx + eyy + (v_next_y[2] - below_z(v_next_y[2]))
-    syy_rows = s_next_y[0] - courant * (s_next_y[1] * trace + 2.0 * s_next_y[2] * eyy)
+    syy_rows = next_y[4, 1] - courant * (next_y[10, 1] * trace + 2.0 * next_y[11, 1] * eyy)
     under = v_prior_y[1]
     exy = (v[0, :, 0, :] - v_prior_y[0]) + (jnp.concatenate([under[1:], vy_corner], axis=0) - under)
     eyz = (above_z(under) - under) + (v[2, :, 0, :] - v_prior_y[2])
-    sxy_rows = s_prior_y[0] - courant * s_prior_y[2] * exy
-    syz_rows = s_prior_y[1] - courant * s_prior_y[2] * eyz
+    sxy_rows = prior_y[6, 1] - courant * prior_y[11, 1] * exy
+    syz_rows = prior_y[8, 1] - courant * prior_y[11, 1] * eyz
     for x in range(cells_x):
         e = strain_plane(
-            v[0, x], v[0, x - 1] if x > 0 else vx_m, v_next_y[0, x : x + 1],
-            v[1, x], v[1, x + 1] if x < last else vy_n, v_prior_y[1, x : x + 1],
-            v[2, x], v[2, x + 1] if x < last else vz_n, v_next_y[2, x : x + 1],
+            v[0, x], v[0, x - 1] if x > 0 else vx_m, v_next_y[0][x : x + 1],
+            v[1, x], v[1, x + 1] if x < last else vy_n, v_prior_y[1][x : x + 1],
+            v[2, x], v[2, x + 1] if x < last else vz_n, v_next_y[2][x : x + 1],
         )
         s = stress_plane([adj[3 + k, x] for k in range(6)], e, lam[x], mu[x])
         for k in range(6):
@@ -262,22 +260,15 @@
             v[k, x] = new[k]
 
 
-def load(plans, sems):
-    copies = [pltpu.make_async_copy(source, target, sems.at[n]) for n, (source, target) in enumerate(plans)]
-    for copy in copies:
-        copy.start()
-    return copies
-
-
 def edges(
-    adj_in, buoy_in, lam_in, mu_in, s_far_in, s_near_in, s_first_in, s_second_in, v_far, v_near, v_first, v_second,
-    far, near, first, second, adj, buoy, lam, mu, s_far, s_near, s_first, s_second, v, stress, sems,
+    adj_in, buoy_in, lam_in, mu_in, far_in, near_in, first_in, second_in, far, near, first, second,
+    adj, buoy, lam, mu, far_here, near_here, first_here, second_here, v, stress, sems,
 ):
-    given = (adj_in, buoy_in, lam_in, mu_in, s_far_in, s_near_in, s_first_in, s_second_in)
-    here = (adj, buoy, lam, mu, s_far, s_near, s_first, s_second)
+    given = (adj_in, buoy_in, lam_in, mu_in, far_in, near_in, first_in, second_in)
+    here = (adj, buoy, lam, mu, far_here, near_here, first_here, second_here)
     for copy in load(zip(given, here), sems):
         copy.wait()
-    half(*here, v_far, v_near, v_first, v_second, v, stress, None, lambda: None)
+    half(*here, v, stress, None, lambda: None)
     _, cells_x, cells_y, _ = v.shape
     over, under = v[1, :, cells_y - 1, :], v[0, :, 0, :]
     first[0], second[0] = first_second(over, under)
@@ -288,11 +279,11 @@
 
 
 def inner(
-    adj_in, buoy_in, lam_in, mu_in, s_far_in, s_near_in, s_first_in, s_second_in, v_far, v_near, v_first, v_second, fields, strain_out,
-    adj, buoy, lam, mu, s_far, s_near, s_first, s_second, v, stress, strain, load_sems, sems,
+    adj_in, buoy_in, lam_in, mu_in, far_in, near_in, first_in, second_in, fields, strain_out,
+    adj, buoy, lam, mu, far, near, first, second, v, stress, strain, load_sems, sems,
 ):
-    given = (adj_in, buoy_in, lam_in, mu_in, s_far_in, s_near_in, s_first_in, s_second_in)
-    here = (adj, buoy, lam, mu, s_far, s_near, s_first, s_second)
+    given = (adj_in, buoy_in, lam_in, mu_in, far_in, near_in, first_in, second_in)
+    here = (adj, buoy, lam, mu, far, near, first, second)
     for copy in load(zip(given, here), load_sems):
         copy.wait()
     copies = [
@@ -300,7 +291,7 @@
         pltpu.make_async_copy(stress, fields.at[pl.ds(3, 6)], sems.at[1]),
         pltpu.make_async_copy(v, fields.at[pl.ds(0, 3)], sems.at[2]),
     ]
-    half(*here, v_far, v_near, v_first, v_second, v, stress, strain, lambda: [copy.start() for copy in copies[:2]])
+    half(*here, v, stress, strain, lambda: [copy.start() for copy in copies[:2]])
     copies[2].start()
     for copy in copies:
         copy.wait()
@@ -401,29 +392,24 @@
     pairs = [[(y, y + 1) for y in range(start, count_y - 1, 2)] for start in (0, 1)]
     pairs = [[*there, *((b, a) for a, b in there)] for there in pairs]
 
-    def swap(far, near, first, second):
-        far = lax.ppermute(far, "gx", off_chip)
-        near = lax.ppermute(near, "gx", on_chip)
-        first = lax.ppermute(first, "gy", pairs[0])
-        second = lax.ppermute(second, "gy", pairs[1])
-        return far, near, first, second
-
     def planes(*count):
         return shape(*count, cells_y, cells_z)
 
     def lines(count):
         return shape(count, cells_x, cells_z)
 
-    sent = call(
-        prepare, 8, (planes(2), planes(2), lines(len(DOWN_ROWS)), lines(len(DOWN_ROWS))),
-        in_hbm(adjoint, buoyancy, lame_lambda, shear_mu), [ANY] * 4,
-        [
-            pltpu.VMEM((len(UP_ROWS) + len(DOWN_ROWS), cells_x, 8, cells_z), F32),
-            pltpu.SemaphoreType.DMA((6,)),
-            pltpu.SemaphoreType.DMA((len(UP_ROWS) + len(DOWN_ROWS),)),
-        ],
-    )
-    s_ghosts = swap(*sent)
+    def rooms(*sizes):
+        return [pltpu.VMEM(size, F32) for size in sizes]
+
+    def semaphores(*counts):
+        return [pltpu.SemaphoreType.DMA((count,)) for count in counts]
+
+    raw = in_hbm(adjoint, buoyancy, lame_lambda, shear_mu)
+    first, second = call(
+        prepare, 8, (lines(len(UP_ROWS)), lines(len(UP_ROWS))), raw, [ANY] * 4, rooms((2, 12, cells_x, 8, cells_z)) + semaphores(8)
+    )
+    first = lax.ppermute(first, "gy", pairs[0])
+    second = lax.ppermute(second, "gy", pairs[1])
 
     by_comp = jnp.transpose(scales.reshape(owners, comp)).reshape(comp, 1, owners)
     size = (owners * (per + 1), 128)
@@ -438,36 +424,31 @@
     message = lax.all_to_all(message.reshape(owners, per + 1, 1, 128), "gx", split_axis=0, concat_axis=0, tiled=True)
     message = message.reshape(owners * (per + 1), 128)
 
-    faces = shape(5 * cells_y + 8, cells_z)
-    strain = (6, cells_x, cells_y, cells_z)
-    speeds = (3, cells_x, cells_y, cells_z)
-
-    def rooms(*sizes):
-        return [pltpu.VMEM(size, F32) for size in sizes]
-
-    def semaphores(*counts):
-        return [pltpu.SemaphoreType.DMA((count,)) for count in counts]
-
     whole = adjoint.shape
-    plane = buoyancy.shape[1:]
-    pair = (2, *plane)
-    ghost_rows = (len(DOWN_ROWS), cells_x, cells_z)
-    sent = call(
-        first_velocity, 12, (faces, faces, lines(3), lines(3)), (adjoint, buoyancy, *in_hbm(lame_lambda, shear_mu), *s_ghosts),
-        [VMEM] * 2 + [ANY] * 2 + [VMEM] * 4, rooms(speeds, (3, *plane)) + semaphores(3),
-    )
-    v_ghosts = swap(*sent)
-
-    kept = in_hbm(adjoint, buoyancy, lame_lambda, shear_mu, *s_ghosts)
-    small = (buoyancy.shape, buoyancy.shape, pair, pair, ghost_rows, ghost_rows)
-    sent = call(
-        edges, 16, (planes(2), planes(2), lines(2), lines(2)), (*kept, *v_ghosts),
-        [ANY] * 8 + [VMEM] * 4, rooms(whole, buoyancy.shape, *small, speeds, strain) + semaphores(8),
-    )
-    w_ghosts = swap(*sent)
+    strain = (6, *buoyancy.shape)
+    speeds = (3, *buoyancy.shape)
+    message_rows = (PLANES * cells_y + 8, cells_z)
+    faces = shape(*message_rows)
+    far, near = call(
+        reach, 12, (faces, faces), (adjoint, buoyancy, *raw[2:], first, second), [VMEM] * 2 + [ANY] * 2 + [VMEM] * 2,
+        rooms((3, cells_y, cells_z)) + semaphores(3),
+    )
+    far = lax.ppermute(far, "gx", off_chip)
+    near = lax.ppermute(near, "gx", on_chip)
+
+    given = (*raw, *in_hbm(far, near, first, second))
+    line_rows = (len(UP_ROWS), cells_x, cells_z)
+    here = (whole, *[buoyancy.shape] * 3, message_rows, message_rows, line_rows, line_rows)
+    far, near, first, second = call(
+        edges, 16, (planes(2), planes(2), lines(2), lines(2)), given, [ANY] * 8, rooms(*here, speeds, strain) + semaphores(8)
+    )
+    w_ghosts = (
+        lax.ppermute(far, "gx", off_chip), lax.ppermute(near, "gx", on_chip),
+        lax.ppermute(first, "gy", pairs[0]), lax.ppermute(second, "gy", pairs[1]),
+    )
     fields, strain1 = call(
-        inner, 24, (pltpu.HBM(whole, F32), pltpu.HBM(strain, F32)), (*kept, *v_ghosts), [ANY] * 8 + [VMEM] * 4,
-        rooms(whole, buoyancy.shape, *small, speeds, strain, strain) + semaphores(8, 3), (ANY, ANY),
+        inner, 24, (pltpu.HBM(whole, F32), pltpu.HBM(strain, F32)), given, [ANY] * 8,
+        rooms(*here, speeds, strain, strain) + semaphores(8, 3), (ANY, ANY),
     )
     grads = (2, *buoyancy.shape)
     adjoint_out, grads = call(

time: 89.3 us -> 89.2 us (level)
  the two profiles are of different devices: /device:TPU:6 before, /device:TPU:70 now
where the time goes in v5:
time: 89.2 us; the launch traced here: 87.5 us
  starting transfers between devices  40.8 us (46%)
  waiting for transfers between devices  26.4 us (30%)
  Pallas kernels  17.2 us (19%)
  local copies, waits for them, and re-layouts  2.26 us (3%)
    pallas_call x6, Pallas kernels, call(): pl.pallas_call(kernel, out_shape=outs, in_specs=in_specs or [VMEM] * len(...  17.2 us
    ppermute x1, waiting for transfers between devices, on_device(): first = lax.ppermute(first, 'gy', pairs[0])  14.7 us
    all_to_all x1, starting transfers between devices, on_device(): lax.all_to_all(message.reshape(owners, per + 1, 1, 128), 'gx', split_axis...  13.1 us
    ppermute x1, waiting for transfers between devices, on_device(): far = lax.ppermute(far, 'gx', off_chip)  11.7 us
    ppermute x1, starting transfers between devices, on_device(): far = lax.ppermute(far, 'gx', off_chip)  10.3 us
    ppermute x1, starting transfers between devices, on_device(): lax.ppermute(far, 'gx', off_chip)  10.2 us
    ppermute x1, starting transfers between devices, on_device(): lax.ppermute(second, 'gy', pairs[1])  2.92 us
    ppermute x1, starting transfers between devices, on_device(): second = lax.ppermute(second, 'gy', pairs[1])  2.89 us
  transfers between devices with their start and end apart: 9, of which 2 were waited for; matrix products, arithmetic and copies ran while one was open for 0% of the time, Pallas kernels for 13%

profile of v5, /device:TPU:70, one launch (start us, length us, event | category | flops | bytes accessed | tf_op | source)
XLA Modules:
  0.0 87.5 jit_solution(12428501667366259786)
XLA Ops:
  0.6 0.7 copy.13
  1.3 2.0 %shard_map.90 = s32[1600,128]{1,0:T(8,128)} custom-call(s32[1536,128]{1,0:T(8,128)} %bitcast.10, f32[12,1,64]{2,1,0:T(1,128)S(1)} %reshape.21.scales), custom_call_target="tpu_custom_call" | custom-call | tf_op jit(solution)/shard_map/pallas_call | solution.py:378
  3.3 0.0 copy-start
  3.4 0.0 copy-start.1
  3.4 13.1 %all-to-all-start = ((s32[64,25,1,128]{3,2,1,0:T(1,128)}), s32[64,25,1,128]{3,2,1,0:T(1,128)S(1)}, u32[]{:S(2)}, u32[]{:S(2)}) async-start(s32[64,25,1,128]{3,2,1,0:T(1,128)} %bitcast.9), calls=%async_computation | async-start | bytes 1638400 | tf_op jit(solution)/shard_map/all_to_all | solution.py:424
  16.5 1.4 %shard_map.86 = (f32[13,4,512]{2,1,0:T(4,128)S(1)}, f32[13,4,512]{2,1,0:T(4,128)S(1)}) custom-call(f32[9,4,32,512]{3,2,1,0:T(8,128)} %adj_in.3, f32[4,32,512]{2,1,0:T(8,128)} %buoy_in.3, f32[4,32,512]{2,1,0:T(8,128)} %lam_in.5, f32[4,32,512]{2,1,0:T(8,128)} %mu_in.5), custom_call_target="tpu_custom_call" | custom-call | tf_op jit(solution)/shard_map/pallas_call | solution.py:378
  18.0 1.1 %collective-permute-start = (f32[13,4,512]{2,1,0:T(4,128)S(1)}, f32[13,4,512]{2,1,0:T(4,128)S(1)}, u32[]{:S(2)}, u32[]{:S(2)}) collective-permute-start(f32[13,4,512]{2,1,0:T(4,128)S(1)} %get-tuple-element.12), channel_id=1, source_target_pairs={{0,1},{2,3},{1,0},{3,2},{4,5},{6,7},{5,4},{7,6},{8,9},{10,11},{9,8... | collective-permute-start | bytes 319496 | tf_op jit(solution)/shard_map/ppermute | solution.py:411
  19.1 2.9 %collective-permute-start.1 = (f32[13,4,512]{2,1,0:T(4,128)S(1)}, f32[13,4,512]{2,1,0:T(4,128)S(1)}, u32[]{:S(2)}, u32[]{:S(2)}) collective-permute-start(f32[13,4,512]{2,1,0:T(4,128)S(1)} %get-tuple-element.13), channel_id=1, source_target_pairs={{1,2},{2,1},{5,6},{6,5},{9,10},{10,9},{13,14},{14,13},{17,18},{18,... | collective-permute-start | bytes 319496 | tf_op jit(solution)/shard_map/ppermute | solution.py:412
  22.0 14.7 %collective-permute-done.first.first_in = f32[13,4,512]{2,1,0:T(4,128)S(1)} collective-permute-done((f32[13,4,512]{2,1,0:T(4,128)S(1)}, f32[13,4,512]{2,1,0:T(4,128)S(1)}, u32[]{:S(2)}, u32[]{:S(2)}) %collective-permute-start) | collective-permute-done | bytes 106528 | tf_op jit(solution)/shard_map/ppermute | solution.py:411
  36.7 0.0 copy-start.2
  36.7 0.0 collective-permute-done.1.second.second_in
  36.7 0.0 copy-done
  36.7 0.0 copy-done.1
  36.7 0.0 copy-start.3
  36.7 1.1 %shard_map.87 = (f32[232,512]{1,0:T(8,128)S(1)}, f32[232,512]{1,0:T(8,128)S(1)}) custom-call(f32[9,4,32,512]{3,2,1,0:T(8,128)S(1)} %copy-done, f32[4,32,512]{2,1,0:T(8,128)S(1)} %copy-done.1, f32[4,32,512]{2,1,0:T(8,128)} %lam_in.5, f32[4,32,512]{2,1,0:T(8,128)} %mu_in.5, f32[13,4,512]{2,1,0:T(4,128)S(1)} %collective-permute-done.first.first_in, ...), custom_call_target="tpu_custom_call" | custom-call | tf_op jit(solution)/shard_map/pallas_call | solution.py:378
  37.9 10.3 %collective-permute-start.2 = (f32[232,512]{1,0:T(8,128)S(1)}, f32[232,512]{1,0:T(8,128)S(1)}, u32[]{:S(2)}, u32[]{:S(2)}) collective-permute-start(f32[232,512]{1,0:T(8,128)S(1)} %get-tuple-element.14), channel_id=1, source_target_pairs={{4,8},{8,4},{12,16},{16,12},{20,24},{24,20},{28,32},{32,28},{36,40... | collective-permute-start | bytes 1425416 | tf_op jit(solution)/shard_map/ppermute | solution.py:436
  48.2 0.1 collective-permute-start.3
  48.3 11.7 %collective-permute-done.2.far_in = f32[232,512]{1,0:T(8,128)S(1)} collective-permute-done((f32[232,512]{1,0:T(8,128)S(1)}, f32[232,512]{1,0:T(8,128)S(1)}, u32[]{:S(2)}, u32[]{:S(2)}) %collective-permute-start.2) | collective-permute-done | bytes 475168 | tf_op jit(solution)/shard_map/ppermute | solution.py:436
  60.0 0.0 copy-start.4
  60.0 0.0 collective-permute-done.3.near_in
  60.0 0.0 copy-done.2
  60.0 0.0 copy-done.3
  60.0 0.8 copy-done.4
  60.7 0.0 copy-start.5
  60.7 0.8 copy-done.5
  61.5 3.6 %shard_map.89 = (f32[2,32,512]{2,1,0:T(8,128)S(1)}, f32[2,32,512]{2,1,0:T(8,128)S(1)}, f32[2,4,512]{2,1,0:T(4,128)S(1)}, f32[2,4,512]{2,1,0:T(4,128)S(1)}) custom-call(f32[9,4,32,512]{3,2,1,0:T(8,128)} %adj_in.3, f32[4,32,512]{2,1,0:T(8,128)} %buoy_in.3, f32[4,32,512]{2,1,0:T(8,128)} %lam_in.5, f32[4,32,512]{2,1,0:T(8,128)} %mu_in.5, f32[232,512]{1,0:T(8,128)} %copy-done.4, ...), custom_call_target="tpu_custom_call" | custom-call | tf_op jit(solution)/shard_map/pallas_call | solution.py:378
  65.2 10.2 %collective-permute-start.4 = (f32[2,32,512]{2,1,0:T(8,128)S(1)}, f32[2,32,512]{2,1,0:T(8,128)S(1)}, u32[]{:S(2)}, u32[]{:S(2)}) collective-permute-start(f32[2,32,512]{2,1,0:T(8,128)S(1)} %get-tuple-element.18), channel_id=1, source_target_pairs={{4,8},{8,4},{12,16},{16,12},{20,24},{24,20},{28,32},{32,28},{36,40... | collective-permute-start | bytes 393224 | tf_op jit(solution)/shard_map/ppermute | solution.py:446
  75.4 0.1 collective-permute-start.5
  75.5 0.1 collective-permute-start.6
  75.6 2.9 %collective-permute-start.7 = (f32[2,4,512]{2,1,0:T(4,128)S(1)}, f32[2,4,512]{2,1,0:T(4,128)S(1)}, u32[]{:S(2)}, u32[]{:S(2)}) collective-permute-start(f32[2,4,512]{2,1,0:T(4,128)S(1)} %get-tuple-element.21), channel_id=1, source_target_pairs={{1,2},{2,1},{5,6},{6,5},{9,10},{10,9},{13,14},{14,13},{17,18},{18,... | collective-permute-start | bytes 49160 | tf_op jit(solution)/shard_map/ppermute | solution.py:447
  78.5 5.3 %shard_map.88 = (f32[9,4,32,512]{3,2,1,0:T(8,128)}, f32[6,4,32,512]{3,2,1,0:T(8,128)}) custom-call(f32[9,4,32,512]{3,2,1,0:T(8,128)} %adj_in.3, f32[4,32,512]{2,1,0:T(8,128)} %buoy_in.3, f32[4,32,512]{2,1,0:T(8,128)} %lam_in.5, f32[4,32,512]{2,1,0:T(8,128)} %mu_in.5, f32[232,512]{1,0:T(8,128)} %copy-done.4, f32[232,512]{1,0:T(8,128)} %copy-done.5, ...), custom_call_target="tpu_custom_call" | custom-call | tf_op jit(solution)/shard_map/pallas_call | solution.py:378
  83.8 0.0 collective-permute-done.6.first
  83.8 0.0 collective-permute-done.7.second
  83.8 0.0 collective-permute-done.4.far
  83.8 0.0 collective-permute-done.5.near
  83.8 0.0 all-to-all-done
  83.8 3.7 %shard_map.91 = (f32[9,4,32,512]{3,2,1,0:T(8,128)}, f32[2,4,32,512]{3,2,1,0:T(8,128)}) custom-call(f32[9,4,32,512]{3,2,1,0:T(8,128)} %get-tuple-element.16.fields, f32[4,32,512]{2,1,0:T(8,128)} %lam_in.5, f32[4,32,512]{2,1,0:T(8,128)} %mu_in.5, f32[6,4,32,512]{3,2,1,0:T(8,128)} %get-tuple-element.17.strain_in, ...), custom_call_target="tpu_custom_call", output_to_operand_aliasing={{0}: (0, {})} | custom-call | tf_op jit(solution)/shard_map/pallas_call | solution.py:378
  (1 shorter events, 0.0 us)
Async XLA Ops:
  3.3 33.4 %copy-start = (f32[9,4,32,512]{3,2,1,0:T(8,128)S(1)}, f32[9,4,32,512]{3,2,1,0:T(8,128)}, u32[]{:S(2)}) copy-start(f32[9,4,32,512]{3,2,1,0:T(8,128)} %adj_in.3) | copy-start | bytes 7077892
  3.4 33.4 %copy-start.1 = (f32[4,32,512]{2,1,0:T(8,128)S(1)}, f32[4,32,512]{2,1,0:T(8,128)}, u32[]{:S(2)}) copy-start(f32[4,32,512]{2,1,0:T(8,128)} %buoy_in.3) | copy-start | bytes 786436
  3.4 80.5 %all-to-all-start = ((s32[64,25,1,128]{3,2,1,0:T(1,128)}), s32[64,25,1,128]{3,2,1,0:T(1,128)S(1)}, u32[]{:S(2)}, u32[]{:S(2)}) async-start(s32[64,25,1,128]{3,2,1,0:T(1,128)} %bitcast.9), calls=%async_computation | async-start | bytes 1638400 | tf_op jit(solution)/shard_map/all_to_all | solution.py:424
  18.0 18.8 %collective-permute-start = (f32[13,4,512]{2,1,0:T(4,128)S(1)}, f32[13,4,512]{2,1,0:T(4,128)S(1)}, u32[]{:S(2)}, u32[]{:S(2)}) collective-permute-start(f32[13,4,512]{2,1,0:T(4,128)S(1)} %get-tuple-element.12), channel_id=1, source_target_pairs={{0,1},{2,3},{1,0},{3,2},{4,5},{6,7},{5,4},{7,6},{8,9},{10,11},{9,8... | collective-permute-start | bytes 319496 | tf_op jit(solution)/shard_map/ppermute | solution.py:411
  19.1 17.7 %collective-permute-start.1 = (f32[13,4,512]{2,1,0:T(4,128)S(1)}, f32[13,4,512]{2,1,0:T(4,128)S(1)}, u32[]{:S(2)}, u32[]{:S(2)}) collective-permute-start(f32[13,4,512]{2,1,0:T(4,128)S(1)} %get-tuple-element.13), channel_id=1, source_target_pairs={{1,2},{2,1},{5,6},{6,5},{9,10},{10,9},{13,14},{14,13},{17,18},{18,... | collective-permute-start | bytes 319496 | tf_op jit(solution)/shard_map/ppermute | solution.py:412
  36.7 23.2 %copy-start.2 = (f32[13,4,512]{2,1,0:T(4,128)}, f32[13,4,512]{2,1,0:T(4,128)S(1)}, u32[]{:S(2)}) copy-start(f32[13,4,512]{2,1,0:T(4,128)S(1)} %collective-permute-done.first.first_in) | copy-start | bytes 319492
  36.7 23.2 %copy-start.3 = (f32[13,4,512]{2,1,0:T(4,128)}, f32[13,4,512]{2,1,0:T(4,128)S(1)}, u32[]{:S(2)}) copy-start(f32[13,4,512]{2,1,0:T(4,128)S(1)} %collective-permute-done.1.second.second_in) | copy-start | bytes 319492
  37.9 22.1 %collective-permute-start.2 = (f32[232,512]{1,0:T(8,128)S(1)}, f32[232,512]{1,0:T(8,128)S(1)}, u32[]{:S(2)}, u32[]{:S(2)}) collective-permute-start(f32[232,512]{1,0:T(8,128)S(1)} %get-tuple-element.14), channel_id=1, source_target_pairs={{4,8},{8,4},{12,16},{16,12},{20,24},{24,20},{28,32},{32,28},{36,40... | collective-permute-start | bytes 1425416 | tf_op jit(solution)/shard_map/ppermute | solution.py:436
  48.2 11.8 %collective-permute-start.3 = (f32[232,512]{1,0:T(8,128)S(1)}, f32[232,512]{1,0:T(8,128)S(1)}, u32[]{:S(2)}, u32[]{:S(2)}) collective-permute-start(f32[232,512]{1,0:T(8,128)S(1)} %get-tuple-element.15), channel_id=1, source_target_pairs={{0,4},{4,0},{8,12},{12,8},{16,20},{20,16},{24,28},{28,24},{32,36},... | collective-permute-start | bytes 1425416 | tf_op jit(solution)/shard_map/ppermute | solution.py:437
  60.0 0.8 copy-start.4
  60.7 0.8 copy-start.5
  65.2 18.6 %collective-permute-start.4 = (f32[2,32,512]{2,1,0:T(8,128)S(1)}, f32[2,32,512]{2,1,0:T(8,128)S(1)}, u32[]{:S(2)}, u32[]{:S(2)}) collective-permute-start(f32[2,32,512]{2,1,0:T(8,128)S(1)} %get-tuple-element.18), channel_id=1, source_target_pairs={{4,8},{8,4},{12,16},{16,12},{20,24},{24,20},{28,32},{32,28},{36,40... | collective-permute-start | bytes 393224 | tf_op jit(solution)/shard_map/ppermute | solution.py:446
  75.4 8.4 %collective-permute-start.5 = (f32[2,32,512]{2,1,0:T(8,128)S(1)}, f32[2,32,512]{2,1,0:T(8,128)S(1)}, u32[]{:S(2)}, u32[]{:S(2)}) collective-permute-start(f32[2,32,512]{2,1,0:T(8,128)S(1)} %get-tuple-element.19), channel_id=1, source_target_pairs={{0,4},{4,0},{8,12},{12,8},{16,20},{20,16},{24,28},{28,24},{32,36},... | collective-permute-start | bytes 393224 | tf_op jit(solution)/shard_map/ppermute | solution.py:446
  75.5 8.3 %collective-permute-start.6 = (f32[2,4,512]{2,1,0:T(4,128)S(1)}, f32[2,4,512]{2,1,0:T(4,128)S(1)}, u32[]{:S(2)}, u32[]{:S(2)}) collective-permute-start(f32[2,4,512]{2,1,0:T(4,128)S(1)} %get-tuple-element.20), channel_id=1, source_target_pairs={{0,1},{2,3},{1,0},{3,2},{4,5},{6,7},{5,4},{7,6},{8,9},{10,11},{9,8... | collective-permute-start | bytes 49160 | tf_op jit(solution)/shard_map/ppermute | solution.py:447
  75.6 8.2 %collective-permute-start.7 = (f32[2,4,512]{2,1,0:T(4,128)S(1)}, f32[2,4,512]{2,1,0:T(4,128)S(1)}, u32[]{:S(2)}, u32[]{:S(2)}) collective-permute-start(f32[2,4,512]{2,1,0:T(4,128)S(1)} %get-tuple-element.21), channel_id=1, source_target_pairs={{1,2},{2,1},{5,6},{6,5},{9,10},{10,9},{13,14},{14,13},{17,18},{18,... | collective-permute-start | bytes 49160 | tf_op jit(solution)/shard_map/ppermute | solution.py:447

commit v6 on v5

--- a/solution.py
+++ b/solution.py
@@ -260,15 +260,20 @@
             v[k, x] = new[k]
 
 
-def edges(
-    adj_in, buoy_in, lam_in, mu_in, far_in, near_in, first_in, second_in, far, near, first, second,
-    adj, buoy, lam, mu, far_here, near_here, first_here, second_here, v, stress, sems,
+def middle(
+    adj_in, buoy_in, lam_in, mu_in, far_in, near_in, first_in, second_in, fields, strain_out, far, near, first, second,
+    adj, buoy, lam, mu, v, stress, strain, load_sems, sems,
 ):
-    given = (adj_in, buoy_in, lam_in, mu_in, far_in, near_in, first_in, second_in)
-    here = (adj, buoy, lam, mu, far_here, near_here, first_here, second_here)
-    for copy in load(zip(given, here), sems):
-        copy.wait()
-    half(*here, v, stress, None, lambda: None)
+    here = (adj, buoy, lam, mu)
+    for copy in load(zip((adj_in, buoy_in, lam_in, mu_in), here), load_sems):
+        copy.wait()
+    copies = [
+        pltpu.make_async_copy(strain, strain_out, sems.at[0]),
+        pltpu.make_async_copy(stress, fields.at[pl.ds(3, 6)], sems.at[1]),
+        pltpu.make_async_copy(v, fields.at[pl.ds(0, 3)], sems.at[2]),
+    ]
+    half(*here, far_in, near_in, first_in, second_in, v, stress, strain, lambda: [copy.start() for copy in copies[:2]])
+    copies[2].start()
     _, cells_x, cells_y, _ = v.shape
     over, under = v[1, :, cells_y - 1, :], v[0, :, 0, :]
     first[0], second[0] = first_second(over, under)
@@ -276,23 +281,6 @@
     first[1], second[1] = first_second(jnp.zeros_like(under), under)
     far[0], near[0] = far_near(v[0, cells_x - 1], v[1, 0])
     far[1], near[1] = far_near(jnp.zeros_like(v[2, 0]), v[2, 0])
-
-
-def inner(
-    adj_in, buoy_in, lam_in, mu_in, far_in, near_in, first_in, second_in, fields, strain_out,
-    adj, buoy, lam, mu, far, near, first, second, v, stress, strain, load_sems, sems,
-):
-    given = (adj_in, buoy_in, lam_in, mu_in, far_in, near_in, first_in, second_in)
-    here = (adj, buoy, lam, mu, far, near, first, second)
-    for copy in load(zip(given, here), load_sems):
-        copy.wait()
-    copies = [
-        pltpu.make_async_copy(strain, strain_out, sems.at[0]),
-        pltpu.make_async_copy(stress, fields.at[pl.ds(3, 6)], sems.at[1]),
-        pltpu.make_async_copy(v, fields.at[pl.ds(0, 3)], sems.at[2]),
-    ]
-    half(*here, v, stress, strain, lambda: [copy.start() for copy in copies[:2]])
-    copies[2].start()
     for copy in copies:
         copy.wait()
 
@@ -436,19 +424,14 @@
     far = lax.ppermute(far, "gx", off_chip)
     near = lax.ppermute(near, "gx", on_chip)
 
-    given = (*raw, *in_hbm(far, near, first, second))
-    line_rows = (len(UP_ROWS), cells_x, cells_z)
-    here = (whole, *[buoyancy.shape] * 3, message_rows, message_rows, line_rows, line_rows)
-    far, near, first, second = call(
-        edges, 16, (planes(2), planes(2), lines(2), lines(2)), given, [ANY] * 8, rooms(*here, speeds, strain) + semaphores(8)
+    fields, strain1, far, near, first, second = call(
+        middle, 16, (pltpu.HBM(whole, F32), pltpu.HBM(strain, F32), planes(2), planes(2), lines(2), lines(2)),
+        (*raw, far, near, first, second), [ANY] * 4 + [VMEM] * 4,
+        rooms(whole, *[buoyancy.shape] * 3, speeds, strain, strain) + semaphores(4, 3), (ANY, ANY, VMEM, VMEM, VMEM, VMEM),
     )
     w_ghosts = (
         lax.ppermute(far, "gx", off_chip), lax.ppermute(near, "gx", on_chip),
         lax.ppermute(first, "gy", pairs[0]), lax.ppermute(second, "gy", pairs[1]),
-    )
-    fields, strain1 = call(
-        inner, 24, (pltpu.HBM(whole, F32), pltpu.HBM(strain, F32)), given, [ANY] * 8,
-        rooms(*here, speeds, strain, strain) + semaphores(8, 3), (ANY, ANY),
     )
     grads = (2, *buoyancy.shape)
     adjoint_out, grads = call(

time: 89.2 us -> 86 us (0.964)
  Pallas kernels: 17.2 us -> 13.3 us
  waiting for transfers between devices: 26.4 us -> 29.1 us
  local copies, waits for them, and re-layouts: 2.26 us -> 0.71 us
    pallas_call x6 -> x5, Pallas kernels: 17.2 us -> 13.3 us  [call(): pl.pallas_call(kernel, out_shape=outs, in_specs=in_specs or [VMEM] * len(...]
    ppermute x1, waiting for transfers between devices: 0.01 us -> 1.91 us  [on_device(): lax.ppermute(second, 'gy', pairs[1])]
    unnamed x13 -> x5, local copies, waits for them, and re-layouts: 2.25 us -> 0.71 us
  transfers between devices with their start and end apart: 9 -> 9, of which waited for: 2 -> 4; matrix products, arithmetic and copies ran while one was open for 0% -> 0% of each run, Pallas kernels for 13% -> 9%
where the time goes in v6:
time: 86 us; the launch traced here: 84.7 us
  starting transfers between devices  40.9 us (48%)
  waiting for transfers between devices  29.1 us (34%)
  Pallas kernels  13.3 us (15%)
    ppermute x1, waiting for transfers between devices, on_device(): first = lax.ppermute(first, 'gy', pairs[0])  14.7 us
    pallas_call x5, Pallas kernels, call(): pl.pallas_call(kernel, out_shape=outs, in_specs=in_specs or [VMEM] * len(...  13.3 us
    all_to_all x1, starting transfers between devices, on_device(): lax.all_to_all(message.reshape(owners, per + 1, 1, 128), 'gx', split_axis...  13.1 us
    ppermute x1, waiting for transfers between devices, on_device(): far = lax.ppermute(far, 'gx', off_chip)  11.7 us
    ppermute x1, starting transfers between devices, on_device(): far = lax.ppermute(far, 'gx', off_chip)  10.3 us
    ppermute x1, starting transfers between devices, on_device(): lax.ppermute(far, 'gx', off_chip)  10.2 us
    ppermute x1, starting transfers between devices, on_device(): lax.ppermute(second, 'gy', pairs[1])  2.92 us
    ppermute x1, starting transfers between devices, on_device(): second = lax.ppermute(second, 'gy', pairs[1])  2.89 us
  transfers between devices with their start and end apart: 9, of which 4 were waited for; matrix products, arithmetic and copies ran while one was open for 0% of the time, Pallas kernels for 9%

profile of v6, /device:TPU:70, one launch (start us, length us, event | category | flops | bytes accessed | tf_op | source)
XLA Modules:
  0.0 84.7 jit_solution(13533172015048182375)
XLA Ops:
  0.6 0.7 copy.13
  1.3 2.0 %shard_map.89 = s32[1600,128]{1,0:T(8,128)} custom-call(s32[1536,128]{1,0:T(8,128)} %bitcast.10, f32[12,1,64]{2,1,0:T(1,128)S(1)} %reshape.21.scales), custom_call_target="tpu_custom_call" | custom-call | tf_op jit(solution)/shard_map/pallas_call | solution.py:366
  3.4 0.0 copy-start
  3.4 0.0 copy-start.1
  3.4 13.1 %all-to-all-start = ((s32[64,25,1,128]{3,2,1,0:T(1,128)}), s32[64,25,1,128]{3,2,1,0:T(1,128)S(1)}, u32[]{:S(2)}, u32[]{:S(2)}) async-start(s32[64,25,1,128]{3,2,1,0:T(1,128)} %bitcast.9), calls=%async_computation | async-start | bytes 1638400 | tf_op jit(solution)/shard_map/all_to_all | solution.py:412
  16.5 1.4 %shard_map.86 = (f32[13,4,512]{2,1,0:T(4,128)S(1)}, f32[13,4,512]{2,1,0:T(4,128)S(1)}) custom-call(f32[9,4,32,512]{3,2,1,0:T(8,128)} %adj_in.1, f32[4,32,512]{2,1,0:T(8,128)} %buoy_in.1, f32[4,32,512]{2,1,0:T(8,128)} %lam_in.3, f32[4,32,512]{2,1,0:T(8,128)} %mu_in.3), custom_call_target="tpu_custom_call" | custom-call | tf_op jit(solution)/shard_map/pallas_call | solution.py:366
  18.0 1.1 %collective-permute-start = (f32[13,4,512]{2,1,0:T(4,128)S(1)}, f32[13,4,512]{2,1,0:T(4,128)S(1)}, u32[]{:S(2)}, u32[]{:S(2)}) collective-permute-start(f32[13,4,512]{2,1,0:T(4,128)S(1)} %get-tuple-element.12), channel_id=1, source_target_pairs={{0,1},{2,3},{1,0},{3,2},{4,5},{6,7},{5,4},{7,6},{8,9},{10,11},{9,8... | collective-permute-start | bytes 319496 | tf_op jit(solution)/shard_map/ppermute | solution.py:399
  19.1 2.9 %collective-permute-start.1 = (f32[13,4,512]{2,1,0:T(4,128)S(1)}, f32[13,4,512]{2,1,0:T(4,128)S(1)}, u32[]{:S(2)}, u32[]{:S(2)}) collective-permute-start(f32[13,4,512]{2,1,0:T(4,128)S(1)} %get-tuple-element.13), channel_id=1, source_target_pairs={{1,2},{2,1},{5,6},{6,5},{9,10},{10,9},{13,14},{14,13},{17,18},{18,... | collective-permute-start | bytes 319496 | tf_op jit(solution)/shard_map/ppermute | solution.py:400
  22.0 14.7 %collective-permute-done.first.first_in = f32[13,4,512]{2,1,0:T(4,128)S(1)} collective-permute-done((f32[13,4,512]{2,1,0:T(4,128)S(1)}, f32[13,4,512]{2,1,0:T(4,128)S(1)}, u32[]{:S(2)}, u32[]{:S(2)}) %collective-permute-start) | collective-permute-done | bytes 106528 | tf_op jit(solution)/shard_map/ppermute | solution.py:399
  36.7 0.0 collective-permute-done.1.second.second_in
  36.7 0.0 copy-done
  36.7 0.0 copy-done.1
  36.7 1.1 %shard_map.87 = (f32[232,512]{1,0:T(8,128)S(1)}, f32[232,512]{1,0:T(8,128)S(1)}) custom-call(f32[9,4,32,512]{3,2,1,0:T(8,128)S(1)} %copy-done, f32[4,32,512]{2,1,0:T(8,128)S(1)} %copy-done.1, f32[4,32,512]{2,1,0:T(8,128)} %lam_in.3, f32[4,32,512]{2,1,0:T(8,128)} %mu_in.3, f32[13,4,512]{2,1,0:T(4,128)S(1)} %collective-permute-done.first.first_in, ...), custom_call_target="tpu_custom_call" | custom-call | tf_op jit(solution)/shard_map/pallas_call | solution.py:366
  37.9 10.3 %collective-permute-start.2 = (f32[232,512]{1,0:T(8,128)S(1)}, f32[232,512]{1,0:T(8,128)S(1)}, u32[]{:S(2)}, u32[]{:S(2)}) collective-permute-start(f32[232,512]{1,0:T(8,128)S(1)} %get-tuple-element.14), channel_id=1, source_target_pairs={{4,8},{8,4},{12,16},{16,12},{20,24},{24,20},{28,32},{32,28},{36,40... | collective-permute-start | bytes 1425416 | tf_op jit(solution)/shard_map/ppermute | solution.py:424
  48.2 0.1 collective-permute-start.3
  48.3 11.7 %collective-permute-done.2.far_in = f32[232,512]{1,0:T(8,128)S(1)} collective-permute-done((f32[232,512]{1,0:T(8,128)S(1)}, f32[232,512]{1,0:T(8,128)S(1)}, u32[]{:S(2)}, u32[]{:S(2)}) %collective-permute-start.2) | collective-permute-done | bytes 475168 | tf_op jit(solution)/shard_map/ppermute | solution.py:424
  60.0 0.0 collective-permute-done.3.near_in
  60.0 5.0 %shard_map.88 = (f32[9,4,32,512]{3,2,1,0:T(8,128)}, f32[6,4,32,512]{3,2,1,0:T(8,128)}, f32[2,32,512]{2,1,0:T(8,128)S(1)}, f32[2,32,512]{2,1,0:T(8,128)S(1)}, f32...) custom-call(f32[9,4,32,512]{3,2,1,0:T(8,128)} %adj_in.1, f32[4,32,512]{2,1,0:T(8,128)} %buoy_in.1, f32[4,32,512]{2,1,0:T(8,128)} %lam_in.3, ...), custom_call_target="tpu_custom_call" | custom-call | tf_op jit(solution)/shard_map/pallas_call | solution.py:366
  64.9 10.2 %collective-permute-start.4 = (f32[2,32,512]{2,1,0:T(8,128)S(1)}, f32[2,32,512]{2,1,0:T(8,128)S(1)}, u32[]{:S(2)}, u32[]{:S(2)}) collective-permute-start(f32[2,32,512]{2,1,0:T(8,128)S(1)} %get-tuple-element.18), channel_id=1, source_target_pairs={{4,8},{8,4},{12,16},{16,12},{20,24},{24,20},{28,32},{32,28},{36,40... | collective-permute-start | bytes 393224 | tf_op jit(solution)/shard_map/ppermute | solution.py:433
  75.1 0.1 collective-permute-start.5
  75.2 0.1 collective-permute-start.6
  75.4 2.9 %collective-permute-start.7 = (f32[2,4,512]{2,1,0:T(4,128)S(1)}, f32[2,4,512]{2,1,0:T(4,128)S(1)}, u32[]{:S(2)}, u32[]{:S(2)}) collective-permute-start(f32[2,4,512]{2,1,0:T(4,128)S(1)} %get-tuple-element.21), channel_id=1, source_target_pairs={{1,2},{2,1},{5,6},{6,5},{9,10},{10,9},{13,14},{14,13},{17,18},{18,... | collective-permute-start | bytes 49160 | tf_op jit(solution)/shard_map/ppermute | solution.py:434
  78.3 0.8 collective-permute-done.6.first
  79.1 1.9 %collective-permute-done.7.second = f32[2,4,512]{2,1,0:T(4,128)S(1)} collective-permute-done((f32[2,4,512]{2,1,0:T(4,128)S(1)}, f32[2,4,512]{2,1,0:T(4,128)S(1)}, u32[]{:S(2)}, u32[]{:S(2)}) %collective-permute-start.7) | collective-permute-done | bytes 16416 | tf_op jit(solution)/shard_map/ppermute | solution.py:434
  81.0 0.0 collective-permute-done.4.far
  81.0 0.0 collective-permute-done.5.near
  81.0 0.0 all-to-all-done
  81.0 3.7 %shard_map.90 = (f32[9,4,32,512]{3,2,1,0:T(8,128)}, f32[2,4,32,512]{3,2,1,0:T(8,128)}) custom-call(f32[9,4,32,512]{3,2,1,0:T(8,128)} %get-tuple-element.16.fields, f32[4,32,512]{2,1,0:T(8,128)} %lam_in.3, f32[4,32,512]{2,1,0:T(8,128)} %mu_in.3, f32[6,4,32,512]{3,2,1,0:T(8,128)} %get-tuple-element.17.strain_in, ...), custom_call_target="tpu_custom_call", output_to_operand_aliasing={{0}: (0, {})} | custom-call | tf_op jit(solution)/shard_map/pallas_call | solution.py:366
  (1 shorter events, 0.0 us)
Async XLA Ops:
  3.4 33.4 %copy-start = (f32[9,4,32,512]{3,2,1,0:T(8,128)S(1)}, f32[9,4,32,512]{3,2,1,0:T(8,128)}, u32[]{:S(2)}) copy-start(f32[9,4,32,512]{3,2,1,0:T(8,128)} %adj_in.1) | copy-start | bytes 7077892
  3.4 33.4 %copy-start.1 = (f32[4,32,512]{2,1,0:T(8,128)S(1)}, f32[4,32,512]{2,1,0:T(8,128)}, u32[]{:S(2)}) copy-start(f32[4,32,512]{2,1,0:T(8,128)} %buoy_in.1) | copy-start | bytes 786436
  3.4 77.6 %all-to-all-start = ((s32[64,25,1,128]{3,2,1,0:T(1,128)}), s32[64,25,1,128]{3,2,1,0:T(1,128)S(1)}, u32[]{:S(2)}, u32[]{:S(2)}) async-start(s32[64,25,1,128]{3,2,1,0:T(1,128)} %bitcast.9), calls=%async_computation | async-start | bytes 1638400 | tf_op jit(solution)/shard_map/all_to_all | solution.py:412
  18.0 18.8 %collective-permute-start = (f32[13,4,512]{2,1,0:T(4,128)S(1)}, f32[13,4,512]{2,1,0:T(4,128)S(1)}, u32[]{:S(2)}, u32[]{:S(2)}) collective-permute-start(f32[13,4,512]{2,1,0:T(4,128)S(1)} %get-tuple-element.12), channel_id=1, source_target_pairs={{0,1},{2,3},{1,0},{3,2},{4,5},{6,7},{5,4},{7,6},{8,9},{10,11},{9,8... | collective-permute-start | bytes 319496 | tf_op jit(solution)/shard_map/ppermute | solution.py:399
  19.1 17.6 %collective-permute-start.1 = (f32[13,4,512]{2,1,0:T(4,128)S(1)}, f32[13,4,512]{2,1,0:T(4,128)S(1)}, u32[]{:S(2)}, u32[]{:S(2)}) collective-permute-start(f32[13,4,512]{2,1,0:T(4,128)S(1)} %get-tuple-element.13), channel_id=1, source_target_pairs={{1,2},{2,1},{5,6},{6,5},{9,10},{10,9},{13,14},{14,13},{17,18},{18,... | collective-permute-start | bytes 319496 | tf_op jit(solution)/shard_map/ppermute | solution.py:400
  37.9 22.1 %collective-permute-start.2 = (f32[232,512]{1,0:T(8,128)S(1)}, f32[232,512]{1,0:T(8,128)S(1)}, u32[]{:S(2)}, u32[]{:S(2)}) collective-permute-start(f32[232,512]{1,0:T(8,128)S(1)} %get-tuple-element.14), channel_id=1, source_target_pairs={{4,8},{8,4},{12,16},{16,12},{20,24},{24,20},{28,32},{32,28},{36,40... | collective-permute-start | bytes 1425416 | tf_op jit(solution)/shard_map/ppermute | solution.py:424
  48.2 11.8 %collective-permute-start.3 = (f32[232,512]{1,0:T(8,128)S(1)}, f32[232,512]{1,0:T(8,128)S(1)}, u32[]{:S(2)}, u32[]{:S(2)}) collective-permute-start(f32[232,512]{1,0:T(8,128)S(1)} %get-tuple-element.15), channel_id=1, source_target_pairs={{0,4},{4,0},{8,12},{12,8},{16,20},{20,16},{24,28},{28,24},{32,36},... | collective-permute-start | bytes 1425416 | tf_op jit(solution)/shard_map/ppermute | solution.py:425
  64.9 16.1 %collective-permute-start.4 = (f32[2,32,512]{2,1,0:T(8,128)S(1)}, f32[2,32,512]{2,1,0:T(8,128)S(1)}, u32[]{:S(2)}, u32[]{:S(2)}) collective-permute-start(f32[2,32,512]{2,1,0:T(8,128)S(1)} %get-tuple-element.18), channel_id=1, source_target_pairs={{4,8},{8,4},{12,16},{16,12},{20,24},{24,20},{28,32},{32,28},{36,40... | collective-permute-start | bytes 393224 | tf_op jit(solution)/shard_map/ppermute | solution.py:433
  75.1 5.8 %collective-permute-start.5 = (f32[2,32,512]{2,1,0:T(8,128)S(1)}, f32[2,32,512]{2,1,0:T(8,128)S(1)}, u32[]{:S(2)}, u32[]{:S(2)}) collective-permute-start(f32[2,32,512]{2,1,0:T(8,128)S(1)} %get-tuple-element.19), channel_id=1, source_target_pairs={{0,4},{4,0},{8,12},{12,8},{16,20},{20,16},{24,28},{28,24},{32,36},... | collective-permute-start | bytes 393224 | tf_op jit(solution)/shard_map/ppermute | solution.py:433
  75.2 3.8 %collective-permute-start.6 = (f32[2,4,512]{2,1,0:T(4,128)S(1)}, f32[2,4,512]{2,1,0:T(4,128)S(1)}, u32[]{:S(2)}, u32[]{:S(2)}) collective-permute-start(f32[2,4,512]{2,1,0:T(4,128)S(1)} %get-tuple-element.20), channel_id=1, source_target_pairs={{0,1},{2,3},{1,0},{3,2},{4,5},{6,7},{5,4},{7,6},{8,9},{10,11},{9,8... | collective-permute-start | bytes 49160 | tf_op jit(solution)/shard_map/ppermute | solution.py:434
  75.4 5.6 %collective-permute-start.7 = (f32[2,4,512]{2,1,0:T(4,128)S(1)}, f32[2,4,512]{2,1,0:T(4,128)S(1)}, u32[]{:S(2)}, u32[]{:S(2)}) collective-permute-start(f32[2,4,512]{2,1,0:T(4,128)S(1)} %get-tuple-element.21), channel_id=1, source_target_pairs={{1,2},{2,1},{5,6},{6,5},{9,10},{10,9},{13,14},{14,13},{17,18},{18,... | collective-permute-start | bytes 49160 | tf_op jit(solution)/shard_map/ppermute | solution.py:434

commit v7 on v6

--- a/solution.py
+++ b/solution.py
@@ -156,11 +156,15 @@
     return [pl.ds(k * cells_y, cells_y) for k in range(PLANES)], [pl.ds(PLANES * cells_y + k, 1) for k in range(6)]
 
 
-def reach(adj, buoy, lam, mu, first, second, far, near, planes, sems):
+def reach(adj_in, buoy_in, lam, mu, first, second, far, near, adj, buoy, planes, sems):
     cells_x, cells_y = adj.shape[1:3]
     last = cells_x - 1
-    loads = load(((mu.at[last], planes.at[0]), (lam.at[0], planes.at[1]), (mu.at[0], planes.at[2])), sems)
+    needed = [(adj_in.at[:, x], adj.at[:, x]) for x in (0, last)] + [(buoy_in.at[x], buoy.at[x]) for x in (0, last)]
+    needed += [(adj_in.at[n, x], adj.at[n, x]) for n, x in ((3, 1), (6, last - 1), (7, last - 1))]
+    loads = load((*needed, (mu.at[last], planes.at[0]), (lam.at[0], planes.at[1]), (mu.at[0], planes.at[2])), sems)
     prior_y, next_y = named_rows(first, second)
+    for copy in loads[:-3]:
+        copy.wait()
     blank = jnp.zeros_like(adj[0, 0])
     up = [*step_one(adj, buoy, last, blank, adj[6, last - 1], adj[7, last - 1], prior_y, next_y), buoy[last], adj[6, last], adj[7, last]]
     down = [*step_one(adj, buoy, 0, adj[3, 1], blank, blank, prior_y, next_y), buoy[0], adj[3, 0]]
@@ -175,7 +179,7 @@
     down_rows = [own[1] - scaled_down * (own[6] + sides), scaled_down, own[3], next_y[3, 1][0:1]]
     down_rows += [jnp.zeros_like(scaled_down)] * 2
     whole, lines = places(cells_y)
-    for copy in loads:
+    for copy in loads[-3:]:
         copy.wait()
     up.append(planes[0])
     down += [planes[1], planes[2]]
@@ -418,8 +422,8 @@
     message_rows = (PLANES * cells_y + 8, cells_z)
     faces = shape(*message_rows)
     far, near = call(
-        reach, 12, (faces, faces), (adjoint, buoyancy, *raw[2:], first, second), [VMEM] * 2 + [ANY] * 2 + [VMEM] * 2,
-        rooms((3, cells_y, cells_z)) + semaphores(3),
+        reach, 12, (faces, faces), (*raw, first, second), [ANY] * 4 + [VMEM] * 2,
+        rooms(whole, buoyancy.shape, (3, cells_y, cells_z)) + semaphores(10),
     )
     far = lax.ppermute(far, "gx", off_chip)
     near = lax.ppermute(near, "gx", on_chip)

time: 86 us -> 86.3 us (level)
  no operation moved by 1% of the time
where the time goes in v7:
time: 86.3 us; the launch traced here: 85 us
  starting transfers between devices  40.7 us (47%)
  waiting for transfers between devices  29.1 us (34%)
  Pallas kernels  13.8 us (16%)
    ppermute x1, waiting for transfers between devices, on_device(): first = lax.ppermute(first, 'gy', pairs[0])  14.7 us
    pallas_call x5, Pallas kernels, call(): pl.pallas_call(kernel, out_shape=outs, in_specs=in_specs or [VMEM] * len(...  13.8 us
    all_to_all x1, starting transfers between devices, on_device(): lax.all_to_all(message.reshape(owners, per + 1, 1, 128), 'gx', split_axis...  13 us
    ppermute x1, waiting for transfers between devices, on_device(): far = lax.ppermute(far, 'gx', off_chip)  11.7 us
    ppermute x1, starting transfers between devices, on_device(): far = lax.ppermute(far, 'gx', off_chip)  10.3 us
    ppermute x1, starting transfers between devices, on_device(): lax.ppermute(far, 'gx', off_chip)  10.2 us
    ppermute x1, starting transfers between devices, on_device(): lax.ppermute(second, 'gy', pairs[1])  2.92 us
    ppermute x1, starting transfers between devices, on_device(): second = lax.ppermute(second, 'gy', pairs[1])  2.89 us
  transfers between devices with their start and end apart: 9, of which 4 were waited for; matrix products, arithmetic and copies ran while one was open for 0% of the time, Pallas kernels for 9%

profile of v7, /device:TPU:70, one launch (start us, length us, event | category | flops | bytes accessed | tf_op | source)
XLA Modules:
  0.0 85.0 jit_solution(10585988895316072325)
XLA Ops:
  0.6 0.7 copy.13
  1.3 2.0 %shard_map.89 = s32[1600,128]{1,0:T(8,128)} custom-call(s32[1536,128]{1,0:T(8,128)} %bitcast.10, f32[12,1,64]{2,1,0:T(1,128)S(1)} %reshape.21.scales), custom_call_target="tpu_custom_call" | custom-call | tf_op jit(solution)/shard_map/pallas_call | solution.py:370
  3.3 13.0 %all-to-all-start = ((s32[64,25,1,128]{3,2,1,0:T(1,128)}), s32[64,25,1,128]{3,2,1,0:T(1,128)S(1)}, u32[]{:S(2)}, u32[]{:S(2)}) async-start(s32[64,25,1,128]{3,2,1,0:T(1,128)} %bitcast.9), calls=%async_computation | async-start | bytes 1638400 | tf_op jit(solution)/shard_map/all_to_all | solution.py:416
  16.4 1.4 %shard_map.86 = (f32[13,4,512]{2,1,0:T(4,128)S(1)}, f32[13,4,512]{2,1,0:T(4,128)S(1)}) custom-call(f32[9,4,32,512]{3,2,1,0:T(8,128)} %adj_in.3, f32[4,32,512]{2,1,0:T(8,128)} %buoy_in.3, f32[4,32,512]{2,1,0:T(8,128)} %lam_in.3, f32[4,32,512]{2,1,0:T(8,128)} %mu_in.3), custom_call_target="tpu_custom_call" | custom-call | tf_op jit(solution)/shard_map/pallas_call | solution.py:370
  17.8 1.1 %collective-permute-start = (f32[13,4,512]{2,1,0:T(4,128)S(1)}, f32[13,4,512]{2,1,0:T(4,128)S(1)}, u32[]{:S(2)}, u32[]{:S(2)}) collective-permute-start(f32[13,4,512]{2,1,0:T(4,128)S(1)} %get-tuple-element.12), channel_id=1, source_target_pairs={{0,1},{2,3},{1,0},{3,2},{4,5},{6,7},{5,4},{7,6},{8,9},{10,11},{9,8... | collective-permute-start | bytes 319496 | tf_op jit(solution)/shard_map/ppermute | solution.py:403
  18.9 2.9 %collective-permute-start.1 = (f32[13,4,512]{2,1,0:T(4,128)S(1)}, f32[13,4,512]{2,1,0:T(4,128)S(1)}, u32[]{:S(2)}, u32[]{:S(2)}) collective-permute-start(f32[13,4,512]{2,1,0:T(4,128)S(1)} %get-tuple-element.13), channel_id=1, source_target_pairs={{1,2},{2,1},{5,6},{6,5},{9,10},{10,9},{13,14},{14,13},{17,18},{18,... | collective-permute-start | bytes 319496 | tf_op jit(solution)/shard_map/ppermute | solution.py:404
  21.8 14.7 %collective-permute-done.first.first_in = f32[13,4,512]{2,1,0:T(4,128)S(1)} collective-permute-done((f32[13,4,512]{2,1,0:T(4,128)S(1)}, f32[13,4,512]{2,1,0:T(4,128)S(1)}, u32[]{:S(2)}, u32[]{:S(2)}) %collective-permute-start) | collective-permute-done | bytes 106528 | tf_op jit(solution)/shard_map/ppermute | solution.py:403
  36.6 0.0 collective-permute-done.1.second.second_in
  36.6 1.6 %shard_map.87 = (f32[232,512]{1,0:T(8,128)S(1)}, f32[232,512]{1,0:T(8,128)S(1)}) custom-call(f32[9,4,32,512]{3,2,1,0:T(8,128)} %adj_in.3, f32[4,32,512]{2,1,0:T(8,128)} %buoy_in.3, f32[4,32,512]{2,1,0:T(8,128)} %lam_in.3, f32[4,32,512]{2,1,0:T(8,128)} %mu_in.3, f32[13,4,512]{2,1,0:T(4,128)S(1)} %collective-permute-done.first.first_in, ...), custom_call_target="tpu_custom_call" | custom-call | tf_op jit(solution)/shard_map/pallas_call | solution.py:370
  38.2 10.3 %collective-permute-start.2 = (f32[232,512]{1,0:T(8,128)S(1)}, f32[232,512]{1,0:T(8,128)S(1)}, u32[]{:S(2)}, u32[]{:S(2)}) collective-permute-start(f32[232,512]{1,0:T(8,128)S(1)} %get-tuple-element.14), channel_id=1, source_target_pairs={{4,8},{8,4},{12,16},{16,12},{20,24},{24,20},{28,32},{32,28},{36,40... | collective-permute-start | bytes 1425416 | tf_op jit(solution)/shard_map/ppermute | solution.py:428
  48.5 0.1 collective-permute-start.3
  48.6 11.7 %collective-permute-done.2.far_in = f32[232,512]{1,0:T(8,128)S(1)} collective-permute-done((f32[232,512]{1,0:T(8,128)S(1)}, f32[232,512]{1,0:T(8,128)S(1)}, u32[]{:S(2)}, u32[]{:S(2)}) %collective-permute-start.2) | collective-permute-done | bytes 475168 | tf_op jit(solution)/shard_map/ppermute | solution.py:428
  60.3 0.0 collective-permute-done.3.near_in
  60.3 5.0 %shard_map.88 = (f32[9,4,32,512]{3,2,1,0:T(8,128)}, f32[6,4,32,512]{3,2,1,0:T(8,128)}, f32[2,32,512]{2,1,0:T(8,128)S(1)}, f32[2,32,512]{2,1,0:T(8,128)S(1)}, f32...) custom-call(f32[9,4,32,512]{3,2,1,0:T(8,128)} %adj_in.3, f32[4,32,512]{2,1,0:T(8,128)} %buoy_in.3, f32[4,32,512]{2,1,0:T(8,128)} %lam_in.3, ...), custom_call_target="tpu_custom_call" | custom-call | tf_op jit(solution)/shard_map/pallas_call | solution.py:370
  65.3 10.2 %collective-permute-start.4 = (f32[2,32,512]{2,1,0:T(8,128)S(1)}, f32[2,32,512]{2,1,0:T(8,128)S(1)}, u32[]{:S(2)}, u32[]{:S(2)}) collective-permute-start(f32[2,32,512]{2,1,0:T(8,128)S(1)} %get-tuple-element.18), channel_id=1, source_target_pairs={{4,8},{8,4},{12,16},{16,12},{20,24},{24,20},{28,32},{32,28},{36,40... | collective-permute-start | bytes 393224 | tf_op jit(solution)/shard_map/ppermute | solution.py:437
  75.5 0.1 collective-permute-start.5
  75.6 0.1 collective-permute-start.6
  75.7 2.9 %collective-permute-start.7 = (f32[2,4,512]{2,1,0:T(4,128)S(1)}, f32[2,4,512]{2,1,0:T(4,128)S(1)}, u32[]{:S(2)}, u32[]{:S(2)}) collective-permute-start(f32[2,4,512]{2,1,0:T(4,128)S(1)} %get-tuple-element.21), channel_id=1, source_target_pairs={{1,2},{2,1},{5,6},{6,5},{9,10},{10,9},{13,14},{14,13},{17,18},{18,... | collective-permute-start | bytes 49160 | tf_op jit(solution)/shard_map/ppermute | solution.py:438
  78.6 0.8 collective-permute-done.6.first
  79.4 1.9 %collective-permute-done.7.second = f32[2,4,512]{2,1,0:T(4,128)S(1)} collective-permute-done((f32[2,4,512]{2,1,0:T(4,128)S(1)}, f32[2,4,512]{2,1,0:T(4,128)S(1)}, u32[]{:S(2)}, u32[]{:S(2)}) %collective-permute-start.7) | collective-permute-done | bytes 16416 | tf_op jit(solution)/shard_map/ppermute | solution.py:438
  81.3 0.0 collective-permute-done.4.far
  81.3 0.0 collective-permute-done.5.near
  81.3 0.0 all-to-all-done
  81.3 3.7 %shard_map.90 = (f32[9,4,32,512]{3,2,1,0:T(8,128)}, f32[2,4,32,512]{3,2,1,0:T(8,128)}) custom-call(f32[9,4,32,512]{3,2,1,0:T(8,128)} %get-tuple-element.16.fields, f32[4,32,512]{2,1,0:T(8,128)} %lam_in.3, f32[4,32,512]{2,1,0:T(8,128)} %mu_in.3, f32[6,4,32,512]{3,2,1,0:T(8,128)} %get-tuple-element.17.strain_in, ...), custom_call_target="tpu_custom_call", output_to_operand_aliasing={{0}: (0, {})} | custom-call | tf_op jit(solution)/shard_map/pallas_call | solution.py:370
  (1 shorter events, 0.0 us)
Async XLA Ops:
  3.3 78.0 %all-to-all-start = ((s32[64,25,1,128]{3,2,1,0:T(1,128)}), s32[64,25,1,128]{3,2,1,0:T(1,128)S(1)}, u32[]{:S(2)}, u32[]{:S(2)}) async-start(s32[64,25,1,128]{3,2,1,0:T(1,128)} %bitcast.9), calls=%async_computation | async-start | bytes 1638400 | tf_op jit(solution)/shard_map/all_to_all | solution.py:416
  17.8 18.8 %collective-permute-start = (f32[13,4,512]{2,1,0:T(4,128)S(1)}, f32[13,4,512]{2,1,0:T(4,128)S(1)}, u32[]{:S(2)}, u32[]{:S(2)}) collective-permute-start(f32[13,4,512]{2,1,0:T(4,128)S(1)} %get-tuple-element.12), channel_id=1, source_target_pairs={{0,1},{2,3},{1,0},{3,2},{4,5},{6,7},{5,4},{7,6},{8,9},{10,11},{9,8... | collective-permute-start | bytes 319496 | tf_op jit(solution)/shard_map/ppermute | solution.py:403
  18.9 17.6 %collective-permute-start.1 = (f32[13,4,512]{2,1,0:T(4,128)S(1)}, f32[13,4,512]{2,1,0:T(4,128)S(1)}, u32[]{:S(2)}, u32[]{:S(2)}) collective-permute-start(f32[13,4,512]{2,1,0:T(4,128)S(1)} %get-tuple-element.13), channel_id=1, source_target_pairs={{1,2},{2,1},{5,6},{6,5},{9,10},{10,9},{13,14},{14,13},{17,18},{18,... | collective-permute-start | bytes 319496 | tf_op jit(solution)/shard_map/ppermute | solution.py:404
  38.2 22.1 %collective-permute-start.2 = (f32[232,512]{1,0:T(8,128)S(1)}, f32[232,512]{1,0:T(8,128)S(1)}, u32[]{:S(2)}, u32[]{:S(2)}) collective-permute-start(f32[232,512]{1,0:T(8,128)S(1)} %get-tuple-element.14), channel_id=1, source_target_pairs={{4,8},{8,4},{12,16},{16,12},{20,24},{24,20},{28,32},{32,28},{36,40... | collective-permute-start | bytes 1425416 | tf_op jit(solution)/shard_map/ppermute | solution.py:428
  48.5 11.8 %collective-permute-start.3 = (f32[232,512]{1,0:T(8,128)S(1)}, f32[232,512]{1,0:T(8,128)S(1)}, u32[]{:S(2)}, u32[]{:S(2)}) collective-permute-start(f32[232,512]{1,0:T(8,128)S(1)} %get-tuple-element.15), channel_id=1, source_target_pairs={{0,4},{4,0},{8,12},{12,8},{16,20},{20,16},{24,28},{28,24},{32,36},... | collective-permute-start | bytes 1425416 | tf_op jit(solution)/shard_map/ppermute | solution.py:429
  65.3 16.1 %collective-permute-start.4 = (f32[2,32,512]{2,1,0:T(8,128)S(1)}, f32[2,32,512]{2,1,0:T(8,128)S(1)}, u32[]{:S(2)}, u32[]{:S(2)}) collective-permute-start(f32[2,32,512]{2,1,0:T(8,128)S(1)} %get-tuple-element.18), channel_id=1, source_target_pairs={{4,8},{8,4},{12,16},{16,12},{20,24},{24,20},{28,32},{32,28},{36,40... | collective-permute-start | bytes 393224 | tf_op jit(solution)/shard_map/ppermute | solution.py:437
  75.5 5.8 %collective-permute-start.5 = (f32[2,32,512]{2,1,0:T(8,128)S(1)}, f32[2,32,512]{2,1,0:T(8,128)S(1)}, u32[]{:S(2)}, u32[]{:S(2)}) collective-permute-start(f32[2,32,512]{2,1,0:T(8,128)S(1)} %get-tuple-element.19), channel_id=1, source_target_pairs={{0,4},{4,0},{8,12},{12,8},{16,20},{20,16},{24,28},{28,24},{32,36},... | collective-permute-start | bytes 393224 | tf_op jit(solution)/shard_map/ppermute | solution.py:437
  75.6 3.8 %collective-permute-start.6 = (f32[2,4,512]{2,1,0:T(4,128)S(1)}, f32[2,4,512]{2,1,0:T(4,128)S(1)}, u32[]{:S(2)}, u32[]{:S(2)}) collective-permute-start(f32[2,4,512]{2,1,0:T(4,128)S(1)} %get-tuple-element.20), channel_id=1, source_target_pairs={{0,1},{2,3},{1,0},{3,2},{4,5},{6,7},{5,4},{7,6},{8,9},{10,11},{9,8... | collective-permute-start | bytes 49160 | tf_op jit(solution)/shard_map/ppermute | solution.py:438
  75.7 5.6 %collective-permute-start.7 = (f32[2,4,512]{2,1,0:T(4,128)S(1)}, f32[2,4,512]{2,1,0:T(4,128)S(1)}, u32[]{:S(2)}, u32[]{:S(2)}) collective-permute-start(f32[2,4,512]{2,1,0:T(4,128)S(1)} %get-tuple-element.21), channel_id=1, source_target_pairs={{1,2},{2,1},{5,6},{6,5},{9,10},{10,9},{13,14},{14,13},{17,18},{18,... | collective-permute-start | bytes 49160 | tf_op jit(solution)/shard_map/ppermute | solution.py:438
